TPU v7x, 8 devices: a whole 2x2x1 slice. The times are simulated.
8 devices in a mesh: rep: 1 (over z), g: 8 (over y, x, core).
Axes of the slice: x: 2, y: 2, z: 1, core: 2. Of those that a mesh axis runs over, the one named last changes fastest.
Arguments:
- hidden: bfloat16 [256, 2048], P(('rep', 'g'))
- cache_lat: bfloat16 [256, 1024, 512], P(('rep', 'g'))
- cache_rope: bfloat16 [256, 1024, 64], P(('rep', 'g'))
- seq_lens: int32 [256], P(('rep', 'g'))
- gain_attn: bfloat16 [2048], replicated
- w_dq: bfloat16 [2048, 768], replicated
- gain_q: bfloat16 [768], replicated
- w_uq: bfloat16 [768, 20, 192], replicated
- w_qr: bfloat16 [768, 20, 64], replicated
- w_dkv: bfloat16 [2048, 576], replicated
- gain_kv: bfloat16 [512], replicated
- w_uk: bfloat16 [512, 20, 192], replicated
- w_uv: bfloat16 [512, 20, 256], replicated
- w_o: bfloat16 [5120, 2048], replicated
- gain_mlp: bfloat16 [2048], replicated
- w_gate: bfloat16 [2048, 10240], P(None, 'g')
- w_up: bfloat16 [2048, 10240], P(None, 'g')
- w_down: bfloat16 [10240, 2048], P('g')
Outputs:
- output 1: bfloat16 [256, 2048], P(('rep', 'g'))
- output 2: bfloat16 [256, 512], P(('rep', 'g'))
- output 3: bfloat16 [256, 64], P(('rep', 'g'))
All inputs are finite; a program needn't handle non-finite values.
Results may differ from a plain program's by a relative error of at most 0.0121209.
Values are sent between devices in bfloat16 or wider.
A program may use at most 1 GiB of HBM per device.

v0:
```python
import jax
import jax.numpy as jnp
from jax import lax
from jax.sharding import PartitionSpec as P


def rms_norm(values, gain_vec):
    mean_sq = jnp.mean(jnp.square(values), axis=-1, keepdims=True)
    return values * lax.rsqrt(mean_sq + 1e-6) * gain_vec.astype(jnp.float32)


def apply_rope(values, positions):
    half_dim = values.shape[-1] // 2
    inv_freq = 10000.0 ** (-jnp.arange(half_dim).astype(jnp.float32) / half_dim)
    angles = positions.astype(jnp.float32)[..., None] * inv_freq
    cos_part = jnp.cos(angles)
    sin_part = jnp.sin(angles)
    first_half = values[..., :half_dim]
    second_half = values[..., half_dim:]
    return jnp.concatenate([first_half * cos_part - second_half * sin_part, first_half * sin_part + second_half * cos_part], axis=-1)


def attention_rows(hidden, cache_lat, cache_rope, seq_lens, gain_attn, w_dq, gain_q, w_uq, w_qr, w_dkv, gain_kv, w_uk, w_uv, w_o):
    kv_dim = w_uk.shape[0]
    cache_len = cache_lat.shape[1]
    score_scale = (w_uq.shape[2] + w_qr.shape[2]) ** -0.5
    normed = rms_norm(hidden.astype(jnp.float32), gain_attn).astype(jnp.bfloat16)
    q_in = rms_norm(jnp.dot(normed, w_dq, preferred_element_type=jnp.float32), gain_q).astype(jnp.bfloat16)
    q_nope = jnp.einsum("bq,qhn->bhn", q_in, w_uq, preferred_element_type=jnp.float32).astype(jnp.bfloat16)
    q_rope = apply_rope(jnp.einsum("bq,qhr->bhr", q_in, w_qr, preferred_element_type=jnp.float32), seq_lens[:, None]).astype(jnp.bfloat16)
    kv_raw = jnp.dot(normed, w_dkv, preferred_element_type=jnp.float32)
    new_lat = rms_norm(kv_raw[:, :kv_dim], gain_kv).astype(jnp.bfloat16)
    new_rope = apply_rope(kv_raw[:, kv_dim:], seq_lens).astype(jnp.bfloat16)
    q_abs = jnp.einsum("bhn,chn->bhc", q_nope, w_uk, preferred_element_type=jnp.float32).astype(jnp.bfloat16)
    past_score = (jnp.einsum("bhc,blc->bhl", q_abs, cache_lat, preferred_element_type=jnp.float32) + jnp.einsum("bhr,blr->bhl", q_rope, cache_rope, preferred_element_type=jnp.float32)) * score_scale
    own_score = (jnp.einsum("bhc,bc->bh", q_abs, new_lat, preferred_element_type=jnp.float32) + jnp.einsum("bhr,br->bh", q_rope, new_rope, preferred_element_type=jnp.float32)) * score_scale
    key_pos = lax.broadcasted_iota(jnp.int32, (1, 1, cache_len), 2)
    past_score = jnp.where(key_pos < seq_lens[:, None, None], past_score, -jnp.inf)
    row_max = jnp.maximum(jnp.max(past_score, axis=-1), own_score)
    past_exp = jnp.exp(past_score - row_max[..., None])
    own_exp = jnp.exp(own_score - row_max)
    row_total = jnp.sum(past_exp, axis=-1) + own_exp
    past_prob = (past_exp / row_total[..., None]).astype(jnp.bfloat16)
    own_prob = (own_exp / row_total).astype(jnp.bfloat16)
    mixed_lat = (jnp.einsum("bhl,blc->bhc", past_prob, cache_lat, preferred_element_type=jnp.float32) + own_prob.astype(jnp.float32)[..., None] * new_lat.astype(jnp.float32)[:, None, :]).astype(jnp.bfloat16)
    out_heads = jnp.einsum("bhc,chv->bhv", mixed_lat, w_uv, preferred_element_type=jnp.float32).astype(jnp.bfloat16)
    attn_out = jnp.dot(out_heads.reshape(out_heads.shape[0], -1), w_o, preferred_element_type=jnp.float32)
    resid_rows = (hidden.astype(jnp.float32) + attn_out).astype(jnp.bfloat16)
    return resid_rows, new_lat, new_rope


def solution(mesh):
    row_spec = P(("rep", "g"))
    full_spec = P()
    in_specs = (row_spec, row_spec, row_spec, row_spec, full_spec, full_spec, full_spec, full_spec, full_spec, full_spec, full_spec, full_spec, full_spec, full_spec, full_spec, P(None, "g"), P(None, "g"), P("g", None))

    def local_step(hidden, cache_lat, cache_rope, seq_lens, gain_attn, w_dq, gain_q, w_uq, w_qr, w_dkv, gain_kv, w_uk, w_uv, w_o, gain_mlp, w_gate, w_up, w_down):
        resid_rows, new_lat, new_rope = attention_rows(hidden, cache_lat, cache_rope, seq_lens, gain_attn, w_dq, gain_q, w_uq, w_qr, w_dkv, gain_kv, w_uk, w_uv, w_o)
        mlp_in = rms_norm(resid_rows.astype(jnp.float32), gain_mlp).astype(jnp.bfloat16)
        group_rows = lax.all_gather(mlp_in, "g", axis=0, tiled=True)
        gate_proj = jnp.dot(group_rows, w_gate, preferred_element_type=jnp.float32)
        up_proj = jnp.dot(group_rows, w_up, preferred_element_type=jnp.float32)
        act_vals = (jax.nn.silu(gate_proj) * up_proj).astype(jnp.bfloat16)
        part_sum = jnp.dot(act_vals, w_down, preferred_element_type=jnp.float32).astype(jnp.bfloat16)
        mlp_rows = lax.psum_scatter(part_sum, "g", scatter_dimension=0, tiled=True)
        out_hidden = (resid_rows.astype(jnp.float32) + mlp_rows.astype(jnp.float32)).astype(jnp.bfloat16)
        return out_hidden, new_lat, new_rope

    return jax.shard_map(local_step, mesh=mesh, in_specs=in_specs, out_specs=(row_spec, row_spec, row_spec), check_vma=False)
```

profile of v0, /device:TPU:0, one launch (start us, length us, event | category | flops | bytes accessed | tf_op | source)
XLA Modules:
  0.0 146.4 jit_solution(13504337181988151782)
XLA Ops:
  7.2 0.0 copy-start
  7.2 0.0 all-gather.2.cloned.1.call-start
  7.2 0.8 convert_element_type.104
  8.1 0.8 iota_compare_fusion
  8.9 1.0 fusion.17
  9.9 0.0 copy-start.3
  9.9 0.8 convert_element_type.106
  10.8 0.7 convert_element_type.99
  11.4 0.7 convert_element_type.97
  12.1 0.7 convert_element_type.117
  12.8 2.5 %fusion.25 = f32[32,576]{1,0:T(8,128)S(1)} fusion(bf16[2048,576]{0,1:T(8,128)(2,1)} %param.27, bf16[32,2048]{1,0:T(8,128)(2,1)} %param.18, f32[2048]{0:T(1024)S(1)} %convert_element_type.97, f32[32]{0:T(128)S(1)} %add_rsqrt_fusion.3), kind=kOutput, calls=%fused_computation.47 | convolution fusion | flops 75759616 | bytes 2572416 | tf_op jit(solution)/shard_map/dot_general | solution.py:31
  15.4 0.1 multiply_reduce_fusion.2
  15.5 0.0 copy-done
  15.5 1.7 %multiply_reduce_fusion.1 = (f32[32]{0:T(128)S(1)}, f32[32,768]{1,0:T(8,128)S(1)}) fusion(bf16[2048,768]{1,0:T(8,128)(2,1)S(1)} %copy-done, bf16[32,2048]{1,0:T(8,128)(2,1)} %param.18, f32[2048]{0:T(1024)S(1)} %convert_element_type.97, f32[32]{0:T(128)S(1)} %add_rsqrt_fusion.3), kind=kOutput, calls=%fused_computation.42 | convolution fusion | flops 100974560 | bytes 3383552 | tf_op jit(solution)/shard_map/dot_general | solution.py:28
  17.2 0.1 fusion.38
  17.3 0.0 copy-start.4
  17.3 0.0 copy-done.3
  17.3 1.0 fusion.33
  18.3 6.5 %fusion.8 = bf16[32,20,512]{2,0,1:T(8,128)(2,1)S(1)} fusion(bf16[512,20,192]{0,2,1:T(8,128)(2,1)} %param.29, bf16[768,20,192]{0,2,1:T(8,128)(2,1)} %param.25, f32[32,768]{1,0:T(8,128)S(1)} %get-tuple-element.14, f32[768]{0:T(1024)S(1)} %convert_element_type.99, f32[32]{0:T(128)S(1)} %add_rsqrt_fusion.2), kind=kOutput, calls=%fused_computation.16 | convolution fusion | flops 315097088 | bytes 10587264 | tf_op jit(solution)/shard_map/bhn,chn->bhc/dot_general | solution.py:34
  24.8 0.0 copy-done.4
  24.8 0.5 fusion.10
  25.3 15.8 %fusion.12 = f32[32,20,1024]{2,1,0:T(8,128)} fusion(bf16[32,1024,512]{2,1,0:T(8,128)(2,1)} %param.19, bf16[32,20,512]{2,0,1:T(8,128)(2,1)S(1)} %fusion.8), kind=kOutput, calls=%fused_computation.22 | convolution fusion | flops 671088640 | bytes 36831232 | tf_op jit(solution)/shard_map/bhc,blc->bhl/dot_general | solution.py:35
  41.1 0.1 subtract_convert_fusion.1
  41.3 0.1 fusion.57
  41.4 0.2 subtract_convert_fusion
  41.5 0.1 pad_maximum_fusion
  41.7 0.2 fusion.20
  41.9 4.3 %fusion.39 = (f32[32,20]{1,0:T(8,128)S(1)}, f32[32,20,1024]{2,1,0:T(8,128)S(1)}) fusion(f32[32,20,1024]{2,1,0:T(8,128)} %fusion.12, bf16[32,1024,64]{1,2,0:T(8,128)(2,1)} %param.20, bf16[32,20,64]{2,0,1:T(8,128)(2,1)S(1)} %pad_maximum_fusion, pred[32,1024]{1,0:T(8,128)(4,1)S(1)} %iota_compare_fusion), kind=kOutput, calls=%fused_computation.69 | convolution fusion | flops 86506880 | bytes 9554432 | tf_op jit(solution)/shard_map/bhr,blr->bhl/dot_general | solution.py:35
  46.2 0.6 fusion
  46.9 14.1 %fusion.4 = f32[32,20,512]{2,1,0:T(8,128)} fusion(bf16[32,1024,512]{2,1,0:T(8,128)(2,1)} %param.19, f32[32,20,1024]{2,1,0:T(8,128)S(1)} %get-tuple-element.16, f32[32,20]{1,0:T(8,128)S(1)} %get-tuple-element.10, f32[32,20]{1,0:T(8,128)S(1)} %fusion.31), kind=kOutput, calls=%fused_computation.10 | convolution fusion | flops 673054720 | bytes 37491712 | tf_op jit(solution)/shard_map/bhl,blc->bhc/dot_general | solution.py:45
  60.9 0.1 copy.26
  61.0 0.0 copy-start.2
  61.0 4.2 %fusion.9 = bf16[20,4,8,256]{3,2,1,0:T(8,128)(2,1)S(1)} fusion(bf16[512,20,256]{2,0,1:T(8,128)(2,1)} %param.30, f32[32,20,512]{2,1,0:T(8,128)} %fusion.4, f32[32,512]{1,0:T(8,128)S(1)} %get-tuple-element.3, f32[32,20]{0,1:T(8,128)S(1)} %copy.26), kind=kOutput, calls=%fused_computation.19 | convolution fusion | flops 168919040 | bytes 6949376 | tf_op jit(solution)/shard_map/bhc,chv->bhv/dot_general | solution.py:46
  65.3 0.0 copy-done.2
  65.3 9.0 %multiply_reduce_fusion = (f32[32]{0:T(128)S(1)}, f32[32,2048]{1,0:T(8,128)S(1)}) fusion(bf16[32,5120]{1,0:T(8,128)(2,1)S(1)} %bitcast.34, bf16[5120,2048]{1,0:T(8,128)(2,1)} %param.31, bf16[32,2048]{1,0:T(8,128)(2,1)S(1)} %copy-done.2), kind=kOutput, calls=%fused_computation.35 | convolution fusion | flops 671481856 | bytes 21692544 | tf_op jit(solution)/shard_map/dot_general | solution.py:47
  74.3 0.8 multiply_convert_fusion
  75.1 0.0 all-gather.2.cloned.1.call-update
  75.1 0.2 reduce-scatter.2.cloned.1.call-start
  75.3 20.3 %all-gather.2.cloned.1.call-done = bf16[256,2048]{1,0:T(8,128)(2,1)} async-done(((bf16[32,2048]{1,0:T(8,128)(2,1)}), bf16[256,2048]{1,0:T(8,128)(2,1)}) %all-gather.2.cloned.1.call-update) | async-done | bytes 1048592 | tf_op jit(solution)/shard_map/all_gather | solution.py:60
  95.6 5.4 %fusion.40 = f32[256,1280]{1,0:T(8,128)} fusion(bf16[256,2048]{1,0:T(8,128)(2,1)} %all-gather.2.cloned.1.call-done, bf16[2048,1280]{1,0:T(8,128)(2,1)} %param.33), kind=kOutput, calls=%fused_computation.70 | convolution fusion | flops 1342177280 | bytes 7602176 | tf_op jit(solution)/shard_map/dot_general | solution.py:61
  101.0 0.0 copy-start.1
  101.0 9.2 %convolution_convert_fusion = bf16[256,2048]{1,0:T(8,128)(2,1)} fusion(bf16[1280,2048]{1,0:T(8,128)(2,1)} %param.35, bf16[256,2048]{1,0:T(8,128)(2,1)} %all-gather.2.cloned.1.call-done, bf16[2048,1280]{1,0:T(8,128)(2,1)} %param.34, f32[256,1280]{1,0:T(8,128)} %fusion.40), kind=kOutput, calls=%fused_computation.6 | convolution fusion | flops 2686844928 | bytes 13893632 | tf_op jit(solution)/shard_map/dot_general | solution.py:64
  110.2 0.0 reduce-scatter.2.cloned.1.call-update
  110.3 0.7 pad_maximum_fusion.1
  110.9 27.0 %reduce-scatter.2.cloned.1.call-done = bf16[32,2048]{1,0:T(8,128)(2,1)} async-done(((bf16[256,2048]{1,0:T(8,128)(2,1)}), bf16[32,2048]{1,0:T(8,128)(2,1)}) %reduce-scatter.2.cloned.1.call-update) | async-done | bytes 131088 | tf_op jit(solution)/shard_map/reduce_scatter | solution.py:65
  138.0 1.6 %add_convert_fusion.1 = bf16[32,2048]{1,0:T(8,128)(2,1)} fusion(f32[32,2048]{1,0:T(8,128)S(1)} %get-tuple-element.18, bf16[32,2048]{1,0:T(8,128)(2,1)} %reduce-scatter.2.cloned.1.call-done), kind=kLoop, calls=%fused_computation.33 | loop fusion | flops 196608 | bytes 524288 | tf_op jit(solution)/shard_map/convert_element_type | solution.py:66
  139.6 0.0 copy-done.1
  (8 shorter events, 0.1 us)
Async XLA Ops:
  7.2 8.3 %copy-start = (bf16[2048,768]{1,0:T(8,128)(2,1)S(1)}, bf16[2048,768]{1,0:T(8,128)(2,1)}, u32[]{:S(2)}) copy-start(bf16[2048,768]{1,0:T(8,128)(2,1)} %param.23) | copy-start | bytes 9437188
  7.2 88.4 %all-gather.2.cloned.1.call-start = ((), (), s32[]{:S(2)}) async-start(), calls=%async_computation.1 | async-start | bytes 1179648 | tf_op jit(solution)/shard_map/all_gather | solution.py:60
  9.9 7.4 %copy-start.3 = (bf16[768,20,64]{0,2,1:T(8,128)(2,1)S(1)}, bf16[768,20,64]{0,2,1:T(8,128)(2,1)}, u32[]{:S(2)}) copy-start(bf16[768,20,64]{0,2,1:T(8,128)(2,1)} %param.26) | copy-start | bytes 5898244
  17.3 7.5 %copy-start.4 = (bf16[32,512]{1,0:T(8,128)(2,1)}, bf16[32,512]{1,0:T(8,128)(2,1)S(1)}, u32[]{:S(2)}) copy-start(bf16[32,512]{1,0:T(8,128)(2,1)S(1)} %get-tuple-element.4) | copy-start | bytes 98308
  61.0 4.3 %copy-start.2 = (bf16[32,2048]{1,0:T(8,128)(2,1)S(1)}, bf16[32,2048]{1,0:T(8,128)(2,1)}, u32[]{:S(2)}) copy-start(bf16[32,2048]{1,0:T(8,128)(2,1)} %param.18) | copy-start | bytes 393220
  75.1 62.9 %reduce-scatter.2.cloned.1.call-start = ((), (), s32[]{:S(2)}) async-start(), calls=%async_computation.2 | async-start | bytes 1179648 | tf_op jit(solution)/shard_map/reduce_scatter | solution.py:65
  101.0 38.5 %copy-start.1 = (bf16[2048,768]{1,0:T(8,128)(2,1)S(1)}, bf16[2048,768]{1,0:T(8,128)(2,1)}, u32[]{:S(2)}) copy-start(bf16[2048,768]{1,0:T(8,128)(2,1)} %param.23) | copy-start | bytes 9437188
Sparse Core Ops, SparseCore 0:
  75.2 20.3 all-gather.1
  110.4 27.5 reduce-scatter.1
where the time goes:
time: 147 us; the launch traced here: 146 us
  matrix products  74.5 us (51%)
  waiting for transfers between devices  47.4 us (32%)
  between operations  14.2 us (10%)
  other arithmetic  9.97 us (7%)
    reduce_scatter x1, waiting for transfers between devices, local_step(): mlp_rows = lax.psum_scatter(part_sum, 'g', scatter_dimension=0, tiled=True)  27 us
    all_gather x1, waiting for transfers between devices, local_step(): group_rows = lax.all_gather(mlp_in, 'g', axis=0, tiled=True)  20.3 us
    dot_general x1, matrix products, attention_rows(): jnp.einsum('bhc,blc->bhl', q_abs, cache_lat, preferred_element_type=jnp.f...  15.8 us
    dot_general x1, matrix products, attention_rows(): jnp.einsum('bhl,blc->bhc', past_prob, cache_lat, preferred_element_type=j...  14.1 us
    dot_general x1, matrix products, local_step(): jnp.dot(act_vals, w_down, preferred_element_type=jnp.float32)  9.21 us
    dot_general x1, matrix products, attention_rows(): jnp.dot(out_heads.reshape(out_heads.shape[0], -1), w_o, preferred_element...  9.02 us
    dot_general x1, matrix products, attention_rows(): jnp.einsum('bhn,chn->bhc', q_nope, w_uk, preferred_element_type=jnp.float32)  6.49 us
    dot_general x1, matrix products, local_step(): gate_proj = jnp.dot(group_rows, w_gate, preferred_element_type=jnp.float32)  5.4 us
  transfers between devices with their start and end apart: 2, of which 2 were waited for; matrix products, arithmetic and copies ran while one was open for 0% of the time, Pallas kernels for 0%

commit v1 on v0

--- a/solution.py
+++ b/solution.py
@@ -1,6 +1,8 @@
 import jax
 import jax.numpy as jnp
 from jax import lax
+from jax.experimental import pallas as pl
+from jax.experimental.pallas import tpu as pltpu
 from jax.sharding import PartitionSpec as P
 
 
@@ -49,6 +51,141 @@
     return resid_rows, new_lat, new_rope
 
 
+MESH = pl.DeviceIdType.MESH
+
+
+def mlp_kernel(m_ref, h_ref, wg_hbm, wu_hbm, wd_hbm, out_ref, wg, wu, wd, gath, keep, s1_send, s1_recv, s2_send, s2_recv,
+               w_sems, ag_send, ag_recv, fw_send, fw_recv, p1_send, p1_recv, p2_send, p2_recv):
+    rows = m_ref.shape[0]
+    me = lax.axis_index("g")
+    core = lax.rem(me, 2)
+    chip_x = lax.rem(me // 2, 2)
+    chip_y = me // 4
+    sibling = me + 1 - 2 * core
+    mine = pl.ds(pl.multiple_of(core * rows, rows), rows)
+    theirs = pl.ds(pl.multiple_of((1 - core) * rows, rows), rows)
+
+    def peer(rel):
+        return me + (rel % 2) * (2 - 4 * chip_x) + (rel // 2) * (4 - 8 * chip_y)
+
+    def gather_copy(rel):
+        target = sibling if rel == 0 else peer(rel)
+        return pltpu.make_async_remote_copy(m_ref, gath.at[rel, mine], ag_send.at[rel], ag_recv.at[rel], device_id={"g": target}, device_id_type=MESH)
+
+    def forward_copy(rel):
+        return pltpu.make_async_remote_copy(gath.at[rel, mine], gath.at[rel, mine], fw_send.at[rel], fw_recv.at[rel], device_id={"g": sibling}, device_id_type=MESH)
+
+    def pair_copy(rel):
+        return pltpu.make_async_remote_copy(s1_send.at[rel], s1_recv.at[rel], p1_send.at[rel], p1_recv.at[rel], device_id={"g": sibling}, device_id_type=MESH)
+
+    def chip_copy(rel):
+        return pltpu.make_async_remote_copy(s2_send.at[rel], s2_recv.at[rel], p2_send.at[rel], p2_recv.at[rel], device_id={"g": peer(rel)}, device_id_type=MESH)
+
+    loads = [pltpu.make_async_copy(src, dst, w_sems.at[k]) for k, (src, dst) in enumerate(((wg_hbm, wg), (wu_hbm, wu), (wd_hbm, wd)))]
+    for load in loads:
+        load.start()
+
+    barrier = pltpu.get_barrier_semaphore()
+    for target in (sibling, peer(1), peer(2), peer(3)):
+        pl.semaphore_signal(barrier, inc=1, device_id={"g": target}, device_id_type=MESH)
+    pl.semaphore_wait(barrier, 4)
+
+    for rel in (1, 2, 3, 0):
+        gather_copy(rel).start()
+    gath[0, mine] = m_ref[...]
+    for rel in (1, 2):
+        gather_copy(rel).wait_recv()
+        forward_copy(rel).start()
+
+    def finish_pair(rel):
+        pair_copy(rel).wait_recv()
+        keep[rel] = keep[rel] + s1_recv[rel]
+
+        @pl.when(rel > 0)
+        def _():
+            s2_send[rel] = keep[rel].astype(jnp.bfloat16)
+            chip_copy(rel).start()
+
+    for load in loads:
+        load.wait()
+
+    def block(step, _):
+        rel = lax.rem(step + 1, 4)
+
+        @pl.when(step == 1)
+        def _():
+            gather_copy(3).wait_recv()
+            forward_copy(3).start()
+
+        @pl.when(step < 3)
+        def _():
+            forward_recv = pltpu.make_async_remote_copy(gath.at[rel, theirs], gath.at[rel, theirs], fw_send.at[rel], fw_recv.at[rel], device_id={"g": sibling}, device_id_type=MESH)
+            forward_recv.wait_recv()
+
+        @pl.when(step == 3)
+        def _():
+            pltpu.make_async_remote_copy(m_ref, gath.at[0, theirs], ag_send.at[0], ag_recv.at[0], device_id={"g": sibling}, device_id_type=MESH).wait_recv()
+
+        block_rows = gath[rel]
+        gate = jnp.dot(block_rows, wg[...], preferred_element_type=jnp.float32)
+        up = jnp.dot(block_rows, wu[...], preferred_element_type=jnp.float32)
+        act = (jax.nn.silu(gate) * up).astype(jnp.bfloat16)
+
+        @pl.when(step > 0)
+        def _():
+            finish_pair(step)
+
+        part = jnp.dot(act, wd[...], preferred_element_type=jnp.float32)
+        low, high = part[:rows], part[rows:]
+        is_low = core == 0
+        keep[rel] = jnp.where(is_low, low, high)
+        s1_send[rel] = jnp.where(is_low, high, low)
+        pair_copy(rel).start()
+        return 0
+
+    lax.fori_loop(0, 4, block, 0)
+    finish_pair(0)
+    total = h_ref[...].astype(jnp.float32) + keep[0]
+    for rel in (1, 2, 3):
+        chip_copy(rel).wait_recv()
+        total = total + s2_recv[rel].astype(jnp.float32)
+    out_ref[...] = total.astype(jnp.bfloat16)
+    for rel in range(4):
+        gather_copy(rel).wait_send()
+        pair_copy(rel).wait_send()
+    for rel in (1, 2, 3):
+        forward_copy(rel).wait_send()
+        chip_copy(rel).wait_send()
+
+
+def mlp_call(m, h, w_gate, w_up, w_down):
+    rows, width = m.shape
+    cols = w_gate.shape[1]
+    vmem = pl.BlockSpec(memory_space=pltpu.VMEM)
+    hbm = pl.BlockSpec(memory_space=pl.ANY)
+    dma = pltpu.SemaphoreType.DMA
+    return pl.pallas_call(
+        mlp_kernel,
+        out_shape=jax.ShapeDtypeStruct((rows, width), jnp.bfloat16),
+        in_specs=[vmem, vmem, hbm, hbm, hbm],
+        out_specs=vmem,
+        scratch_shapes=[
+            pltpu.VMEM((width, cols), jnp.bfloat16),
+            pltpu.VMEM((width, cols), jnp.bfloat16),
+            pltpu.VMEM((cols, width), jnp.bfloat16),
+            pltpu.VMEM((4, 2 * rows, width), jnp.bfloat16),
+            pltpu.VMEM((4, rows, width), jnp.float32),
+            pltpu.VMEM((4, rows, width), jnp.float32),
+            pltpu.VMEM((4, rows, width), jnp.float32),
+            pltpu.VMEM((4, rows, width), jnp.bfloat16),
+            pltpu.VMEM((4, rows, width), jnp.bfloat16),
+            dma((3,)), dma((4,)), dma((4,)), dma((4,)), dma((4,)), dma((4,)), dma((4,)), dma((4,)), dma((4,)),
+        ],
+        compiler_params=pltpu.CompilerParams(collective_id=0, has_side_effects=True, vmem_limit_bytes=48 * 1024 * 1024),
+        name="mlp_exchange",
+    )(m, h, w_gate, w_up, w_down)
+
+
 def solution(mesh):
     row_spec = P(("rep", "g"))
     full_spec = P()
@@ -57,13 +194,7 @@
     def local_step(hidden, cache_lat, cache_rope, seq_lens, gain_attn, w_dq, gain_q, w_uq, w_qr, w_dkv, gain_kv, w_uk, w_uv, w_o, gain_mlp, w_gate, w_up, w_down):
         resid_rows, new_lat, new_rope = attention_rows(hidden, cache_lat, cache_rope, seq_lens, gain_attn, w_dq, gain_q, w_uq, w_qr, w_dkv, gain_kv, w_uk, w_uv, w_o)
         mlp_in = rms_norm(resid_rows.astype(jnp.float32), gain_mlp).astype(jnp.bfloat16)
-        group_rows = lax.all_gather(mlp_in, "g", axis=0, tiled=True)
-        gate_proj = jnp.dot(group_rows, w_gate, preferred_element_type=jnp.float32)
-        up_proj = jnp.dot(group_rows, w_up, preferred_element_type=jnp.float32)
-        act_vals = (jax.nn.silu(gate_proj) * up_proj).astype(jnp.bfloat16)
-        part_sum = jnp.dot(act_vals, w_down, preferred_element_type=jnp.float32).astype(jnp.bfloat16)
-        mlp_rows = lax.psum_scatter(part_sum, "g", scatter_dimension=0, tiled=True)
-        out_hidden = (resid_rows.astype(jnp.float32) + mlp_rows.astype(jnp.float32)).astype(jnp.bfloat16)
+        out_hidden = mlp_call(mlp_in, resid_rows, w_gate, w_up, w_down)
         return out_hidden, new_lat, new_rope
 
     return jax.shard_map(local_step, mesh=mesh, in_specs=in_specs, out_specs=(row_spec, row_spec, row_spec), check_vma=False)

time: 147 us -> 97.7 us (0.66)
  waiting for transfers between devices: 47.4 us -> 0 us
  Pallas kernels: 0 us -> 26.9 us
  matrix products: 74.5 us -> 59.4 us
  between operations: 14.2 us -> 0.85 us
    reduce_scatter x1 -> x0, waiting for transfers between devices: 27 us -> none  [local_step(): mlp_rows = lax.psum_scatter(part_sum, 'g', scatter_dimension=0, tiled=True)]
    pallas_call x0 -> x1, Pallas kernels: none -> 26.9 us  [mlp_call(): pl.pallas_call(mlp_kernel, out_shape=jax.ShapeDtypeStruct((rows, width),...]
    all_gather x1 -> x0, waiting for transfers between devices: 20.3 us -> none  [local_step(): group_rows = lax.all_gather(mlp_in, 'g', axis=0, tiled=True)]
    dot_general x2 -> x0, matrix products: 14.6 us -> none  [the longest x1 9.21 us: local_step(): jnp.dot(act_vals, w_down, preferred_element_type=jnp.float32)]
    convert_element_type x1 -> x0, other arithmetic: 1.58 us -> none  [local_step(): (resid_rows.astype(jnp.float32) + mlp_rows.astype(jnp.float32)).astype(jn...]
  transfers between devices with their start and end apart: 2 -> 0, of which waited for: 2 -> 0; matrix products, arithmetic and copies ran while one was open for 0% -> 0% of each run, Pallas kernels for 0% -> 0%
where the time goes in v1:
time: 97.7 us; the launch traced here: 97.4 us
  matrix products  59.4 us (61%)
  Pallas kernels  26.9 us (28%)
  other arithmetic  9.53 us (10%)
    pallas_call x1, Pallas kernels, mlp_call(): pl.pallas_call(mlp_kernel, out_shape=jax.ShapeDtypeStruct((rows, width),...  26.9 us
    dot_general x1, matrix products, attention_rows(): jnp.einsum('bhc,blc->bhl', q_abs, cache_lat, preferred_element_type=jnp.f...  15.9 us
    dot_general x1, matrix products, attention_rows(): jnp.einsum('bhl,blc->bhc', past_prob, cache_lat, preferred_element_type=j...  14.1 us
    dot_general x1, matrix products, attention_rows(): jnp.dot(out_heads.reshape(out_heads.shape[0], -1), w_o, preferred_element...  9.19 us
    dot_general x1, matrix products, attention_rows(): jnp.einsum('bhn,chn->bhc', q_nope, w_uk, preferred_element_type=jnp.float32)  6.5 us
    dot_general x1, matrix products, attention_rows(): jnp.einsum('bhr,blr->bhl', q_rope, cache_rope, preferred_element_type=jnp...  4.28 us
    dot_general x1, matrix products, attention_rows(): jnp.einsum('bhc,chv->bhv', mixed_lat, w_uv, preferred_element_type=jnp.fl...  4.18 us
    convert_element_type x4, other arithmetic, rms_norm(): return values * lax.rsqrt(mean_sq + 1e-06) * gain_vec.astype(jnp.float32)  3.33 us

profile of v1, /device:TPU:0, one launch (start us, length us, event | category | flops | bytes accessed | tf_op | source)
XLA Modules:
  0.0 97.4 jit_solution(2211040205762655977)
XLA Ops:
  0.6 0.0 copy-start
  0.6 0.0 copy-start.2
  0.7 0.8 convert_element_type.91
  1.5 1.2 %fusion.18 = f32[32]{0:T(128)S(1)} fusion(bf16[32,2048]{1,0:T(8,128)(2,1)} %param.18), kind=kLoop, calls=%fused_computation.31 | loop fusion | flops 196576 | bytes 131200 | tf_op jit(solution)/shard_map/reduce_sum | solution.py:10
  2.7 0.7 convert_element_type.93
  3.4 0.7 convert_element_type.86
  4.1 0.7 convert_element_type.84
  4.8 1.3 %convert_element_type.104 = f32[2048]{0:T(1024)} convert(bf16[2048]{0:T(1024)(128)(2,1)} %param.32) | non-fusion elementwise | flops 2048 | bytes 12288 | tf_op jit(solution)/shard_map/convert_element_type | solution.py:11
  6.0 1.4 %iota_compare_fusion = pred[32,1024]{1,0:T(8,128)(4,1)} fusion(s32[32]{0:T(128)} %param.21), kind=kLoop, calls=%fused_computation.38 | loop fusion | flops 32768 | bytes 32896 | tf_op jit(solution)/shard_map/lt | solution.py:40
  7.4 2.7 %fusion.26 = f32[32,576]{1,0:T(8,128)S(1)} fusion(bf16[2048,576]{0,1:T(8,128)(2,1)} %param.27, bf16[32,2048]{1,0:T(8,128)(2,1)} %param.18, f32[2048]{0:T(1024)S(1)} %convert_element_type.84, f32[32]{0:T(128)S(1)} %add_rsqrt_fusion.3), kind=kOutput, calls=%fused_computation.45 | convolution fusion | flops 75759616 | bytes 2572416 | tf_op jit(solution)/shard_map/dot_general | solution.py:33
  10.0 0.1 multiply_reduce_fusion.1
  10.2 0.1 subtract_convert_fusion.1
  10.3 0.1 fusion.51
  10.4 0.7 pad_maximum_fusion.1
  11.1 0.7 fusion.38
  11.8 0.0 copy-done
  11.8 0.0 copy-done.2
  11.8 0.8 multiply_reduce_fusion
  12.6 0.0 copy-done.6
  12.6 0.0 copy-done.3
  12.6 1.0 %fusion.33 = f32[32,20,64]{2,0,1:T(8,128)S(1)} fusion(bf16[768,20,64]{0,2,1:T(8,128)(2,1)S(1)} %copy-done.3, f32[32,768]{1,0:T(8,128)S(1)} %get-tuple-element.14, f32[768]{0:T(1024)S(1)} %convert_element_type.86, f32[32]{0:T(128)S(1)} %add_rsqrt_fusion.2), kind=kOutput, calls=%fused_computation.63 | convolution fusion | flops 62988288 | bytes 2231424 | tf_op jit(solution)/shard_map/bq,qhr->bhr/dot_general | solution.py:32
  13.7 0.2 subtract_convert_fusion
  13.9 0.1 pad_maximum_fusion
  14.0 0.2 fusion.21
  14.2 6.5 %fusion.6 = bf16[32,20,512]{2,0,1:T(8,128)(2,1)S(1)} fusion(bf16[512,20,192]{0,2,1:T(8,128)(2,1)} %param.29, bf16[768,20,192]{0,2,1:T(8,128)(2,1)} %param.25, f32[32,768]{1,0:T(8,128)S(1)} %get-tuple-element.14, f32[768]{0:T(1024)} %copy-done.6, f32[32]{0:T(128)S(1)} %add_rsqrt_fusion.2), kind=kOutput, calls=%fused_computation.12 | convolution fusion | flops 315097088 | bytes 10587264 | tf_op jit(solution)/shard_map/bhn,chn->bhc/dot_general | solution.py:36
  20.7 0.0 copy-done.8
  20.7 0.5 fusion.8
  21.2 15.9 %fusion.10 = f32[32,20,1024]{2,1,0:T(8,128)} fusion(bf16[32,1024,512]{2,1,0:T(8,128)(2,1)} %param.19, bf16[32,20,512]{2,0,1:T(8,128)(2,1)S(1)} %fusion.6), kind=kOutput, calls=%fused_computation.18 | convolution fusion | flops 671088640 | bytes 36831232 | tf_op jit(solution)/shard_map/bhc,blc->bhl/dot_general | solution.py:37
  37.1 0.0 copy-done.5
  37.1 4.3 %fusion.39 = (f32[32,20]{1,0:T(8,128)S(1)}, f32[32,20,1024]{2,1,0:T(8,128)S(1)}) fusion(f32[32,20,1024]{2,1,0:T(8,128)} %fusion.10, bf16[32,1024,64]{1,2,0:T(8,128)(2,1)} %param.20, bf16[32,20,64]{2,0,1:T(8,128)(2,1)S(1)} %pad_maximum_fusion, pred[32,1024]{1,0:T(8,128)(4,1)S(1)} %copy-done.5), kind=kOutput, calls=%fused_computation.66 | convolution fusion | flops 86506880 | bytes 9554432 | tf_op jit(solution)/shard_map/bhr,blr->bhl/dot_general | solution.py:37
  41.4 0.6 fusion
  42.1 0.0 copy-start.4
  42.1 14.1 %fusion.2 = f32[32,20,512]{2,1,0:T(8,128)} fusion(bf16[32,1024,512]{2,1,0:T(8,128)(2,1)} %param.19, f32[32,20,1024]{2,1,0:T(8,128)S(1)} %get-tuple-element.16, f32[32,20]{1,0:T(8,128)S(1)} %get-tuple-element.10, f32[32,20]{1,0:T(8,128)S(1)} %fusion.32), kind=kOutput, calls=%fused_computation.6 | convolution fusion | flops 673054720 | bytes 37491712 | tf_op jit(solution)/shard_map/bhl,blc->bhc/dot_general | solution.py:47
  56.2 0.1 copy.26
  56.3 0.0 copy-done.4
  56.3 4.2 %fusion.7 = bf16[20,4,8,256]{3,2,1,0:T(8,128)(2,1)S(1)} fusion(bf16[512,20,256]{2,0,1:T(8,128)(2,1)} %param.30, f32[32,20,512]{2,1,0:T(8,128)} %fusion.2, f32[32,512]{1,0:T(8,128)S(1)} %copy-done.4, f32[32,20]{0,1:T(8,128)S(1)} %copy.26), kind=kOutput, calls=%fused_computation.15 | convolution fusion | flops 168919040 | bytes 6949376 | tf_op jit(solution)/shard_map/bhc,chv->bhv/dot_general | solution.py:48
  60.5 0.0 slice-start
  60.5 0.0 copy-start.7
  60.6 0.0 slice-start.1
  60.6 9.2 %fusion.15 = (f32[32]{0:T(128)S(1)}, bf16[32,2048]{1,0:T(8,128)(2,1)S(1)}) fusion(bf16[32,5120]{1,0:T(8,128)(2,1)S(1)} %bitcast.31, bf16[5120,2048]{1,0:T(8,128)(2,1)} %param.31, bf16[32,2048]{1,0:T(8,128)(2,1)S(1)} %copy-done.2), kind=kOutput, calls=%fused_computation.28 | convolution fusion | flops 671481856 | bytes 21561472 | tf_op jit(solution)/shard_map/dot_general | solution.py:49
  69.8 0.0 copy-done.7
  69.8 0.1 fusion.17.m_ref
  69.9 0.0 slice-done
  69.9 0.0 slice-done.1
  69.9 0.0 copy-start.1
  69.9 26.9 %mlp_exchange.1 = bf16[32,2048]{1,0:T(8,128)(2,1)S(1)} custom-call(bf16[32,2048]{1,0:T(8,128)(2,1)S(1)} %fusion.17.m_ref, bf16[32,2048]{1,0:T(8,128)(2,1)S(1)} %get-tuple-element.18.h_ref, bf16[2048,1280]{1,0:T(8,128)(2,1)S(1)} %bitcast.30, bf16[2048,1280]{1,0:T(8,128)(2,1)} %wu_hbm.1, bf16[1280,2048]{1,0:T(8,128)(2,1)} %wd_hbm.1), custom_call_target="tpu_custom_call" | custom-call | tf_op jit(solution)/shard_map/mlp_exchange/pallas_call | solution.py:167
  96.8 0.7 copy.53
  97.4 0.0 copy-done.1
  (13 shorter events, 0.1 us)
Async XLA Ops:
  0.6 11.2 %copy-start = (bf16[2048,768]{1,0:T(8,128)(2,1)S(1)}, bf16[2048,768]{1,0:T(8,128)(2,1)}, u32[]{:S(2)}) copy-start(bf16[2048,768]{1,0:T(8,128)(2,1)} %param.23) | copy-start | bytes 9437188
  0.6 11.2 %copy-start.2 = (bf16[32,2048]{1,0:T(8,128)(2,1)S(1)}, bf16[32,2048]{1,0:T(8,128)(2,1)}, u32[]{:S(2)}) copy-start(bf16[32,2048]{1,0:T(8,128)(2,1)} %param.18) | copy-start | bytes 393220
  4.1 8.6 %copy-start.6 = (f32[768]{0:T(1024)}, f32[768]{0:T(1024)S(1)}, u32[]{:S(2)}) copy-start(f32[768]{0:T(1024)S(1)} %convert_element_type.86) | copy-start | bytes 9220
  7.4 5.3 %copy-start.3 = (bf16[768,20,64]{0,2,1:T(8,128)(2,1)S(1)}, bf16[768,20,64]{0,2,1:T(8,128)(2,1)}, u32[]{:S(2)}) copy-start(bf16[768,20,64]{0,2,1:T(8,128)(2,1)} %param.26) | copy-start | bytes 5898244
  14.2 6.5 %copy-start.8 = (bf16[32,512]{1,0:T(8,128)(2,1)S(1)}, bf16[32,512]{1,0:T(8,128)(2,1)}, u32[]{:S(2)}) copy-start(bf16[32,512]{1,0:T(8,128)(2,1)} %get-tuple-element.23) | copy-start | bytes 98308
  21.2 16.0 %copy-start.5 = (pred[32,1024]{1,0:T(8,128)(4,1)S(1)}, pred[32,1024]{1,0:T(8,128)(4,1)}, u32[]{:S(2)}) copy-start(pred[32,1024]{1,0:T(8,128)(4,1)} %iota_compare_fusion) | copy-start | bytes 98308
  42.1 14.2 %copy-start.4 = (f32[32,512]{1,0:T(8,128)S(1)}, f32[32,512]{1,0:T(8,128)}, u32[]{:S(2)}) copy-start(f32[32,512]{1,0:T(8,128)} %get-tuple-element.3) | copy-start | bytes 196612
  60.5 9.4 %slice-start = ((s8[5242880]{0:T(1024)(128)(4,1)}), s8[4194304]{0:T(1024)(128)(4,1)S(1)}, s32[]{:S(2)}) async-start(s8[5242880]{0:T(1024)(128)(4,1)} %bitcast.29), calls=%async_computation | async-start | bytes 8388608
  60.5 9.2 %copy-start.7 = (f32[2048]{0:T(1024)S(1)}, f32[2048]{0:T(1024)}, u32[]{:S(2)}) copy-start(f32[2048]{0:T(1024)} %convert_element_type.104) | copy-start | bytes 24580
  60.6 9.3 %slice-start.1 = ((s8[5242880]{0:T(1024)(128)(4,1)}), s8[1048576]{0:T(1024)(128)(4,1)S(1)}, s32[]{:S(2)}) async-start(s8[5242880]{0:T(1024)(128)(4,1)} %bitcast.29), calls=%async_computation.1 | async-start | bytes 2097152
  69.9 27.5 %copy-start.1 = (bf16[2048,768]{1,0:T(8,128)(2,1)S(1)}, bf16[2048,768]{1,0:T(8,128)(2,1)}, u32[]{:S(2)}) copy-start(bf16[2048,768]{1,0:T(8,128)(2,1)} %param.23) | copy-start | bytes 9437188

commit v2 on v1

--- a/solution.py
+++ b/solution.py
@@ -6,49 +6,223 @@
 from jax.sharding import PartitionSpec as P
 
 
-def rms_norm(values, gain_vec):
-    mean_sq = jnp.mean(jnp.square(values), axis=-1, keepdims=True)
-    return values * lax.rsqrt(mean_sq + 1e-6) * gain_vec.astype(jnp.float32)
-
-
-def apply_rope(values, positions):
-    half_dim = values.shape[-1] // 2
-    inv_freq = 10000.0 ** (-jnp.arange(half_dim).astype(jnp.float32) / half_dim)
-    angles = positions.astype(jnp.float32)[..., None] * inv_freq
-    cos_part = jnp.cos(angles)
-    sin_part = jnp.sin(angles)
-    first_half = values[..., :half_dim]
-    second_half = values[..., half_dim:]
-    return jnp.concatenate([first_half * cos_part - second_half * sin_part, first_half * sin_part + second_half * cos_part], axis=-1)
-
-
-def attention_rows(hidden, cache_lat, cache_rope, seq_lens, gain_attn, w_dq, gain_q, w_uq, w_qr, w_dkv, gain_kv, w_uk, w_uv, w_o):
-    kv_dim = w_uk.shape[0]
-    cache_len = cache_lat.shape[1]
-    score_scale = (w_uq.shape[2] + w_qr.shape[2]) ** -0.5
-    normed = rms_norm(hidden.astype(jnp.float32), gain_attn).astype(jnp.bfloat16)
-    q_in = rms_norm(jnp.dot(normed, w_dq, preferred_element_type=jnp.float32), gain_q).astype(jnp.bfloat16)
-    q_nope = jnp.einsum("bq,qhn->bhn", q_in, w_uq, preferred_element_type=jnp.float32).astype(jnp.bfloat16)
-    q_rope = apply_rope(jnp.einsum("bq,qhr->bhr", q_in, w_qr, preferred_element_type=jnp.float32), seq_lens[:, None]).astype(jnp.bfloat16)
-    kv_raw = jnp.dot(normed, w_dkv, preferred_element_type=jnp.float32)
-    new_lat = rms_norm(kv_raw[:, :kv_dim], gain_kv).astype(jnp.bfloat16)
-    new_rope = apply_rope(kv_raw[:, kv_dim:], seq_lens).astype(jnp.bfloat16)
-    q_abs = jnp.einsum("bhn,chn->bhc", q_nope, w_uk, preferred_element_type=jnp.float32).astype(jnp.bfloat16)
-    past_score = (jnp.einsum("bhc,blc->bhl", q_abs, cache_lat, preferred_element_type=jnp.float32) + jnp.einsum("bhr,blr->bhl", q_rope, cache_rope, preferred_element_type=jnp.float32)) * score_scale
-    own_score = (jnp.einsum("bhc,bc->bh", q_abs, new_lat, preferred_element_type=jnp.float32) + jnp.einsum("bhr,br->bh", q_rope, new_rope, preferred_element_type=jnp.float32)) * score_scale
-    key_pos = lax.broadcasted_iota(jnp.int32, (1, 1, cache_len), 2)
-    past_score = jnp.where(key_pos < seq_lens[:, None, None], past_score, -jnp.inf)
-    row_max = jnp.maximum(jnp.max(past_score, axis=-1), own_score)
-    past_exp = jnp.exp(past_score - row_max[..., None])
-    own_exp = jnp.exp(own_score - row_max)
-    row_total = jnp.sum(past_exp, axis=-1) + own_exp
-    past_prob = (past_exp / row_total[..., None]).astype(jnp.bfloat16)
-    own_prob = (own_exp / row_total).astype(jnp.bfloat16)
-    mixed_lat = (jnp.einsum("bhl,blc->bhc", past_prob, cache_lat, preferred_element_type=jnp.float32) + own_prob.astype(jnp.float32)[..., None] * new_lat.astype(jnp.float32)[:, None, :]).astype(jnp.bfloat16)
-    out_heads = jnp.einsum("bhc,chv->bhv", mixed_lat, w_uv, preferred_element_type=jnp.float32).astype(jnp.bfloat16)
-    attn_out = jnp.dot(out_heads.reshape(out_heads.shape[0], -1), w_o, preferred_element_type=jnp.float32)
-    resid_rows = (hidden.astype(jnp.float32) + attn_out).astype(jnp.bfloat16)
-    return resid_rows, new_lat, new_rope
+HEADS = 20
+HEAD_PAD = 24
+RING = 12
+GROUP = 4
+
+
+def attn_kernel(lens_ref, hid_ref, ga_ref, gq_ref, gkv_ref, gm_ref, lat_hbm, rope_hbm, wdq_hbm, wdkv_hbm, wqr_hbm, wuq_hbm, wuk_hbm, wuv_hbm, wo_hbm,
+                resid_ref, mlp_ref, newlat_ref, newrope_ref,
+                wdq, wdkv, wqr, wuq, wuk, wuv, wo, lat_buf, rope_buf, q_scr, qr_scr, o_scr, nl_scr, nr_scr, heads_scr,
+                w_sems, o_sems, lat_sems, rope_sems):
+    rows = hid_ref.shape[0]
+    kv_dim = lat_buf.shape[2]
+    rope_dim = rope_buf.shape[1]
+    cache_len = lat_buf.shape[1]
+    nope_dim = wuk.shape[1]
+    v_dim = wuv.shape[2]
+    half = rope_dim // 2
+    f32, bf16 = jnp.float32, jnp.bfloat16
+    nt = (((1,), (1,)), ((), ()))
+
+    early = [pltpu.make_async_copy(src, dst, w_sems.at[k]) for k, (src, dst) in enumerate(((wdq_hbm, wdq), (wdkv_hbm, wdkv), (wqr_hbm, wqr), (wuq_hbm, wuq), (wuk_hbm, wuk)))]
+    for copy in early:
+        copy.start()
+
+    def lat_copy(row, slot):
+        count = pl.multiple_of(((lens_ref[row] + 15) // 16) * 16, 16)
+        return pltpu.make_async_copy(lat_hbm.at[row, pl.ds(0, count)], lat_buf.at[slot, pl.ds(0, count)], lat_sems.at[slot])
+
+    def rope_copy(row, slot):
+        return pltpu.make_async_copy(rope_hbm.at[row], rope_buf.at[slot], rope_sems.at[slot])
+
+    def start_row(row, slot):
+        lat_copy(row, slot).start()
+        rope_copy(row, slot).start()
+
+    def uv_copy(head):
+        return pltpu.make_async_copy(wuv_hbm.at[head], wuv.at[head], o_sems.at[0])
+
+    wo_rows = wo.shape[0] // rows
+
+    def wo_copy(part):
+        span = pl.ds(pl.multiple_of(part * wo_rows, 32), wo_rows)
+        return pltpu.make_async_copy(wo_hbm.at[span], wo.at[span], o_sems.at[1])
+
+    def clear_and_start(slot, _):
+        lat_buf[slot, pl.ds(256, cache_len - 256)] = jnp.zeros((cache_len - 256, kv_dim), bf16)
+        start_row(slot, slot)
+        return 0
+
+    lax.fori_loop(0, RING, clear_and_start, 0)
+
+    def norm(values, gain_ref):
+        mean_sq = jnp.mean(values * values, axis=-1, keepdims=True)
+        return values * lax.rsqrt(mean_sq + 1e-6) * gain_ref[...].astype(f32)
+
+    row_id = lax.broadcasted_iota(jnp.int32, (rows, 128), 0)
+    position = jnp.zeros((rows, 128), jnp.int32)
+    for row in range(rows):
+        position = jnp.where(row_id == row, lens_ref[row], position)
+    lane = lax.broadcasted_iota(jnp.int32, (rows, 128), 1)
+    freq_id = lane & (half - 1)
+    inv_freq = jnp.exp(freq_id.astype(f32) * (-jnp.log(jnp.float32(10000.0)) / half))
+    angle = position.astype(f32) * inv_freq
+    first_half = (lane & half) == 0
+    cos_part = jnp.cos(angle)
+    sin_part = jnp.where(first_half, -jnp.sin(angle), jnp.sin(angle))
+
+    def rotate(values):
+        swapped = jnp.where(first_half, pltpu.roll(values, 128 - half, 1), pltpu.roll(values, half, 1))
+        return values * cos_part + swapped * sin_part
+
+    hidden = hid_ref[...].astype(f32)
+    normed = norm(hidden, ga_ref).astype(bf16)
+    q_scr[...] = jnp.zeros_like(q_scr)
+    qr_scr[...] = jnp.zeros_like(qr_scr)
+
+    early[0].wait()
+    q_in = norm(jnp.dot(normed, wdq[...], preferred_element_type=f32), gq_ref).astype(bf16)
+    early[1].wait()
+    kv_raw = lax.dot_general(normed, wdkv[...], nt, preferred_element_type=f32)
+    new_lat = norm(kv_raw[:, :kv_dim], gkv_ref).astype(bf16)
+    newlat_ref[...] = new_lat
+    nl_scr[...] = new_lat.astype(f32)
+    kv_rope = jnp.concatenate([kv_raw[:, kv_dim:], jnp.zeros((rows, 128 - rope_dim), f32)], axis=1)
+    new_rope = rotate(kv_rope).astype(bf16)
+    newrope_ref[...] = new_rope[:, :rope_dim]
+    low_lanes = lane < rope_dim
+    nr_scr[...] = jnp.where(low_lanes, new_rope.astype(f32), 0.0)
+
+    early[2].wait()
+    for pair in range(HEADS // 2):
+        raw = lax.dot_general(q_in, wqr[pl.ds(pair * 128, 128)], nt, preferred_element_type=f32)
+        turned = rotate(raw).astype(bf16).astype(f32)
+        qr_scr[pl.ds(2 * pair, rows, stride=HEAD_PAD), :] = turned
+        qr_scr[pl.ds(2 * pair + 1, rows, stride=HEAD_PAD), :] = pltpu.roll(turned, rope_dim, 1)
+
+    early[3].wait()
+    early[4].wait()
+    for quad in range(HEADS // 4):
+        q_nope = lax.dot_general(q_in, wuq[pl.ds(quad * 4 * nope_dim, 4 * nope_dim)], nt, preferred_element_type=f32)
+        for sub in range(4):
+            head = quad * 4 + sub
+            one = q_nope[:, sub * nope_dim:(sub + 1) * nope_dim].astype(bf16)
+            q_abs = jnp.dot(one, wuk[head], preferred_element_type=f32).astype(bf16).astype(f32)
+            for col in range(kv_dim // 128):
+                q_scr[col, pl.ds(head, rows, stride=HEAD_PAD), :] = q_abs[:, col * 128:(col + 1) * 128]
+
+    scale = (nope_dim + rope_dim) ** -0.5
+    key_pos = lax.broadcasted_iota(jnp.int32, (HEAD_PAD, cache_len), 1)
+
+    def attend(row, slot):
+        head_rows = pl.ds(pl.multiple_of(row * HEAD_PAD, 8), HEAD_PAD)
+        q_cols = [q_scr[col, head_rows, :] for col in range(kv_dim // 128)]
+        q_lat = jnp.concatenate(q_cols, axis=1)
+        q_rope = qr_scr[head_rows, :]
+        lat = lat_buf[slot]
+        own_lat = nl_scr[pl.ds(row, 1), :]
+        score = lax.dot_general(q_lat.astype(bf16), lat, nt, preferred_element_type=f32)
+        score = score + jnp.dot(q_rope[:, :rope_dim].astype(bf16), rope_buf[slot], preferred_element_type=f32)
+        score = jnp.where(key_pos < lens_ref[row], score * scale, -jnp.inf)
+        own = jnp.sum(q_lat * own_lat, axis=-1, keepdims=True) + jnp.sum(q_rope * nr_scr[pl.ds(row, 1), :], axis=-1, keepdims=True)
+        own = own * scale
+        top = jnp.maximum(jnp.max(score, axis=-1, keepdims=True), own)
+        weight = jnp.exp(score - top)
+        own_weight = jnp.exp(own - top)
+        total = jnp.sum(weight, axis=-1, keepdims=True) + own_weight
+        prob = (weight / total).astype(bf16)
+        own_prob = (own_weight / total).astype(bf16).astype(f32)
+        mixed = jnp.dot(prob, lat, preferred_element_type=f32) + own_prob * own_lat
+        mixed = mixed.astype(bf16).astype(f32)
+        for col in range(kv_dim // 128):
+            o_scr[col, head_rows, :] = mixed[:, col * 128:(col + 1) * 128]
+
+    def group_step(group, _):
+        base = group * GROUP
+        for sub in range(GROUP):
+            part = base + sub
+            wo_copy(part).start()
+
+            @pl.when(part < HEADS)
+            def _():
+                uv_copy(part).start()
+        slots = [lax.rem(base, RING) + sub for sub in range(GROUP)]
+        for sub in range(GROUP):
+            lat_copy(base + sub, slots[sub]).wait()
+            rope_copy(base + sub, slots[sub]).wait()
+        for sub in range(GROUP):
+            attend(base + sub, slots[sub])
+
+        @pl.when(base + RING < rows)
+        def _():
+            for sub in range(GROUP):
+                start_row(base + RING + sub, slots[sub])
+        return 0
+
+    lax.fori_loop(0, rows // GROUP, group_step, 0)
+
+    pltpu.make_async_copy(wuv_hbm, wuv, o_sems.at[0]).wait()
+    for head in range(HEADS):
+        cols = [o_scr[col, pl.ds(head, rows, stride=HEAD_PAD), :] for col in range(kv_dim // 128)]
+        mixed = jnp.concatenate(cols, axis=1).astype(bf16)
+        heads_scr[:, head * v_dim:(head + 1) * v_dim] = jnp.dot(mixed, wuv[head], preferred_element_type=f32).astype(bf16)
+    pltpu.make_async_copy(wo_hbm, wo, o_sems.at[1]).wait()
+    attn_out = jnp.dot(heads_scr[...], wo[...], preferred_element_type=f32)
+    resid = (hid_ref[...].astype(f32) + attn_out).astype(bf16)
+    resid_ref[...] = resid
+    mlp_ref[...] = norm(resid.astype(f32), gm_ref).astype(bf16)
+
+
+def attn_call(hidden, cache_lat, cache_rope, seq_lens, gain_attn, w_dq, gain_q, w_uq, w_qr, w_dkv, gain_kv, w_uk, w_uv, w_o, gain_mlp):
+    rows, width = hidden.shape
+    cache_len, kv_dim = cache_lat.shape[1:]
+    rope_dim = cache_rope.shape[2]
+    q_dim, heads, nope_dim = w_uq.shape
+    v_dim = w_uv.shape[2]
+    bf16, f32 = jnp.bfloat16, jnp.float32
+    vmem = pl.BlockSpec(memory_space=pltpu.VMEM)
+    smem = pl.BlockSpec(memory_space=pltpu.SMEM)
+    hbm = pl.BlockSpec(memory_space=pl.ANY)
+    dma = pltpu.SemaphoreType.DMA
+    rope_keys = jnp.swapaxes(cache_rope, 1, 2)
+    dkv_t = w_dkv.T
+    qr_t = jnp.transpose(w_qr, (1, 2, 0)).reshape(heads * rope_dim, q_dim)
+    uq_t = jnp.transpose(w_uq, (1, 2, 0)).reshape(heads * nope_dim, q_dim)
+    uk_t = jnp.transpose(w_uk, (1, 2, 0))
+    uv_t = jnp.swapaxes(w_uv, 0, 1)
+    return pl.pallas_call(
+        attn_kernel,
+        out_shape=(
+            jax.ShapeDtypeStruct((rows, width), bf16),
+            jax.ShapeDtypeStruct((rows, width), bf16),
+            jax.ShapeDtypeStruct((rows, kv_dim), bf16),
+            jax.ShapeDtypeStruct((rows, rope_dim), bf16),
+        ),
+        in_specs=[smem, vmem, vmem, vmem, vmem, vmem] + [hbm] * 9,
+        out_specs=(vmem, vmem, vmem, vmem),
+        scratch_shapes=[
+            pltpu.VMEM(w_dq.shape, bf16),
+            pltpu.VMEM(dkv_t.shape, bf16),
+            pltpu.VMEM(qr_t.shape, bf16),
+            pltpu.VMEM(uq_t.shape, bf16),
+            pltpu.VMEM(uk_t.shape, bf16),
+            pltpu.VMEM(uv_t.shape, bf16),
+            pltpu.VMEM(w_o.shape, bf16),
+            pltpu.VMEM((RING, cache_len, kv_dim), bf16),
+            pltpu.VMEM((RING, rope_dim, cache_len), bf16),
+            pltpu.VMEM((kv_dim // 128, rows * HEAD_PAD, 128), f32),
+            pltpu.VMEM((rows * HEAD_PAD, 128), f32),
+            pltpu.VMEM((kv_dim // 128, rows * HEAD_PAD, 128), f32),
+            pltpu.VMEM((rows, kv_dim), f32),
+            pltpu.VMEM((rows, 128), f32),
+            pltpu.VMEM((rows, heads * v_dim), bf16),
+            dma((5,)), dma((2,)), dma((RING,)), dma((RING,)),
+        ],
+        compiler_params=pltpu.CompilerParams(vmem_limit_bytes=67043328),
+        name="attention",
+    )(seq_lens, hidden, gain_attn, gain_q, gain_kv, gain_mlp, cache_lat, rope_keys, w_dq, dkv_t, qr_t, uq_t, uk_t, uv_t, w_o)
 
 
 MESH = pl.DeviceIdType.MESH
@@ -192,8 +366,7 @@
     in_specs = (row_spec, row_spec, row_spec, row_spec, full_spec, full_spec, full_spec, full_spec, full_spec, full_spec, full_spec, full_spec, full_spec, full_spec, full_spec, P(None, "g"), P(None, "g"), P("g", None))
 
     def local_step(hidden, cache_lat, cache_rope, seq_lens, gain_attn, w_dq, gain_q, w_uq, w_qr, w_dkv, gain_kv, w_uk, w_uv, w_o, gain_mlp, w_gate, w_up, w_down):
-        resid_rows, new_lat, new_rope = attention_rows(hidden, cache_lat, cache_rope, seq_lens, gain_attn, w_dq, gain_q, w_uq, w_qr, w_dkv, gain_kv, w_uk, w_uv, w_o)
-        mlp_in = rms_norm(resid_rows.astype(jnp.float32), gain_mlp).astype(jnp.bfloat16)
+        resid_rows, mlp_in, new_lat, new_rope = attn_call(hidden, cache_lat, cache_rope, seq_lens, gain_attn, w_dq, gain_q, w_uq, w_qr, w_dkv, gain_kv, w_uk, w_uv, w_o, gain_mlp)
         out_hidden = mlp_call(mlp_in, resid_rows, w_gate, w_up, w_down)
         return out_hidden, new_lat, new_rope
 

time: 97.7 us -> 74.2 us (0.76)
  matrix products: 59.4 us -> 0 us
  Pallas kernels: 26.9 us -> 68.4 us
  other arithmetic: 9.53 us -> 0 us
  local copies, waits for them, and re-layouts: 0.83 us -> 4.95 us
    dot_general x11 -> x0, matrix products: 59.4 us -> none  [the longest x1 15.9 us: attention_rows(): jnp.einsum('bhc,blc->bhl', q_abs, cache_lat, preferred_element_type=jnp.f...]
    pallas_call x0 -> x1, Pallas kernels: none -> 41.6 us  [attn_call(): pl.pallas_call(attn_kernel, out_shape=(jax.ShapeDtypeStruct((rows, width)...]
    convert_element_type x8 -> x0, other arithmetic: 4.97 us -> none  [the longest x4 3.33 us: rms_norm(): return values * lax.rsqrt(mean_sq + 1e-06) * gain_vec.astype(jnp.float32)]
    unnamed x23 -> x7, local copies, waits for them, and re-layouts: 0.73 us -> 4.95 us
    reduce_sum x3 -> x0, other arithmetic: 1.94 us -> none  [the longest x2 1.33 us: rms_norm(): mean_sq = jnp.mean(jnp.square(values), axis=-1, keepdims=True)]
    lt x1 -> x0, other arithmetic: 1.35 us -> none  [attention_rows(): key_pos < seq_lens[:, None, None]]
where the time goes in v2:
time: 74.2 us; the launch traced here: 74 us
  Pallas kernels  68.4 us (92%)
  local copies, waits for them, and re-layouts  4.95 us (7%)
    pallas_call x1, Pallas kernels, attn_call(): pl.pallas_call(attn_kernel, out_shape=(jax.ShapeDtypeStruct((rows, width)...  41.6 us
    pallas_call x1, Pallas kernels, mlp_call(): pl.pallas_call(mlp_kernel, out_shape=jax.ShapeDtypeStruct((rows, width),...  26.8 us
    unnamed x7, local copies, waits for them, and re-layouts  4.95 us

profile of v2, /device:TPU:0, one launch (start us, length us, event | category | flops | bytes accessed | tf_op | source)
XLA Modules:
  0.0 74.0 jit_solution(4183141428367801630)
XLA Ops:
  0.6 41.6 %attention.1 = (bf16[32,2048]{1,0:T(8,128)(2,1)}, bf16[32,2048]{1,0:T(8,128)(2,1)}, bf16[32,512]{1,0:T(8,128)(2,1)}, bf16[32,64]{1,0:T(8,128)(2,1)}) custom-call(s32[32]{0:T(128)} %lens_ref.1, bf16[32,2048]{1,0:T(8,128)(2,1)} %hid_ref.1, bf16[2048]{0:T(1024)(128)(2,1)} %ga_ref.1, bf16[768]{0:T(1024)(128)(2,1)} %gq_ref.1, bf16[512]{0:T(512)(128)(2,1)} %gkv_ref.1, ...), custom_call_target="tpu_custom_call" | custom-call | tf_op jit(solution)/shard_map/attention/pallas_call | solution.py:195
  42.2 0.0 copy-start
  42.2 2.5 %copy-done = bf16[2048,1280]{1,0:T(8,128)(2,1)S(1)} copy-done((bf16[2048,1280]{1,0:T(8,128)(2,1)S(1)}, bf16[2048,1280]{1,0:T(8,128)(2,1)}, u32[]{:S(2)}) %copy-start) | copy-done | bytes 5242904
  44.7 0.0 copy-start.1
  44.7 0.9 %copy-done.1 = bf16[32,2048]{1,0:T(8,128)(2,1)S(1)} copy-done((bf16[32,2048]{1,0:T(8,128)(2,1)S(1)}, bf16[32,2048]{1,0:T(8,128)(2,1)}, u32[]{:S(2)}) %copy-start.1) | copy-done | bytes 131096
  45.6 0.0 copy-start.2
  45.6 0.9 %copy-done.2 = bf16[32,2048]{1,0:T(8,128)(2,1)S(1)} copy-done((bf16[32,2048]{1,0:T(8,128)(2,1)S(1)}, bf16[32,2048]{1,0:T(8,128)(2,1)}, u32[]{:S(2)}) %copy-start.2) | copy-done | bytes 131096
  46.5 26.8 %mlp_exchange.1 = bf16[32,2048]{1,0:T(8,128)(2,1)S(1)} custom-call(bf16[32,2048]{1,0:T(8,128)(2,1)S(1)} %copy-done.2, bf16[32,2048]{1,0:T(8,128)(2,1)S(1)} %copy-done.1, bf16[2048,1280]{1,0:T(8,128)(2,1)S(1)} %copy-done, bf16[2048,1280]{1,0:T(8,128)(2,1)} %wu_hbm.1, bf16[1280,2048]{1,0:T(8,128)(2,1)} %wd_hbm.1), custom_call_target="tpu_custom_call" | custom-call | tf_op jit(solution)/shard_map/mlp_exchange/pallas_call | solution.py:341
  73.4 0.7 copy.22
Async XLA Ops:
  42.2 2.5 %copy-start = (bf16[2048,1280]{1,0:T(8,128)(2,1)S(1)}, bf16[2048,1280]{1,0:T(8,128)(2,1)}, u32[]{:S(2)}) copy-start(bf16[2048,1280]{1,0:T(8,128)(2,1)} %wg_hbm.1) | copy-start | bytes 15728644
  44.7 0.9 %copy-start.1 = (bf16[32,2048]{1,0:T(8,128)(2,1)S(1)}, bf16[32,2048]{1,0:T(8,128)(2,1)}, u32[]{:S(2)}) copy-start(bf16[32,2048]{1,0:T(8,128)(2,1)} %get-tuple-element.8.h_ref) | copy-start | bytes 393220
  45.6 0.9 %copy-start.2 = (bf16[32,2048]{1,0:T(8,128)(2,1)S(1)}, bf16[32,2048]{1,0:T(8,128)(2,1)}, u32[]{:S(2)}) copy-start(bf16[32,2048]{1,0:T(8,128)(2,1)} %get-tuple-element.7.m_ref) | copy-start | bytes 393220

commit v3 on v2

--- a/solution.py
+++ b/solution.py
@@ -1,3 +1,5 @@
+import functools
+
 import jax
 import jax.numpy as jnp
 from jax import lax
@@ -10,12 +12,15 @@
 HEAD_PAD = 24
 RING = 12
 GROUP = 4
+WO_PARTS = 20
+WO_EARLY = 6
+WO_STEP = 2
 
 
 def attn_kernel(lens_ref, hid_ref, ga_ref, gq_ref, gkv_ref, gm_ref, lat_hbm, rope_hbm, wdq_hbm, wdkv_hbm, wqr_hbm, wuq_hbm, wuk_hbm, wuv_hbm, wo_hbm,
                 resid_ref, mlp_ref, newlat_ref, newrope_ref,
-                wdq, wdkv, wqr, wuq, wuk, wuv, wo, lat_buf, rope_buf, q_scr, qr_scr, o_scr, nl_scr, nr_scr, heads_scr,
-                w_sems, o_sems, lat_sems, rope_sems):
+                wdq, wdkv, wqr, wuq, wuk, wuv, wo, lat_buf, rope_buf, q_scr, qr_scr, o_scr, nl_scr, nr_scr, heads_scr, s_scr,
+                order, fill, w_sems, o_sems, lat_sems, rope_sems):
     rows = hid_ref.shape[0]
     kv_dim = lat_buf.shape[2]
     rope_dim = rope_buf.shape[1]
@@ -23,6 +28,7 @@
     nope_dim = wuk.shape[1]
     v_dim = wuv.shape[2]
     half = rope_dim // 2
+    groups = rows // GROUP
     f32, bf16 = jnp.float32, jnp.bfloat16
     nt = (((1,), (1,)), ((), ()))
 
@@ -30,21 +36,45 @@
     for copy in early:
         copy.start()
 
+    def bucket(row):
+        return (lens_ref[row] + 127) // 128
+
+    for k in range(9):
+        fill[k] = 0
+
+    def count(row, _):
+        k = bucket(row)
+        fill[k] = fill[k] + 1
+        return 0
+
+    lax.fori_loop(0, rows, count, 0)
+    running = jnp.int32(0)
+    for k in range(9):
+        size = fill[k]
+        fill[k] = running
+        running = running + size
+
+    def place(row, _):
+        k = bucket(row)
+        order[fill[k]] = row
+        fill[k] = fill[k] + 1
+        return 0
+
+    lax.fori_loop(0, rows, place, 0)
+
     def lat_copy(row, slot):
-        count = pl.multiple_of(((lens_ref[row] + 15) // 16) * 16, 16)
-        return pltpu.make_async_copy(lat_hbm.at[row, pl.ds(0, count)], lat_buf.at[slot, pl.ds(0, count)], lat_sems.at[slot])
+        count16 = pl.multiple_of(((lens_ref[row] + 15) // 16) * 16, 16)
+        return pltpu.make_async_copy(lat_hbm.at[row, pl.ds(0, count16)], lat_buf.at[slot, pl.ds(0, count16)], lat_sems.at[slot])
 
     def rope_copy(row, slot):
         return pltpu.make_async_copy(rope_hbm.at[row], rope_buf.at[slot], rope_sems.at[slot])
 
-    def start_row(row, slot):
+    def start_place(place_id, slot):
+        row = order[place_id]
         lat_copy(row, slot).start()
         rope_copy(row, slot).start()
 
-    def uv_copy(head):
-        return pltpu.make_async_copy(wuv_hbm.at[head], wuv.at[head], o_sems.at[0])
-
-    wo_rows = wo.shape[0] // rows
+    wo_rows = wo.shape[0] // WO_PARTS
 
     def wo_copy(part):
         span = pl.ds(pl.multiple_of(part * wo_rows, 32), wo_rows)
@@ -52,10 +82,14 @@
 
     def clear_and_start(slot, _):
         lat_buf[slot, pl.ds(256, cache_len - 256)] = jnp.zeros((cache_len - 256, kv_dim), bf16)
-        start_row(slot, slot)
+        start_place(slot, slot)
         return 0
 
     lax.fori_loop(0, RING, clear_and_start, 0)
+    uv_copy = pltpu.make_async_copy(wuv_hbm, wuv, o_sems.at[0])
+    uv_copy.start()
+    for part in range(WO_EARLY):
+        wo_copy(part).start()
 
     def norm(values, gain_ref):
         mean_sq = jnp.mean(values * values, axis=-1, keepdims=True)
@@ -83,29 +117,24 @@
     qr_scr[...] = jnp.zeros_like(qr_scr)
 
     early[0].wait()
-    q_in = norm(jnp.dot(normed, wdq[...], preferred_element_type=f32), gq_ref).astype(bf16)
+    q_raw = jnp.dot(normed, wdq[...], preferred_element_type=f32)
     early[1].wait()
     kv_raw = lax.dot_general(normed, wdkv[...], nt, preferred_element_type=f32)
+    q_in = norm(q_raw, gq_ref).astype(bf16)
+    early[2].wait()
+    rope_raw = lax.dot_general(q_in, wqr[...], nt, preferred_element_type=f32)
     new_lat = norm(kv_raw[:, :kv_dim], gkv_ref).astype(bf16)
     newlat_ref[...] = new_lat
     nl_scr[...] = new_lat.astype(f32)
     kv_rope = jnp.concatenate([kv_raw[:, kv_dim:], jnp.zeros((rows, 128 - rope_dim), f32)], axis=1)
     new_rope = rotate(kv_rope).astype(bf16)
     newrope_ref[...] = new_rope[:, :rope_dim]
-    low_lanes = lane < rope_dim
-    nr_scr[...] = jnp.where(low_lanes, new_rope.astype(f32), 0.0)
-
-    early[2].wait()
-    for pair in range(HEADS // 2):
-        raw = lax.dot_general(q_in, wqr[pl.ds(pair * 128, 128)], nt, preferred_element_type=f32)
-        turned = rotate(raw).astype(bf16).astype(f32)
-        qr_scr[pl.ds(2 * pair, rows, stride=HEAD_PAD), :] = turned
-        qr_scr[pl.ds(2 * pair + 1, rows, stride=HEAD_PAD), :] = pltpu.roll(turned, rope_dim, 1)
-
-    early[3].wait()
-    early[4].wait()
-    for quad in range(HEADS // 4):
-        q_nope = lax.dot_general(q_in, wuq[pl.ds(quad * 4 * nope_dim, 4 * nope_dim)], nt, preferred_element_type=f32)
+    nr_scr[...] = jnp.where(lane < rope_dim, new_rope.astype(f32), 0.0)
+
+    def nope_quad(quad):
+        return lax.dot_general(q_in, wuq[pl.ds(quad * 4 * nope_dim, 4 * nope_dim)], nt, preferred_element_type=f32)
+
+    def absorb_quad(quad, q_nope):
         for sub in range(4):
             head = quad * 4 + sub
             one = q_nope[:, sub * nope_dim:(sub + 1) * nope_dim].astype(bf16)
@@ -113,57 +142,115 @@
             for col in range(kv_dim // 128):
                 q_scr[col, pl.ds(head, rows, stride=HEAD_PAD), :] = q_abs[:, col * 128:(col + 1) * 128]
 
+    early[3].wait()
+    quads = HEADS // 4
+    ahead = nope_quad(0)
+    for pair in range(HEADS // 2):
+        turned = rotate(rope_raw[:, pair * 128:(pair + 1) * 128]).astype(bf16).astype(f32)
+        qr_scr[pl.ds(2 * pair, rows, stride=HEAD_PAD), :] = turned
+        qr_scr[pl.ds(2 * pair + 1, rows, stride=HEAD_PAD), :] = pltpu.roll(turned, rope_dim, 1)
+    for quad in range(quads):
+        now = ahead
+        if quad + 1 < quads:
+            ahead = nope_quad(quad + 1)
+        if quad == 0:
+            early[4].wait()
+        absorb_quad(quad, now)
+
     scale = (nope_dim + rope_dim) ** -0.5
-    key_pos = lax.broadcasted_iota(jnp.int32, (HEAD_PAD, cache_len), 1)
-
-    def attend(row, slot):
-        head_rows = pl.ds(pl.multiple_of(row * HEAD_PAD, 8), HEAD_PAD)
-        q_cols = [q_scr[col, head_rows, :] for col in range(kv_dim // 128)]
-        q_lat = jnp.concatenate(q_cols, axis=1)
-        q_rope = qr_scr[head_rows, :]
-        lat = lat_buf[slot]
-        own_lat = nl_scr[pl.ds(row, 1), :]
-        score = lax.dot_general(q_lat.astype(bf16), lat, nt, preferred_element_type=f32)
-        score = score + jnp.dot(q_rope[:, :rope_dim].astype(bf16), rope_buf[slot], preferred_element_type=f32)
+
+    def head_rows(row):
+        return pl.ds(pl.multiple_of(row * HEAD_PAD, 8), HEAD_PAD)
+
+    def query(row):
+        return jnp.concatenate([q_scr[col, head_rows(row), :] for col in range(kv_dim // 128)], axis=1)
+
+    def score_part(row, slot, span):
+        lat = lat_buf[slot, pl.ds(0, span)]
+        score = lax.dot_general(query(row).astype(bf16), lat, nt, preferred_element_type=f32)
+        q_rope = qr_scr[head_rows(row), :][:, :rope_dim].astype(bf16)
+        return score + jnp.dot(q_rope, rope_buf[slot, :, pl.ds(0, span)], preferred_element_type=f32)
+
+    def soft_part(row, score):
+        key_pos = lax.broadcasted_iota(jnp.int32, score.shape, 1)
         score = jnp.where(key_pos < lens_ref[row], score * scale, -jnp.inf)
-        own = jnp.sum(q_lat * own_lat, axis=-1, keepdims=True) + jnp.sum(q_rope * nr_scr[pl.ds(row, 1), :], axis=-1, keepdims=True)
+        q_rope = qr_scr[head_rows(row), :]
+        own = jnp.sum(query(row) * nl_scr[pl.ds(row, 1), :], axis=-1, keepdims=True) + jnp.sum(q_rope * nr_scr[pl.ds(row, 1), :], axis=-1, keepdims=True)
         own = own * scale
         top = jnp.maximum(jnp.max(score, axis=-1, keepdims=True), own)
         weight = jnp.exp(score - top)
         own_weight = jnp.exp(own - top)
         total = jnp.sum(weight, axis=-1, keepdims=True) + own_weight
-        prob = (weight / total).astype(bf16)
-        own_prob = (own_weight / total).astype(bf16).astype(f32)
-        mixed = jnp.dot(prob, lat, preferred_element_type=f32) + own_prob * own_lat
+        return (weight / total).astype(bf16), (own_weight / total).astype(bf16).astype(f32)
+
+    def mix_part(row, slot, prob, own_prob, span):
+        mixed = jnp.dot(prob, lat_buf[slot, pl.ds(0, span)], preferred_element_type=f32) + own_prob * nl_scr[pl.ds(row, 1), :]
         mixed = mixed.astype(bf16).astype(f32)
         for col in range(kv_dim // 128):
-            o_scr[col, head_rows, :] = mixed[:, col * 128:(col + 1) * 128]
+            o_scr[col, head_rows(row), :] = mixed[:, col * 128:(col + 1) * 128]
+
+    def members(group):
+        return [(order[group * GROUP + sub], lax.rem(group * GROUP, RING) + sub) for sub in range(GROUP)]
+
+    def wait_members(items):
+        for row, slot in items:
+            lat_copy(row, slot).wait()
+            rope_copy(row, slot).wait()
+
+    def group_blocks(group):
+        return (lens_ref[order[group * GROUP + GROUP - 1]] + 255) // 256
+
+    def by_span(blocks, run):
+        for size, test in ((2, blocks <= 2), (3, blocks == 3), (4, blocks == 4)):
+            pl.when(test)(functools.partial(run, size * cache_len // 4))
+
+    first = members(0)
+    wait_members(first)
+
+    def first_scores(span):
+        for sub, (row, slot) in enumerate(first):
+            s_scr[sub, :, pl.ds(0, span)] = score_part(row, slot, span)
+
+    by_span(group_blocks(0), first_scores)
 
     def group_step(group, _):
-        base = group * GROUP
-        for sub in range(GROUP):
-            part = base + sub
-            wo_copy(part).start()
-
-            @pl.when(part < HEADS)
-            def _():
-                uv_copy(part).start()
-        slots = [lax.rem(base, RING) + sub for sub in range(GROUP)]
-        for sub in range(GROUP):
-            lat_copy(base + sub, slots[sub]).wait()
-            rope_copy(base + sub, slots[sub]).wait()
-        for sub in range(GROUP):
-            attend(base + sub, slots[sub])
-
-        @pl.when(base + RING < rows)
-        def _():
+        now = members(group)
+        later = members(group + 1)
+        wait_members(later)
+
+        def run(span):
+            pending = None
             for sub in range(GROUP):
-                start_row(base + RING + sub, slots[sub])
+                fresh = score_part(*later[sub], span)
+                probs = soft_part(now[sub][0], s_scr[sub, :, pl.ds(0, span)])
+                s_scr[sub, :, pl.ds(0, span)] = fresh
+                if pending is not None:
+                    mix_part(*pending, span)
+                pending = (*now[sub], *probs)
+            mix_part(*pending, span)
+
+        by_span(group_blocks(group + 1), run)
+
+        @pl.when(group < groups - RING // GROUP)
+        def _():
+            for sub in range(GROUP):
+                start_place(group * GROUP + RING + sub, now[sub][1])
+
+        for extra in range(WO_STEP):
+            wo_copy(WO_EARLY + group * WO_STEP + extra).start()
         return 0
 
-    lax.fori_loop(0, rows // GROUP, group_step, 0)
-
-    pltpu.make_async_copy(wuv_hbm, wuv, o_sems.at[0]).wait()
+    lax.fori_loop(0, groups - 1, group_step, 0)
+    last = members(groups - 1)
+    pending = None
+    for sub in range(GROUP):
+        probs = soft_part(last[sub][0], s_scr[sub])
+        if pending is not None:
+            mix_part(*pending, cache_len)
+        pending = (*last[sub], *probs)
+    mix_part(*pending, cache_len)
+
+    uv_copy.wait()
     for head in range(HEADS):
         cols = [o_scr[col, pl.ds(head, rows, stride=HEAD_PAD), :] for col in range(kv_dim // 128)]
         mixed = jnp.concatenate(cols, axis=1).astype(bf16)
@@ -218,6 +305,9 @@
             pltpu.VMEM((rows, kv_dim), f32),
             pltpu.VMEM((rows, 128), f32),
             pltpu.VMEM((rows, heads * v_dim), bf16),
+            pltpu.VMEM((GROUP, HEAD_PAD, cache_len), f32),
+            pltpu.SMEM((rows,), jnp.int32),
+            pltpu.SMEM((9,), jnp.int32),
             dma((5,)), dma((2,)), dma((RING,)), dma((RING,)),
         ],
         compiler_params=pltpu.CompilerParams(vmem_limit_bytes=67043328),
@@ -355,7 +445,7 @@
             pltpu.VMEM((4, rows, width), jnp.bfloat16),
             dma((3,)), dma((4,)), dma((4,)), dma((4,)), dma((4,)), dma((4,)), dma((4,)), dma((4,)), dma((4,)),
         ],
-        compiler_params=pltpu.CompilerParams(collective_id=0, has_side_effects=True, vmem_limit_bytes=48 * 1024 * 1024),
+        compiler_params=pltpu.CompilerParams(collective_id=0, has_side_effects=True, vmem_limit_bytes=67043328),
         name="mlp_exchange",
     )(m, h, w_gate, w_up, w_down)
 

time: 74.2 us -> 61.1 us (0.82)
  Pallas kernels: 68.4 us -> 58.8 us
  local copies, waits for them, and re-layouts: 4.95 us -> 1.57 us
    pallas_call x1, Pallas kernels: 41.6 us -> 30.5 us  [attn_call(): pl.pallas_call(attn_kernel, out_shape=(jax.ShapeDtypeStruct((rows, width)...]
    unnamed x7 -> x1, local copies, waits for them, and re-layouts: 4.95 us -> 1.57 us
    pallas_call x1, Pallas kernels: 26.8 us -> 28.3 us  [mlp_call(): pl.pallas_call(mlp_kernel, out_shape=jax.ShapeDtypeStruct((rows, width),...]
where the time goes in v3:
time: 61.1 us; the launch traced here: 61 us
  Pallas kernels  58.8 us (96%)
  local copies, waits for them, and re-layouts  1.57 us (3%)
  between operations  0.65 us (1%)
    pallas_call x1, Pallas kernels, attn_call(): pl.pallas_call(attn_kernel, out_shape=(jax.ShapeDtypeStruct((rows, width)...  30.5 us
    pallas_call x1, Pallas kernels, mlp_call(): pl.pallas_call(mlp_kernel, out_shape=jax.ShapeDtypeStruct((rows, width),...  28.3 us
    unnamed x1, local copies, waits for them, and re-layouts  1.57 us

profile of v3, /device:TPU:0, one launch (start us, length us, event | category | flops | bytes accessed | tf_op | source)
XLA Modules:
  0.0 61.0 jit_solution(7371635278290346516)
XLA Ops:
  0.6 30.5 %attention.1 = (bf16[32,2048]{1,0:T(8,128)(2,1)}, bf16[32,2048]{1,0:T(8,128)(2,1)}, bf16[32,512]{1,0:T(8,128)(2,1)}, bf16[32,64]{1,0:T(8,128)(2,1)}) custom-call(s32[32]{0:T(128)} %lens_ref.1, bf16[32,2048]{1,0:T(8,128)(2,1)} %hid_ref.1, bf16[2048]{0:T(1024)(128)(2,1)} %ga_ref.1, bf16[768]{0:T(1024)(128)(2,1)} %gq_ref.1, bf16[512]{0:T(512)(128)(2,1)} %gkv_ref.1, ...), custom_call_target="tpu_custom_call" | custom-call | tf_op jit(solution)/shard_map/attention/pallas_call | solution.py:282
  31.1 28.3 %mlp_exchange.1 = bf16[32,2048]{1,0:T(8,128)(2,1)} custom-call(bf16[32,2048]{1,0:T(8,128)(2,1)} %get-tuple-element.7.m_ref, bf16[32,2048]{1,0:T(8,128)(2,1)} %get-tuple-element.8.h_ref, bf16[2048,1280]{1,0:T(8,128)(2,1)} %wg_hbm.1, bf16[2048,1280]{1,0:T(8,128)(2,1)} %wu_hbm.1, bf16[1280,2048]{1,0:T(8,128)(2,1)} %wd_hbm.1), custom_call_target="tpu_custom_call" | custom-call | tf_op jit(solution)/shard_map/mlp_exchange/pallas_call | solution.py:431
  59.4 1.6 %copy.22 = bf16[32,2048]{1,0:T(8,128)(2,1)} copy(bf16[32,2048]{1,0:T(8,128)(2,1)} %mlp_exchange.1) | data formatting | bytes 262144

commit v4 on v3

v4 whole, which is shorter than its diff:
```python
import functools

import jax
import jax.numpy as jnp
from jax import lax
from jax.experimental import pallas as pl
from jax.experimental.pallas import tpu as pltpu
from jax.sharding import PartitionSpec as P


HEADS = 20
HEAD_PAD = 24
RING = 16
GROUP = 4
WO_PARTS = 20
WO_STEP = 3


def attn_kernel(lens_ref, hid_ref, ga_ref, gq_ref, gkv_ref, lat_hbm, rope_hbm, wdq_hbm, wdkv_hbm, wqr_hbm, wuq_hbm, wuk_hbm, wuv_hbm, wo_hbm,
                newlat_ref, newrope_ref, o_scr, hid_out, wuv, wo,
                wdq, wdkv, wuk, lat_buf, rope_buf, q_scr, qr_scr, nl_scr, nr_scr, s_scr,
                order, fill, w_sems, o_sems, lat_sems, rope_sems):
    rows = hid_ref.shape[0]
    kv_dim = lat_buf.shape[2]
    rope_dim = rope_buf.shape[1]
    cache_len = lat_buf.shape[1]
    nope_dim = wuk.shape[1]
    q_dim = wdq.shape[1]
    half = rope_dim // 2
    groups = rows // GROUP
    f32, bf16 = jnp.float32, jnp.bfloat16
    nt = (((1,), (1,)), ((), ()))

    wuq = wo.at[pl.ds(0, HEADS * nope_dim), pl.ds(0, q_dim)]
    wqr = wo.at[pl.ds(0, HEADS * rope_dim), pl.ds(q_dim, q_dim)]
    early = [pltpu.make_async_copy(src, dst, w_sems.at[k]) for k, (src, dst) in enumerate(((wdq_hbm, wdq), (wdkv_hbm, wdkv), (wqr_hbm, wqr), (wuq_hbm, wuq), (wuk_hbm, wuk)))]
    for copy in early:
        copy.start()

    def bucket(row):
        return 8 - (lens_ref[row] + 127) // 128

    for k in range(9):
        fill[k] = 0

    def count(row, _):
        k = bucket(row)
        fill[k] = fill[k] + 1
        return 0

    lax.fori_loop(0, rows, count, 0)
    running = jnp.int32(0)
    for k in range(9):
        size = fill[k]
        fill[k] = running
        running = running + size

    def place(row, _):
        k = bucket(row)
        order[fill[k]] = row
        fill[k] = fill[k] + 1
        return 0

    lax.fori_loop(0, rows, place, 0)

    def lat_copy(row, slot):
        count16 = pl.multiple_of(((lens_ref[row] + 15) // 16) * 16, 16)
        return pltpu.make_async_copy(lat_hbm.at[row, pl.ds(0, count16)], lat_buf.at[slot, pl.ds(0, count16)], lat_sems.at[slot])

    def rope_copy(row, slot):
        return pltpu.make_async_copy(rope_hbm.at[row], rope_buf.at[slot], rope_sems.at[slot])

    def start_place(place_id, slot):
        row = order[place_id]
        lat_copy(row, slot).start()
        rope_copy(row, slot).start()

    wo_rows = wo.shape[0] // WO_PARTS

    def wo_copy(part):
        span = pl.ds(pl.multiple_of(part * wo_rows, 32), wo_rows)
        return pltpu.make_async_copy(wo_hbm.at[span], wo.at[span], o_sems.at[1])

    def clear_and_start(slot, _):
        lat_buf[slot, pl.ds(256, cache_len - 256)] = jnp.zeros((cache_len - 256, kv_dim), bf16)
        start_place(slot, slot)
        return 0

    lax.fori_loop(0, RING, clear_and_start, 0)
    uv_copy = pltpu.make_async_copy(wuv_hbm, wuv, o_sems.at[0])

    def norm(values, gain_ref):
        mean_sq = jnp.mean(values * values, axis=-1, keepdims=True)
        return values * lax.rsqrt(mean_sq + 1e-6) * gain_ref[...].astype(f32)

    row_id = lax.broadcasted_iota(jnp.int32, (rows, 128), 0)
    position = jnp.zeros((rows, 128), jnp.int32)
    for row in range(rows):
        position = jnp.where(row_id == row, lens_ref[row], position)
    lane = lax.broadcasted_iota(jnp.int32, (rows, 128), 1)
    freq_id = lane & (half - 1)
    inv_freq = jnp.exp(freq_id.astype(f32) * (-jnp.log(jnp.float32(10000.0)) / half))
    angle = position.astype(f32) * inv_freq
    first_half = (lane & half) == 0
    cos_part = jnp.cos(angle)
    sin_part = jnp.where(first_half, -jnp.sin(angle), jnp.sin(angle))

    def rotate(values):
        swapped = jnp.where(first_half, pltpu.roll(values, 128 - half, 1), pltpu.roll(values, half, 1))
        return values * cos_part + swapped * sin_part

    hid_out[...] = hid_ref[...]
    hidden = hid_ref[...].astype(f32)
    normed = norm(hidden, ga_ref).astype(bf16)
    q_scr[...] = jnp.zeros_like(q_scr)
    qr_scr[...] = jnp.zeros_like(qr_scr)

    early[0].wait()
    q_raw = jnp.dot(normed, wdq[...], preferred_element_type=f32)
    early[1].wait()
    kv_raw = lax.dot_general(normed, wdkv[...], nt, preferred_element_type=f32)
    q_in = norm(q_raw, gq_ref).astype(bf16)
    early[2].wait()
    rope_raw = lax.dot_general(q_in, wo[pl.ds(0, HEADS * rope_dim), pl.ds(q_dim, q_dim)], nt, preferred_element_type=f32)
    new_lat = norm(kv_raw[:, :kv_dim], gkv_ref).astype(bf16)
    newlat_ref[...] = new_lat
    nl_scr[...] = new_lat.astype(f32)
    kv_rope = jnp.concatenate([kv_raw[:, kv_dim:], jnp.zeros((rows, 128 - rope_dim), f32)], axis=1)
    new_rope = rotate(kv_rope).astype(bf16)
    newrope_ref[...] = new_rope[:, :rope_dim]
    nr_scr[...] = jnp.where(lane < rope_dim, new_rope.astype(f32), 0.0)

    def nope_quad(quad):
        return lax.dot_general(q_in, wo[pl.ds(quad * 4 * nope_dim, 4 * nope_dim), pl.ds(0, q_dim)], nt, preferred_element_type=f32)

    def absorb_quad(quad, q_nope):
        for sub in range(4):
            head = quad * 4 + sub
            one = q_nope[:, sub * nope_dim:(sub + 1) * nope_dim].astype(bf16)
            q_abs = jnp.dot(one, wuk[head], preferred_element_type=f32).astype(bf16).astype(f32)
            for col in range(kv_dim // 128):
                q_scr[col, pl.ds(head, rows, stride=HEAD_PAD), :] = q_abs[:, col * 128:(col + 1) * 128]

    early[3].wait()
    quads = HEADS // 4
    ahead = nope_quad(0)
    for pair in range(HEADS // 2):
        turned = rotate(rope_raw[:, pair * 128:(pair + 1) * 128]).astype(bf16).astype(f32)
        qr_scr[pl.ds(2 * pair, rows, stride=HEAD_PAD), :] = turned
        qr_scr[pl.ds(2 * pair + 1, rows, stride=HEAD_PAD), :] = pltpu.roll(turned, rope_dim, 1)
    for quad in range(quads):
        now = ahead
        if quad + 1 < quads:
            ahead = nope_quad(quad + 1)
        if quad == 0:
            early[4].wait()
        absorb_quad(quad, now)

    scale = (nope_dim + rope_dim) ** -0.5

    def head_rows(row):
        return pl.ds(pl.multiple_of(row * HEAD_PAD, 8), HEAD_PAD)

    def query(row):
        return jnp.concatenate([q_scr[col, head_rows(row), :] for col in range(kv_dim // 128)], axis=1)

    def score_part(row, slot, span):
        lat = lat_buf[slot, pl.ds(0, span)]
        score = lax.dot_general(query(row).astype(bf16), lat, nt, preferred_element_type=f32)
        q_rope = qr_scr[head_rows(row), :][:, :rope_dim].astype(bf16)
        return score + jnp.dot(q_rope, rope_buf[slot, :, pl.ds(0, span)], preferred_element_type=f32)

    def soft_part(row, score):
        key_pos = lax.broadcasted_iota(jnp.int32, score.shape, 1)
        score = jnp.where(key_pos < lens_ref[row], score * scale, -jnp.inf)
        q_rope = qr_scr[head_rows(row), :]
        own = jnp.sum(query(row) * nl_scr[pl.ds(row, 1), :], axis=-1, keepdims=True) + jnp.sum(q_rope * nr_scr[pl.ds(row, 1), :], axis=-1, keepdims=True)
        own = own * scale
        top = jnp.maximum(jnp.max(score, axis=-1, keepdims=True), own)
        weight = jnp.exp(score - top)
        own_weight = jnp.exp(own - top)
        total = jnp.sum(weight, axis=-1, keepdims=True) + own_weight
        return (weight / total).astype(bf16), (own_weight / total).astype(bf16).astype(f32)

    def mix_part(row, slot, prob, own_prob, span):
        mixed = jnp.dot(prob, lat_buf[slot, pl.ds(0, span)], preferred_element_type=f32) + own_prob * nl_scr[pl.ds(row, 1), :]
        mixed = mixed.astype(bf16).astype(f32)
        for col in range(kv_dim // 128):
            o_scr[col, head_rows(row), :] = mixed[:, col * 128:(col + 1) * 128]

    def members(group):
        return [(order[group * GROUP + sub], lax.rem(group * GROUP, RING) + sub) for sub in range(GROUP)]

    def wait_members(items):
        for row, slot in items:
            lat_copy(row, slot).wait()
            rope_copy(row, slot).wait()

    def group_blocks(group):
        return (lens_ref[order[group * GROUP]] + 255) // 256

    def by_span(blocks, run):
        for size, test in ((2, blocks <= 2), (3, blocks == 3), (4, blocks == 4)):
            pl.when(test)(functools.partial(run, size * cache_len // 4))

    first = members(0)
    wait_members(first)

    def first_scores(span):
        for sub, (row, slot) in enumerate(first):
            s_scr[sub, :, pl.ds(0, span)] = score_part(row, slot, span)

    by_span(group_blocks(0), first_scores)

    def group_step(group, _):
        now = members(group)
        later = members(group + 1)
        wait_members(later)

        def run(span):
            pending = None
            for sub in range(GROUP):
                fresh = score_part(*later[sub], span)
                probs = soft_part(now[sub][0], s_scr[sub, :, pl.ds(0, span)])
                s_scr[sub, :, pl.ds(0, span)] = fresh
                if pending is not None:
                    mix_part(*pending, span)
                pending = (*now[sub], *probs)
            mix_part(*pending, span)

        by_span(group_blocks(group), run)

        @pl.when(group < groups - RING // GROUP)
        def _():
            for sub in range(GROUP):
                start_place(group * GROUP + RING + sub, now[sub][1])

        @pl.when(group == 0)
        def _():
            uv_copy.start()

        for extra in range(WO_STEP):
            part = group * WO_STEP + extra
            pl.when(part < WO_PARTS)(lambda part=part: wo_copy(part).start())
        return 0

    lax.fori_loop(0, groups - 1, group_step, 0)
    last = members(groups - 1)

    def last_mix(span):
        pending = None
        for sub in range(GROUP):
            probs = soft_part(last[sub][0], s_scr[sub, :, pl.ds(0, span)])
            if pending is not None:
                mix_part(*pending, span)
            pending = (*last[sub], *probs)
        mix_part(*pending, span)

    by_span(group_blocks(groups - 1), last_mix)
    uv_copy.wait()
    pltpu.make_async_copy(wo_hbm, wo, o_sems.at[1]).wait()


def attn_call(hidden, cache_lat, cache_rope, seq_lens, gain_attn, w_dq, gain_q, w_uq, w_qr, w_dkv, gain_kv, w_uk, w_uv, w_o):
    rows, width = hidden.shape
    cache_len, kv_dim = cache_lat.shape[1:]
    rope_dim = cache_rope.shape[2]
    q_dim, heads, nope_dim = w_uq.shape
    bf16, f32 = jnp.bfloat16, jnp.float32
    vmem = pl.BlockSpec(memory_space=pltpu.VMEM)
    smem = pl.BlockSpec(memory_space=pltpu.SMEM)
    hbm = pl.BlockSpec(memory_space=pltpu.HBM)
    dma = pltpu.SemaphoreType.DMA
    rope_keys = jnp.swapaxes(cache_rope, 1, 2)
    dkv_t = w_dkv.T
    qr_t = jnp.transpose(w_qr, (1, 2, 0)).reshape(heads * rope_dim, q_dim)
    uq_t = jnp.transpose(w_uq, (1, 2, 0)).reshape(heads * nope_dim, q_dim)
    uk_t = jnp.transpose(w_uk, (1, 2, 0))
    uv_t = jnp.swapaxes(w_uv, 0, 1)
    handed = (
        pltpu.VMEM((kv_dim // 128, rows * HEAD_PAD, 128), f32),
        pltpu.VMEM(hidden.shape, bf16),
        pltpu.VMEM(uv_t.shape, bf16),
        pltpu.VMEM(w_o.shape, bf16),
    )
    return pl.pallas_call(
        attn_kernel,
        out_shape=(jax.ShapeDtypeStruct((rows, kv_dim), bf16), jax.ShapeDtypeStruct((rows, rope_dim), bf16)) + handed,
        in_specs=[smem, vmem, vmem, vmem, vmem] + [hbm] * 9,
        out_specs=(vmem,) * 6,
        scratch_shapes=[
            pltpu.VMEM(w_dq.shape, bf16),
            pltpu.VMEM(dkv_t.shape, bf16),
            pltpu.VMEM(uk_t.shape, bf16),
            pltpu.VMEM((RING, cache_len, kv_dim), bf16),
            pltpu.VMEM((RING, rope_dim, cache_len), bf16),
            pltpu.VMEM((kv_dim // 128, rows * HEAD_PAD, 128), f32),
            pltpu.VMEM((rows * HEAD_PAD, 128), f32),
            pltpu.VMEM((rows, kv_dim), f32),
            pltpu.VMEM((rows, 128), f32),
            pltpu.VMEM((GROUP, HEAD_PAD, cache_len), f32),
            pltpu.SMEM((rows,), jnp.int32),
            pltpu.SMEM((9,), jnp.int32),
            dma((5,)), dma((2,)), dma((RING,)), dma((RING,)),
        ],
        compiler_params=pltpu.CompilerParams(vmem_limit_bytes=33 * 1024 * 1024),
        name="attention",
    )(seq_lens, hidden, gain_attn, gain_q, gain_kv, cache_lat, rope_keys, w_dq, dkv_t, qr_t, uq_t, uk_t, uv_t, w_o)


MESH = pl.DeviceIdType.MESH
CHUNKS = 4


def mlp_kernel(o_ref, hid_ref, wuv, wo, gm_ref, wg_hbm, wu_hbm, wd_hbm, out_ref,
               wg, wu, wd, heads_scr, h_scr, gath, m_scr, keep, s1_send, s1_recv, s2_send, s2_recv,
               w_sems, near_send, near_recv, far_send, far_recv, fw_send, fw_recv, p1_send, p1_recv, p2_send, p2_recv):
    rows, width = hid_ref.shape
    part_width = width // CHUNKS
    heads, kv_dim, v_dim = wuv.shape
    f32, bf16 = jnp.float32, jnp.bfloat16
    me = lax.axis_index("g")
    core = lax.rem(me, 2)
    chip_x = lax.rem(me // 2, 2)
    chip_y = me // 4
    is_low = core == 0
    sibling = me + 1 - 2 * core
    mine = pl.ds(pl.multiple_of(core * rows, rows), rows)
    theirs = pl.ds(pl.multiple_of((1 - core) * rows, rows), rows)

    def peer(rel):
        return me + (rel % 2) * (2 - 4 * chip_x) + (rel // 2) * (4 - 8 * chip_y)

    def remote(src, dst, send, recv, target):
        return pltpu.make_async_remote_copy(src, dst, send, recv, device_id={"g": target}, device_id_type=MESH)

    def near_copy(rel, part):
        return remote(h_scr.at[part], gath.at[rel, part, mine], near_send.at[rel, part], near_recv.at[rel, part], peer(rel))

    def far_copy(rel):
        return remote(h_scr, gath.at[rel, :, mine], far_send.at[rel], far_recv.at[rel], sibling if rel == 0 else peer(rel))

    def sibling_rows_arrived():
        remote(h_scr, gath.at[0, :, theirs], far_send.at[0], far_recv.at[0], sibling).wait_recv()

    def forward_copy(rel):
        return remote(gath.at[rel, :, mine], gath.at[rel, :, mine], fw_send.at[rel], fw_recv.at[rel], sibling)

    def forward_arrived(rel):
        remote(gath.at[rel, :, theirs], gath.at[rel, :, theirs], fw_send.at[rel], fw_recv.at[rel], sibling).wait_recv()

    def pair_copy(rel):
        return remote(s1_send.at[rel], s1_recv.at[rel], p1_send.at[rel], p1_recv.at[rel], sibling)

    def chip_copy(rel):
        return remote(s2_send.at[rel], s2_recv.at[rel], p2_send.at[rel], p2_recv.at[rel], peer(rel))

    loads = [pltpu.make_async_copy(src, dst, w_sems.at[k]) for k, (src, dst) in enumerate(((wg_hbm, wg), (wu_hbm, wu), (wd_hbm, wd)))]
    for load in loads:
        load.start()
    barrier = pltpu.get_barrier_semaphore()
    for target in (sibling, peer(1), peer(2), peer(3)):
        pl.semaphore_signal(barrier, inc=1, device_id={"g": target}, device_id_type=MESH)

    for head in range(heads):
        cols = [o_ref[col, pl.ds(head, rows, stride=HEAD_PAD), :] for col in range(kv_dim // 128)]
        mixed = jnp.concatenate(cols, axis=1).astype(bf16)
        heads_scr[:, head * v_dim:(head + 1) * v_dim] = jnp.dot(mixed, wuv[head], preferred_element_type=f32).astype(bf16)

    def columns(part):
        return pl.ds(part * part_width, part_width)

    for part in range(CHUNKS):
        attn_out = jnp.dot(heads_scr[...], wo[:, columns(part)], preferred_element_type=f32)
        resid = (hid_ref[:, columns(part)].astype(f32) + attn_out).astype(bf16)
        h_scr[part] = resid
        gath[0, part, mine] = resid
        if part == 0:
            pl.semaphore_wait(barrier, 4)
        near_copy(1, part).start()
        near_copy(2, part).start()
    far_copy(3).start()
    far_copy(0).start()

    def normed_rows(rel, at):
        square = jnp.zeros((2 * rows, 1), f32)
        for part in range(CHUNKS):
            piece = gath[rel, part].astype(f32)
            square = square + jnp.sum(piece * piece, axis=-1, keepdims=True)
        factor = lax.rsqrt(square / width + 1e-6)
        for part in range(CHUNKS):
            piece = gath[rel, part].astype(f32) * factor * gm_ref[columns(part)].astype(f32)
            m_scr[pl.ds(at, 2 * rows), columns(part)] = piece.astype(bf16)

    def activation(count):
        block = m_scr[pl.ds(0, count)]
        gate = jnp.dot(block, wg[...], preferred_element_type=f32)
        up = jnp.dot(block, wu[...], preferred_element_type=f32)
        return (jax.nn.silu(gate) * up).astype(bf16)

    def contract(act, rels):
        part = jnp.dot(act, wd[...], preferred_element_type=f32)
        for index, rel in enumerate(rels):
            low = part[2 * index * rows:(2 * index + 1) * rows]
            high = part[(2 * index + 1) * rows:(2 * index + 2) * rows]
            s1_send[rel] = jnp.where(is_low, high, low)
            keep[rel] = jnp.where(is_low, low, high)
            pair_copy(rel).start()

    def send_sum(rel):
        pair_copy(rel).wait_recv()
        s2_send[rel] = (keep[rel] + s1_recv[rel]).astype(bf16)
        chip_copy(rel).start()

    sibling_rows_arrived()
    normed_rows(0, 0)
    loads[0].wait()
    loads[1].wait()
    act = activation(2 * rows)
    for rel in (1, 2):
        for part in range(CHUNKS):
            near_copy(rel, part).wait_recv()
        forward_copy(rel).start()
    loads[2].wait()
    contract(act, (0,))

    forward_arrived(1)
    normed_rows(1, 0)
    forward_arrived(2)
    normed_rows(2, 2 * rows)
    contract(activation(4 * rows), (1, 2))
    far_copy(3).wait_recv()
    forward_copy(3).start()
    send_sum(1)
    send_sum(2)

    forward_arrived(3)
    normed_rows(3, 0)
    contract(activation(2 * rows), (3,))
    pair_copy(0).wait_recv()
    send_sum(3)

    cols = [h_scr[part].astype(f32) for part in range(CHUNKS)]
    total = jnp.concatenate(cols, axis=1) + (keep[0] + s1_recv[0])
    for rel in (1, 2, 3):
        chip_copy(rel).wait_recv()
        total = total + s2_recv[rel].astype(f32)
    out_ref[...] = total.astype(bf16)
    for rel in (1, 2):
        for part in range(CHUNKS):
            near_copy(rel, part).wait_send()
    far_copy(3).wait_send()
    far_copy(0).wait_send()
    for rel in range(4):
        pair_copy(rel).wait_send()
    for rel in (1, 2, 3):
        forward_copy(rel).wait_send()
        chip_copy(rel).wait_send()


def mlp_call(o_lat, hidden, w_uv, w_o, gain_mlp, w_gate, w_up, w_down):
    rows, width = hidden.shape
    cols = w_gate.shape[1]
    bf16, f32 = jnp.bfloat16, jnp.float32
    vmem = pl.BlockSpec(memory_space=pltpu.VMEM)
    hbm = pl.BlockSpec(memory_space=pltpu.HBM)
    dma = pltpu.SemaphoreType.DMA
    part_width = width // CHUNKS
    held = [pltpu.with_memory_space_constraint(x, pltpu.VMEM) for x in (o_lat, hidden, w_uv, w_o)]
    streamed = [pltpu.with_memory_space_constraint(x, pltpu.HBM) for x in (w_gate, w_up, w_down)]
    return pl.pallas_call(
        mlp_kernel,
        out_shape=jax.ShapeDtypeStruct((rows, width), bf16),
        in_specs=[vmem, vmem, vmem, vmem, vmem, hbm, hbm, hbm],
        out_specs=vmem,
        scratch_shapes=[
            pltpu.VMEM((width, cols), bf16),
            pltpu.VMEM((width, cols), bf16),
            pltpu.VMEM((cols, width), bf16),
            pltpu.VMEM((rows, w_o.shape[0]), bf16),
            pltpu.VMEM((CHUNKS, rows, part_width), bf16),
            pltpu.VMEM((4, CHUNKS, 2 * rows, part_width), bf16),
            pltpu.VMEM((4 * rows, width), bf16),
            pltpu.VMEM((4, rows, width), f32),
            pltpu.VMEM((4, rows, width), f32),
            pltpu.VMEM((4, rows, width), f32),
            pltpu.VMEM((4, rows, width), bf16),
            pltpu.VMEM((4, rows, width), bf16),
            dma((3,)), dma((4, CHUNKS)), dma((4, CHUNKS)), dma((4,)), dma((4,)), dma((4,)), dma((4,)), dma((4,)), dma((4,)), dma((4,)), dma((4,)),
        ],
        compiler_params=pltpu.CompilerParams(collective_id=0, has_side_effects=True, vmem_limit_bytes=33 * 1024 * 1024),
        name="mlp_exchange",
    )(*held, gain_mlp, *streamed)


def solution(mesh):
    row_spec = P(("rep", "g"))
    full_spec = P()
    in_specs = (row_spec, row_spec, row_spec, row_spec, full_spec, full_spec, full_spec, full_spec, full_spec, full_spec, full_spec, full_spec, full_spec, full_spec, full_spec, P(None, "g"), P(None, "g"), P("g", None))

    def local_step(hidden, cache_lat, cache_rope, seq_lens, gain_attn, w_dq, gain_q, w_uq, w_qr, w_dkv, gain_kv, w_uk, w_uv, w_o, gain_mlp, w_gate, w_up, w_down):
        new_lat, new_rope, o_lat, hid_rows, uv_held, wo_held = attn_call(hidden, cache_lat, cache_rope, seq_lens, gain_attn, w_dq, gain_q, w_uq, w_qr, w_dkv, gain_kv, w_uk, w_uv, w_o)
        out_hidden = mlp_call(o_lat, hid_rows, uv_held, wo_held, gain_mlp, w_gate, w_up, w_down)
        return out_hidden, new_lat, new_rope

    return jax.shard_map(local_step, mesh=mesh, in_specs=in_specs, out_specs=(row_spec, row_spec, row_spec), check_vma=False)
```

time: 61.1 us -> 57.3 us (0.938); the launches traced: 61 us -> 57.8 us
  Pallas kernels: 58.8 us -> 55.6 us
    pallas_call x1, Pallas kernels: 30.5 us -> 25.5 us  [attn_call(): pl.pallas_call(attn_kernel, out_shape=(jax.ShapeDtypeStruct((rows, kv_dim...]
    pallas_call x1, Pallas kernels: 28.3 us -> 30.1 us  [mlp_call(): pl.pallas_call(mlp_kernel, out_shape=jax.ShapeDtypeStruct((rows, width),...]
where the time goes in v4:
time: 57.3 us; the launch traced here: 57.8 us
  Pallas kernels  55.6 us (97%)
  local copies, waits for them, and re-layouts  1.57 us (3%)
  between operations  0.65 us (1%)
    pallas_call x1, Pallas kernels, mlp_call(): pl.pallas_call(mlp_kernel, out_shape=jax.ShapeDtypeStruct((rows, width),...  30.1 us
    pallas_call x1, Pallas kernels, attn_call(): pl.pallas_call(attn_kernel, out_shape=(jax.ShapeDtypeStruct((rows, kv_dim...  25.5 us
    unnamed x1, local copies, waits for them, and re-layouts  1.57 us

profile of v4, /device:TPU:0, one launch (start us, length us, event | category | flops | bytes accessed | tf_op | source)
XLA Modules:
  0.0 57.8 jit_solution(6531320640658565950)
XLA Ops:
  0.6 25.5 %attention.1 = (bf16[32,512]{1,0:T(8,128)(2,1)}, bf16[32,64]{1,0:T(8,128)(2,1)}, f32[4,768,128]{2,1,0:T(8,128)S(1)}, bf16[32,2048]{1,0:T(8,128)(2,1)S(1)}, bf16[...) custom-call(s32[32]{0:T(128)} %lens_ref.1, bf16[32,2048]{1,0:T(8,128)(2,1)} %hid_ref.1, ...), custom_call_target="tpu_custom_call" | custom-call | tf_op jit(solution)/shard_map/attention/pallas_call | solution.py:286
  26.2 30.1 %mlp_exchange.1 = bf16[32,2048]{1,0:T(8,128)(2,1)} custom-call(f32[4,768,128]{2,1,0:T(8,128)S(1)} %get-tuple-element.9.o_ref, bf16[32,2048]{1,0:T(8,128)(2,1)S(1)} %get-tuple-element.10.hid_ref, bf16[20,512,256]{2,1,0:T(8,128)(2,1)S(1)} %get-tuple-element.11.wuv, bf16[5120,2048]{1,0:T(8,128)(2,1)S(1)} %get-tuple-element.12.wo, bf16[2048]{0:T(1024)(128)(2,1)} %gm_ref.1, ...), custom_call_target="tpu_custom_call" | custom-call | tf_op jit(solution)/shard_map/mlp_exchange/pallas_call | solution.py:471
  56.3 1.6 %copy.22 = bf16[32,2048]{1,0:T(8,128)(2,1)} copy(bf16[32,2048]{1,0:T(8,128)(2,1)} %mlp_exchange.1) | data formatting | bytes 262144

commit v5 on v4

--- a/solution.py
+++ b/solution.py
@@ -16,10 +16,10 @@
 WO_STEP = 3
 
 
-def attn_kernel(lens_ref, hid_ref, ga_ref, gq_ref, gkv_ref, lat_hbm, rope_hbm, wdq_hbm, wdkv_hbm, wqr_hbm, wuq_hbm, wuk_hbm, wuv_hbm, wo_hbm,
-                newlat_ref, newrope_ref, o_scr, hid_out, wuv, wo,
+def attn_kernel(lens_hbm, hid_hbm, ga_hbm, gq_hbm, gkv_hbm, lat_hbm, rope_hbm, wdq_hbm, wdkv_hbm, wqr_hbm, wuq_hbm, wuk_hbm, wuv_hbm, wo_hbm,
+                newlat_hbm, newrope_hbm, o_scr, hid_ref, wuv, wo,
                 wdq, wdkv, wuk, lat_buf, rope_buf, q_scr, qr_scr, nl_scr, nr_scr, s_scr,
-                order, fill, w_sems, o_sems, lat_sems, rope_sems):
+                ga_ref, gq_ref, gkv_ref, newlat_ref, newrope_ref, lens_ref, order, fill, w_sems, o_sems, in_sems, new_sems, lat_sems, rope_sems):
     rows = hid_ref.shape[0]
     kv_dim = lat_buf.shape[2]
     rope_dim = rope_buf.shape[1]
@@ -34,11 +34,13 @@
     wuq = wo.at[pl.ds(0, HEADS * nope_dim), pl.ds(0, q_dim)]
     wqr = wo.at[pl.ds(0, HEADS * rope_dim), pl.ds(q_dim, q_dim)]
     early = [pltpu.make_async_copy(src, dst, w_sems.at[k]) for k, (src, dst) in enumerate(((wdq_hbm, wdq), (wdkv_hbm, wdkv), (wqr_hbm, wqr), (wuq_hbm, wuq), (wuk_hbm, wuk)))]
-    for copy in early:
+    small = [pltpu.make_async_copy(src, dst, in_sems.at[k]) for k, (src, dst) in enumerate(((lens_hbm, lens_ref), (hid_hbm, hid_ref), (ga_hbm, ga_ref), (gq_hbm, gq_ref), (gkv_hbm, gkv_ref)))]
+    for copy in small + early:
         copy.start()
+    small[0].wait()
 
     def bucket(row):
-        return 8 - (lens_ref[row] + 127) // 128
+        return 8 - ((lens_ref[row] + 127) >> 7)
 
     for k in range(9):
         fill[k] = 0
@@ -63,17 +65,19 @@
 
     lax.fori_loop(0, rows, place, 0)
 
-    def lat_copy(row, slot):
-        count16 = pl.multiple_of(((lens_ref[row] + 15) // 16) * 16, 16)
-        return pltpu.make_async_copy(lat_hbm.at[row, pl.ds(0, count16)], lat_buf.at[slot, pl.ds(0, count16)], lat_sems.at[slot])
+    def lat_copy(place_id, slot):
+        row = order[place_id]
+        span = jnp.maximum((lens_ref[order[(place_id // GROUP) * GROUP]] + 255) >> 8, 2) << 8
+        count = jnp.where(place_id < RING, span, ((lens_ref[row] + 15) >> 4) << 4)
+        count = pl.multiple_of(count, 16)
+        return pltpu.make_async_copy(lat_hbm.at[row, pl.ds(0, count)], lat_buf.at[slot, pl.ds(0, count)], lat_sems.at[slot])
 
     def rope_copy(row, slot):
         return pltpu.make_async_copy(rope_hbm.at[row], rope_buf.at[slot], rope_sems.at[slot])
 
     def start_place(place_id, slot):
-        row = order[place_id]
-        lat_copy(row, slot).start()
-        rope_copy(row, slot).start()
+        lat_copy(place_id, slot).start()
+        rope_copy(order[place_id], slot).start()
 
     wo_rows = wo.shape[0] // WO_PARTS
 
@@ -81,12 +85,11 @@
         span = pl.ds(pl.multiple_of(part * wo_rows, 32), wo_rows)
         return pltpu.make_async_copy(wo_hbm.at[span], wo.at[span], o_sems.at[1])
 
-    def clear_and_start(slot, _):
-        lat_buf[slot, pl.ds(256, cache_len - 256)] = jnp.zeros((cache_len - 256, kv_dim), bf16)
+    def fill_ring(slot, _):
         start_place(slot, slot)
         return 0
 
-    lax.fori_loop(0, RING, clear_and_start, 0)
+    lax.fori_loop(0, RING, fill_ring, 0)
     uv_copy = pltpu.make_async_copy(wuv_hbm, wuv, o_sems.at[0])
 
     def norm(values, gain_ref):
@@ -109,12 +112,15 @@
         swapped = jnp.where(first_half, pltpu.roll(values, 128 - half, 1), pltpu.roll(values, half, 1))
         return values * cos_part + swapped * sin_part
 
-    hid_out[...] = hid_ref[...]
+    small[1].wait()
+    small[2].wait()
     hidden = hid_ref[...].astype(f32)
     normed = norm(hidden, ga_ref).astype(bf16)
     q_scr[...] = jnp.zeros_like(q_scr)
     qr_scr[...] = jnp.zeros_like(qr_scr)
 
+    small[3].wait()
+    small[4].wait()
     early[0].wait()
     q_raw = jnp.dot(normed, wdq[...], preferred_element_type=f32)
     early[1].wait()
@@ -128,6 +134,7 @@
     kv_rope = jnp.concatenate([kv_raw[:, kv_dim:], jnp.zeros((rows, 128 - rope_dim), f32)], axis=1)
     new_rope = rotate(kv_rope).astype(bf16)
     newrope_ref[...] = new_rope[:, :rope_dim]
+    outgoing = [pltpu.make_async_copy(newlat_ref, newlat_hbm, new_sems.at[0]), pltpu.make_async_copy(newrope_ref, newrope_hbm, new_sems.at[1])]
     nr_scr[...] = jnp.where(lane < rope_dim, new_rope.astype(f32), 0.0)
 
     def nope_quad(quad):
@@ -156,6 +163,8 @@
             early[4].wait()
         absorb_quad(quad, now)
 
+    for copy in outgoing:
+        copy.start()
     scale = (nope_dim + rope_dim) ** -0.5
 
     def head_rows(row):
@@ -191,20 +200,20 @@
     def members(group):
         return [(order[group * GROUP + sub], lax.rem(group * GROUP, RING) + sub) for sub in range(GROUP)]
 
-    def wait_members(items):
-        for row, slot in items:
-            lat_copy(row, slot).wait()
+    def wait_members(group):
+        for sub, (row, slot) in enumerate(members(group)):
+            lat_copy(group * GROUP + sub, slot).wait()
             rope_copy(row, slot).wait()
 
     def group_blocks(group):
-        return (lens_ref[order[group * GROUP]] + 255) // 256
+        return (lens_ref[order[group * GROUP]] + 255) >> 8
 
     def by_span(blocks, run):
         for size, test in ((2, blocks <= 2), (3, blocks == 3), (4, blocks == 4)):
             pl.when(test)(functools.partial(run, size * cache_len // 4))
 
     first = members(0)
-    wait_members(first)
+    wait_members(0)
 
     def first_scores(span):
         for sub, (row, slot) in enumerate(first):
@@ -215,7 +224,7 @@
     def group_step(group, _):
         now = members(group)
         later = members(group + 1)
-        wait_members(later)
+        wait_members(group + 1)
 
         def run(span):
             pending = None
@@ -259,6 +268,8 @@
     by_span(group_blocks(groups - 1), last_mix)
     uv_copy.wait()
     pltpu.make_async_copy(wo_hbm, wo, o_sems.at[1]).wait()
+    for copy in outgoing:
+        copy.wait()
 
 
 def attn_call(hidden, cache_lat, cache_rope, seq_lens, gain_attn, w_dq, gain_q, w_uq, w_qr, w_dkv, gain_kv, w_uk, w_uv, w_o):
@@ -268,7 +279,6 @@
     q_dim, heads, nope_dim = w_uq.shape
     bf16, f32 = jnp.bfloat16, jnp.float32
     vmem = pl.BlockSpec(memory_space=pltpu.VMEM)
-    smem = pl.BlockSpec(memory_space=pltpu.SMEM)
     hbm = pl.BlockSpec(memory_space=pltpu.HBM)
     dma = pltpu.SemaphoreType.DMA
     rope_keys = jnp.swapaxes(cache_rope, 1, 2)
@@ -286,8 +296,8 @@
     return pl.pallas_call(
         attn_kernel,
         out_shape=(jax.ShapeDtypeStruct((rows, kv_dim), bf16), jax.ShapeDtypeStruct((rows, rope_dim), bf16)) + handed,
-        in_specs=[smem, vmem, vmem, vmem, vmem] + [hbm] * 9,
-        out_specs=(vmem,) * 6,
+        in_specs=[hbm] * 14,
+        out_specs=(hbm, hbm, vmem, vmem, vmem, vmem),
         scratch_shapes=[
             pltpu.VMEM(w_dq.shape, bf16),
             pltpu.VMEM(dkv_t.shape, bf16),
@@ -299,9 +309,15 @@
             pltpu.VMEM((rows, kv_dim), f32),
             pltpu.VMEM((rows, 128), f32),
             pltpu.VMEM((GROUP, HEAD_PAD, cache_len), f32),
+            pltpu.VMEM(gain_attn.shape, bf16),
+            pltpu.VMEM(gain_q.shape, bf16),
+            pltpu.VMEM(gain_kv.shape, bf16),
+            pltpu.VMEM((rows, kv_dim), bf16),
+            pltpu.VMEM((rows, rope_dim), bf16),
+            pltpu.SMEM((rows,), jnp.int32),
             pltpu.SMEM((rows,), jnp.int32),
             pltpu.SMEM((9,), jnp.int32),
-            dma((5,)), dma((2,)), dma((RING,)), dma((RING,)),
+            dma((5,)), dma((2,)), dma((5,)), dma((2,)), dma((RING,)), dma((RING,)),
         ],
         compiler_params=pltpu.CompilerParams(vmem_limit_bytes=33 * 1024 * 1024),
         name="attention",
@@ -312,8 +328,8 @@
 CHUNKS = 4
 
 
-def mlp_kernel(o_ref, hid_ref, wuv, wo, gm_ref, wg_hbm, wu_hbm, wd_hbm, out_ref,
-               wg, wu, wd, heads_scr, h_scr, gath, m_scr, keep, s1_send, s1_recv, s2_send, s2_recv,
+def mlp_kernel(o_ref, hid_ref, wuv, wo, gm_hbm, wg_hbm, wu_hbm, wd_hbm, out_ref,
+               gm_ref, wg, wu, wd, heads_scr, h_scr, gath, m_scr, keep, s1_send, s1_recv, s2_send, s2_recv,
                w_sems, near_send, near_recv, far_send, far_recv, fw_send, fw_recv, p1_send, p1_recv, p2_send, p2_recv):
     rows, width = hid_ref.shape
     part_width = width // CHUNKS
@@ -355,7 +371,7 @@
     def chip_copy(rel):
         return remote(s2_send.at[rel], s2_recv.at[rel], p2_send.at[rel], p2_recv.at[rel], peer(rel))
 
-    loads = [pltpu.make_async_copy(src, dst, w_sems.at[k]) for k, (src, dst) in enumerate(((wg_hbm, wg), (wu_hbm, wu), (wd_hbm, wd)))]
+    loads = [pltpu.make_async_copy(src, dst, w_sems.at[k]) for k, (src, dst) in enumerate(((wg_hbm, wg), (wu_hbm, wu), (wd_hbm, wd), (gm_hbm, gm_ref)))]
     for load in loads:
         load.start()
     barrier = pltpu.get_barrier_semaphore()
@@ -412,18 +428,12 @@
         s2_send[rel] = (keep[rel] + s1_recv[rel]).astype(bf16)
         chip_copy(rel).start()
 
-    sibling_rows_arrived()
-    normed_rows(0, 0)
-    loads[0].wait()
-    loads[1].wait()
-    act = activation(2 * rows)
     for rel in (1, 2):
         for part in range(CHUNKS):
             near_copy(rel, part).wait_recv()
         forward_copy(rel).start()
-    loads[2].wait()
-    contract(act, (0,))
-
+    for load in loads:
+        load.wait()
     forward_arrived(1)
     normed_rows(1, 0)
     forward_arrived(2)
@@ -431,14 +441,16 @@
     contract(activation(4 * rows), (1, 2))
     far_copy(3).wait_recv()
     forward_copy(3).start()
+    sibling_rows_arrived()
+    normed_rows(0, 2 * rows)
     send_sum(1)
     send_sum(2)
 
     forward_arrived(3)
     normed_rows(3, 0)
-    contract(activation(2 * rows), (3,))
+    contract(activation(4 * rows), (3, 0))
+    send_sum(3)
     pair_copy(0).wait_recv()
-    send_sum(3)
 
     cols = [h_scr[part].astype(f32) for part in range(CHUNKS)]
     total = jnp.concatenate(cols, axis=1) + (keep[0] + s1_recv[0])
@@ -470,10 +482,11 @@
     streamed = [pltpu.with_memory_space_constraint(x, pltpu.HBM) for x in (w_gate, w_up, w_down)]
     return pl.pallas_call(
         mlp_kernel,
-        out_shape=jax.ShapeDtypeStruct((rows, width), bf16),
-        in_specs=[vmem, vmem, vmem, vmem, vmem, hbm, hbm, hbm],
+        out_shape=pltpu.VMEM((rows, width), bf16),
+        in_specs=[vmem, vmem, vmem, vmem, hbm, hbm, hbm, hbm],
         out_specs=vmem,
         scratch_shapes=[
+            pltpu.VMEM(gain_mlp.shape, bf16),
             pltpu.VMEM((width, cols), bf16),
             pltpu.VMEM((width, cols), bf16),
             pltpu.VMEM((cols, width), bf16),
@@ -486,7 +499,7 @@
             pltpu.VMEM((4, rows, width), f32),
             pltpu.VMEM((4, rows, width), bf16),
             pltpu.VMEM((4, rows, width), bf16),
-            dma((3,)), dma((4, CHUNKS)), dma((4, CHUNKS)), dma((4,)), dma((4,)), dma((4,)), dma((4,)), dma((4,)), dma((4,)), dma((4,)), dma((4,)),
+            dma((4,)), dma((4, CHUNKS)), dma((4, CHUNKS)), dma((4,)), dma((4,)), dma((4,)), dma((4,)), dma((4,)), dma((4,)), dma((4,)), dma((4,)),
         ],
         compiler_params=pltpu.CompilerParams(collective_id=0, has_side_effects=True, vmem_limit_bytes=33 * 1024 * 1024),
         name="mlp_exchange",

time: 57.3 us -> 53.4 us (0.932)
  the two profiles are of different devices: /device:TPU:0 before, /device:TPU:5 now
where the time goes in v5:
time: 53.4 us; the launch traced here: 52.6 us
  Pallas kernels  51.3 us (96%)
  local copies, waits for them, and re-layouts  0.66 us (1%)
  between operations  0.65 us (1%)
    pallas_call x1, Pallas kernels, attn_call(): pl.pallas_call(attn_kernel, out_shape=(jax.ShapeDtypeStruct((rows, kv_dim...  26 us
    pallas_call x1, Pallas kernels, mlp_call(): pl.pallas_call(mlp_kernel, out_shape=pltpu.VMEM((rows, width), bf16), in_...  25.3 us

profile of v5, /device:TPU:5, one launch (start us, length us, event | category | flops | bytes accessed | tf_op | source)
XLA Modules:
  0.0 52.6 jit_solution(6180170438360612750)
XLA Ops:
  0.6 26.0 %attention.1 = (bf16[32,512]{1,0:T(8,128)(2,1)}, bf16[32,64]{1,0:T(8,128)(2,1)}, f32[4,768,128]{2,1,0:T(8,128)S(1)}, bf16[32,2048]{1,0:T(8,128)(2,1)S(1)}, bf16[...) custom-call(s32[32]{0:T(128)} %lens_hbm.1, bf16[32,2048]{1,0:T(8,128)(2,1)} %hid_hbm.1, ...), custom_call_target="tpu_custom_call" | custom-call | tf_op jit(solution)/shard_map/attention/pallas_call | solution.py:296
  26.6 25.3 %mlp_exchange.1 = bf16[32,2048]{1,0:T(8,128)(2,1)S(1)} custom-call(f32[4,768,128]{2,1,0:T(8,128)S(1)} %get-tuple-element.9.o_ref, bf16[32,2048]{1,0:T(8,128)(2,1)S(1)} %get-tuple-element.10.hid_ref, bf16[20,512,256]{2,1,0:T(8,128)(2,1)S(1)} %get-tuple-element.11.wuv, bf16[5120,2048]{1,0:T(8,128)(2,1)S(1)} %get-tuple-element.12.wo, bf16[2048]{0:T(1024)(128)(2,1)} %gm_hbm.1, ...), custom_call_target="tpu_custom_call" | custom-call | tf_op jit(solution)/shard_map/mlp_exchange/pallas_call | solution.py:483
  52.0 0.7 %copy.22 = bf16[32,2048]{1,0:T(8,128)(2,1)} copy(bf16[32,2048]{1,0:T(8,128)(2,1)S(1)} %mlp_exchange.1) | data formatting | bytes 262144

commit v6 on v5

--- a/solution.py
+++ b/solution.py
@@ -10,9 +10,10 @@
 
 HEADS = 20
 HEAD_PAD = 24
-RING = 16
+RING = 24
 GROUP = 4
-WO_PARTS = 20
+VMEM_LIMIT = 43 * 1024 * 1024
+WO_PARTS = 16
 WO_STEP = 3
 
 
@@ -32,7 +33,7 @@
     nt = (((1,), (1,)), ((), ()))
 
     wuq = wo.at[pl.ds(0, HEADS * nope_dim), pl.ds(0, q_dim)]
-    wqr = wo.at[pl.ds(0, HEADS * rope_dim), pl.ds(q_dim, q_dim)]
+    wqr = wo.at[pl.ds(HEADS * nope_dim, HEADS * rope_dim), pl.ds(0, q_dim)]
     early = [pltpu.make_async_copy(src, dst, w_sems.at[k]) for k, (src, dst) in enumerate(((wdq_hbm, wdq), (wdkv_hbm, wdkv), (wqr_hbm, wqr), (wuq_hbm, wuq), (wuk_hbm, wuk)))]
     small = [pltpu.make_async_copy(src, dst, in_sems.at[k]) for k, (src, dst) in enumerate(((lens_hbm, lens_ref), (hid_hbm, hid_ref), (ga_hbm, ga_ref), (gq_hbm, gq_ref), (gkv_hbm, gkv_ref)))]
     for copy in small + early:
@@ -83,7 +84,7 @@
 
     def wo_copy(part):
         span = pl.ds(pl.multiple_of(part * wo_rows, 32), wo_rows)
-        return pltpu.make_async_copy(wo_hbm.at[span], wo.at[span], o_sems.at[1])
+        return pltpu.make_async_copy(wo_hbm.at[span, pl.ds(0, wo.shape[1])], wo.at[span], o_sems.at[1])
 
     def fill_ring(slot, _):
         start_place(slot, slot)
@@ -127,7 +128,7 @@
     kv_raw = lax.dot_general(normed, wdkv[...], nt, preferred_element_type=f32)
     q_in = norm(q_raw, gq_ref).astype(bf16)
     early[2].wait()
-    rope_raw = lax.dot_general(q_in, wo[pl.ds(0, HEADS * rope_dim), pl.ds(q_dim, q_dim)], nt, preferred_element_type=f32)
+    rope_raw = lax.dot_general(q_in, wo[pl.ds(HEADS * nope_dim, HEADS * rope_dim), pl.ds(0, q_dim)], nt, preferred_element_type=f32)
     new_lat = norm(kv_raw[:, :kv_dim], gkv_ref).astype(bf16)
     newlat_ref[...] = new_lat
     nl_scr[...] = new_lat.astype(f32)
@@ -267,7 +268,7 @@
 
     by_span(group_blocks(groups - 1), last_mix)
     uv_copy.wait()
-    pltpu.make_async_copy(wo_hbm, wo, o_sems.at[1]).wait()
+    pltpu.make_async_copy(wo_hbm.at[:, pl.ds(0, wo.shape[1])], wo, o_sems.at[1]).wait()
     for copy in outgoing:
         copy.wait()
 
@@ -291,7 +292,7 @@
         pltpu.VMEM((kv_dim // 128, rows * HEAD_PAD, 128), f32),
         pltpu.VMEM(hidden.shape, bf16),
         pltpu.VMEM(uv_t.shape, bf16),
-        pltpu.VMEM(w_o.shape, bf16),
+        pltpu.VMEM((w_o.shape[0], width // 2), bf16),
     )
     return pl.pallas_call(
         attn_kernel,
@@ -319,7 +320,7 @@
             pltpu.SMEM((9,), jnp.int32),
             dma((5,)), dma((2,)), dma((5,)), dma((2,)), dma((RING,)), dma((RING,)),
         ],
-        compiler_params=pltpu.CompilerParams(vmem_limit_bytes=33 * 1024 * 1024),
+        compiler_params=pltpu.CompilerParams(vmem_limit_bytes=VMEM_LIMIT),
         name="attention",
     )(seq_lens, hidden, gain_attn, gain_q, gain_kv, cache_lat, rope_keys, w_dq, dkv_t, qr_t, uq_t, uk_t, uv_t, w_o)
 
@@ -328,9 +329,9 @@
 CHUNKS = 4
 
 
-def mlp_kernel(o_ref, hid_ref, wuv, wo, gm_hbm, wg_hbm, wu_hbm, wd_hbm, out_ref,
-               gm_ref, wg, wu, wd, heads_scr, h_scr, gath, m_scr, keep, s1_send, s1_recv, s2_send, s2_recv,
-               w_sems, near_send, near_recv, far_send, far_recv, fw_send, fw_recv, p1_send, p1_recv, p2_send, p2_recv):
+def mlp_kernel(o_ref, hid_ref, wuv, wo_low, gm_hbm, wo_hbm, wg_hbm, wu_hbm, wd_hbm, out_ref,
+               gm_ref, wo_high, wg, wu, wd, heads_scr, h_scr, gath, m_scr, keep, s1_send, s1_recv, s2_send, s2_recv,
+               w_sems, wo_sems, near_send, near_recv, far_send, far_recv, fw_send, fw_recv, p1_send, p1_recv, p2_send, p2_recv):
     rows, width = hid_ref.shape
     part_width = width // CHUNKS
     heads, kv_dim, v_dim = wuv.shape
@@ -354,7 +355,7 @@
         return remote(h_scr.at[part], gath.at[rel, part, mine], near_send.at[rel, part], near_recv.at[rel, part], peer(rel))
 
     def far_copy(rel):
-        return remote(h_scr, gath.at[rel, :, mine], far_send.at[rel], far_recv.at[rel], sibling if rel == 0 else peer(rel))
+        return remote(h_scr, gath.at[rel, :, mine], far_send.at[rel], far_recv.at[rel], sibling)
 
     def sibling_rows_arrived():
         remote(h_scr, gath.at[0, :, theirs], far_send.at[0], far_recv.at[0], sibling).wait_recv()
@@ -371,8 +372,10 @@
     def chip_copy(rel):
         return remote(s2_send.at[rel], s2_recv.at[rel], p2_send.at[rel], p2_recv.at[rel], peer(rel))
 
+    half_width = wo_low.shape[1]
+    late = [pltpu.make_async_copy(wo_hbm.at[:, pl.ds(half_width + k * part_width, part_width)], wo_high.at[k], wo_sems.at[k]) for k in range(2)]
     loads = [pltpu.make_async_copy(src, dst, w_sems.at[k]) for k, (src, dst) in enumerate(((wg_hbm, wg), (wu_hbm, wu), (wd_hbm, wd), (gm_hbm, gm_ref)))]
-    for load in loads:
+    for load in late + loads:
         load.start()
     barrier = pltpu.get_barrier_semaphore()
     for target in (sibling, peer(1), peer(2), peer(3)):
@@ -387,7 +390,12 @@
         return pl.ds(part * part_width, part_width)
 
     for part in range(CHUNKS):
-        attn_out = jnp.dot(heads_scr[...], wo[:, columns(part)], preferred_element_type=f32)
+        if part < 2:
+            weights = wo_low[:, columns(part)]
+        else:
+            late[part - 2].wait()
+            weights = wo_high[part - 2]
+        attn_out = jnp.dot(heads_scr[...], weights, preferred_element_type=f32)
         resid = (hid_ref[:, columns(part)].astype(f32) + attn_out).astype(bf16)
         h_scr[part] = resid
         gath[0, part, mine] = resid
@@ -395,7 +403,9 @@
             pl.semaphore_wait(barrier, 4)
         near_copy(1, part).start()
         near_copy(2, part).start()
-    far_copy(3).start()
+        if part > 0:
+            near_copy(3, part - 1).start()
+    near_copy(3, CHUNKS - 1).start()
     far_copy(0).start()
 
     def normed_rows(rel, at):
@@ -439,16 +449,18 @@
     forward_arrived(2)
     normed_rows(2, 2 * rows)
     contract(activation(4 * rows), (1, 2))
-    far_copy(3).wait_recv()
+    for part in range(CHUNKS):
+        near_copy(3, part).wait_recv()
     forward_copy(3).start()
     sibling_rows_arrived()
     normed_rows(0, 2 * rows)
+
+    forward_arrived(3)
+    normed_rows(3, 0)
+    act = activation(4 * rows)
     send_sum(1)
     send_sum(2)
-
-    forward_arrived(3)
-    normed_rows(3, 0)
-    contract(activation(4 * rows), (3, 0))
+    contract(act, (3, 0))
     send_sum(3)
     pair_copy(0).wait_recv()
 
@@ -458,10 +470,9 @@
         chip_copy(rel).wait_recv()
         total = total + s2_recv[rel].astype(f32)
     out_ref[...] = total.astype(bf16)
-    for rel in (1, 2):
+    for rel in (1, 2, 3):
         for part in range(CHUNKS):
             near_copy(rel, part).wait_send()
-    far_copy(3).wait_send()
     far_copy(0).wait_send()
     for rel in range(4):
         pair_copy(rel).wait_send()
@@ -470,7 +481,7 @@
         chip_copy(rel).wait_send()
 
 
-def mlp_call(o_lat, hidden, w_uv, w_o, gain_mlp, w_gate, w_up, w_down):
+def mlp_call(o_lat, hidden, w_uv, wo_low, gain_mlp, w_o, w_gate, w_up, w_down):
     rows, width = hidden.shape
     cols = w_gate.shape[1]
     bf16, f32 = jnp.bfloat16, jnp.float32
@@ -478,15 +489,16 @@
     hbm = pl.BlockSpec(memory_space=pltpu.HBM)
     dma = pltpu.SemaphoreType.DMA
     part_width = width // CHUNKS
-    held = [pltpu.with_memory_space_constraint(x, pltpu.VMEM) for x in (o_lat, hidden, w_uv, w_o)]
-    streamed = [pltpu.with_memory_space_constraint(x, pltpu.HBM) for x in (w_gate, w_up, w_down)]
+    held = [pltpu.with_memory_space_constraint(x, pltpu.VMEM) for x in (o_lat, hidden, w_uv, wo_low)]
+    streamed = [pltpu.with_memory_space_constraint(x, pltpu.HBM) for x in (w_o, w_gate, w_up, w_down)]
     return pl.pallas_call(
         mlp_kernel,
         out_shape=pltpu.VMEM((rows, width), bf16),
-        in_specs=[vmem, vmem, vmem, vmem, hbm, hbm, hbm, hbm],
+        in_specs=[vmem, vmem, vmem, vmem, hbm, hbm, hbm, hbm, hbm],
         out_specs=vmem,
         scratch_shapes=[
             pltpu.VMEM(gain_mlp.shape, bf16),
+            pltpu.VMEM((2, w_o.shape[0], part_width), bf16),
             pltpu.VMEM((width, cols), bf16),
             pltpu.VMEM((width, cols), bf16),
             pltpu.VMEM((cols, width), bf16),
@@ -499,9 +511,9 @@
             pltpu.VMEM((4, rows, width), f32),
             pltpu.VMEM((4, rows, width), bf16),
             pltpu.VMEM((4, rows, width), bf16),
-            dma((4,)), dma((4, CHUNKS)), dma((4, CHUNKS)), dma((4,)), dma((4,)), dma((4,)), dma((4,)), dma((4,)), dma((4,)), dma((4,)), dma((4,)),
+            dma((4,)), dma((2,)), dma((4, CHUNKS)), dma((4, CHUNKS)), dma((4,)), dma((4,)), dma((4,)), dma((4,)), dma((4,)), dma((4,)), dma((4,)), dma((4,)),
         ],
-        compiler_params=pltpu.CompilerParams(collective_id=0, has_side_effects=True, vmem_limit_bytes=33 * 1024 * 1024),
+        compiler_params=pltpu.CompilerParams(collective_id=0, has_side_effects=True, vmem_limit_bytes=VMEM_LIMIT),
         name="mlp_exchange",
     )(*held, gain_mlp, *streamed)
 
@@ -513,7 +525,7 @@
 
     def local_step(hidden, cache_lat, cache_rope, seq_lens, gain_attn, w_dq, gain_q, w_uq, w_qr, w_dkv, gain_kv, w_uk, w_uv, w_o, gain_mlp, w_gate, w_up, w_down):
         new_lat, new_rope, o_lat, hid_rows, uv_held, wo_held = attn_call(hidden, cache_lat, cache_rope, seq_lens, gain_attn, w_dq, gain_q, w_uq, w_qr, w_dkv, gain_kv, w_uk, w_uv, w_o)
-        out_hidden = mlp_call(o_lat, hid_rows, uv_held, wo_held, gain_mlp, w_gate, w_up, w_down)
+        out_hidden = mlp_call(o_lat, hid_rows, uv_held, wo_held, gain_mlp, w_o, w_gate, w_up, w_down)
         return out_hidden, new_lat, new_rope
 
     return jax.shard_map(local_step, mesh=mesh, in_specs=in_specs, out_specs=(row_spec, row_spec, row_spec), check_vma=False)

time: 53.4 us -> 57.3 us (1.073)
  the two profiles are of different devices: /device:TPU:5 before, /device:TPU:0 now
where the time goes in v6:
time: 57.3 us; the launch traced here: 57.2 us
  Pallas kernels  55.9 us (98%)
  local copies, waits for them, and re-layouts  0.66 us (1%)
  between operations  0.65 us (1%)
    pallas_call x1, Pallas kernels, mlp_call(): pl.pallas_call(mlp_kernel, out_shape=pltpu.VMEM((rows, width), bf16), in_...  29.8 us
    pallas_call x1, Pallas kernels, attn_call(): pl.pallas_call(attn_kernel, out_shape=(jax.ShapeDtypeStruct((rows, kv_dim...  26.1 us

profile of v6, /device:TPU:0, one launch (start us, length us, event | category | flops | bytes accessed | tf_op | source)
XLA Modules:
  0.0 57.2 jit_solution(7187666964152675873)
XLA Ops:
  0.6 26.1 %attention.1 = (bf16[32,512]{1,0:T(8,128)(2,1)}, bf16[32,64]{1,0:T(8,128)(2,1)}, f32[4,768,128]{2,1,0:T(8,128)S(1)}, bf16[32,2048]{1,0:T(8,128)(2,1)S(1)}, bf16[...) custom-call(s32[32]{0:T(128)} %lens_hbm.1, bf16[32,2048]{1,0:T(8,128)(2,1)} %hid_hbm.1, ...), custom_call_target="tpu_custom_call" | custom-call | tf_op jit(solution)/shard_map/attention/pallas_call | solution.py:297
  26.7 29.8 %mlp_exchange.1 = bf16[32,2048]{1,0:T(8,128)(2,1)S(1)} custom-call(f32[4,768,128]{2,1,0:T(8,128)S(1)} %get-tuple-element.9.o_ref, bf16[32,2048]{1,0:T(8,128)(2,1)S(1)} %get-tuple-element.10.hid_ref, bf16[20,512,256]{2,1,0:T(8,128)(2,1)S(1)} %get-tuple-element.11.wuv, bf16[5120,1024]{1,0:T(8,128)(2,1)S(1)} %get-tuple-element.12.wo_low, ...), custom_call_target="tpu_custom_call" | custom-call | tf_op jit(solution)/shard_map/mlp_exchange/pallas_call | solution.py:494
  56.5 0.7 %copy.22 = bf16[32,2048]{1,0:T(8,128)(2,1)} copy(bf16[32,2048]{1,0:T(8,128)(2,1)S(1)} %mlp_exchange.1) | data formatting | bytes 262144

commit v7 on v6

--- a/solution.py
+++ b/solution.py
@@ -10,9 +10,9 @@
 
 HEADS = 20
 HEAD_PAD = 24
-RING = 24
+RING = 20
 GROUP = 4
-VMEM_LIMIT = 43 * 1024 * 1024
+VMEM_LIMIT = 39 * 1024 * 1024
 WO_PARTS = 16
 WO_STEP = 3
 
@@ -32,11 +32,14 @@
     f32, bf16 = jnp.float32, jnp.bfloat16
     nt = (((1,), (1,)), ((), ()))
 
-    wuq = wo.at[pl.ds(0, HEADS * nope_dim), pl.ds(0, q_dim)]
     wqr = wo.at[pl.ds(HEADS * nope_dim, HEADS * rope_dim), pl.ds(0, q_dim)]
-    early = [pltpu.make_async_copy(src, dst, w_sems.at[k]) for k, (src, dst) in enumerate(((wdq_hbm, wdq), (wdkv_hbm, wdkv), (wqr_hbm, wqr), (wuq_hbm, wuq), (wuk_hbm, wuk)))]
+    cut = 8 * nope_dim
+    uq_low = wo.at[pl.ds(0, cut), pl.ds(0, q_dim)]
+    uq_high = wo.at[pl.ds(cut, HEADS * nope_dim - cut), pl.ds(0, q_dim)]
+    pairs = ((wdq_hbm, wdq), (wdkv_hbm, wdkv), (wqr_hbm, wqr), (wuq_hbm.at[pl.ds(0, cut)], uq_low), (wuq_hbm.at[pl.ds(cut, HEADS * nope_dim - cut)], uq_high), (wuk_hbm, wuk))
+    early = [pltpu.make_async_copy(src, dst, w_sems.at[k]) for k, (src, dst) in enumerate(pairs)]
     small = [pltpu.make_async_copy(src, dst, in_sems.at[k]) for k, (src, dst) in enumerate(((lens_hbm, lens_ref), (hid_hbm, hid_ref), (ga_hbm, ga_ref), (gq_hbm, gq_ref), (gkv_hbm, gkv_ref)))]
-    for copy in small + early:
+    for copy in small + early[:2]:
         copy.start()
     small[0].wait()
 
@@ -86,11 +89,10 @@
         span = pl.ds(pl.multiple_of(part * wo_rows, 32), wo_rows)
         return pltpu.make_async_copy(wo_hbm.at[span, pl.ds(0, wo.shape[1])], wo.at[span], o_sems.at[1])
 
-    def fill_ring(slot, _):
-        start_place(slot, slot)
-        return 0
-
-    lax.fori_loop(0, RING, fill_ring, 0)
+    def start_group(group):
+        for sub in range(GROUP):
+            start_place(group * GROUP + sub, lax.rem(group * GROUP, RING) + sub)
+
     uv_copy = pltpu.make_async_copy(wuv_hbm, wuv, o_sems.at[0])
 
     def norm(values, gain_ref):
@@ -123,11 +125,15 @@
     small[3].wait()
     small[4].wait()
     early[0].wait()
+    early[2].start()
+    early[3].start()
     q_raw = jnp.dot(normed, wdq[...], preferred_element_type=f32)
     early[1].wait()
+    early[4].start()
     kv_raw = lax.dot_general(normed, wdkv[...], nt, preferred_element_type=f32)
     q_in = norm(q_raw, gq_ref).astype(bf16)
     early[2].wait()
+    early[5].start()
     rope_raw = lax.dot_general(q_in, wo[pl.ds(HEADS * nope_dim, HEADS * rope_dim), pl.ds(0, q_dim)], nt, preferred_element_type=f32)
     new_lat = norm(kv_raw[:, :kv_dim], gkv_ref).astype(bf16)
     newlat_ref[...] = new_lat
@@ -150,19 +156,23 @@
                 q_scr[col, pl.ds(head, rows, stride=HEAD_PAD), :] = q_abs[:, col * 128:(col + 1) * 128]
 
     early[3].wait()
+    start_group(0)
     quads = HEADS // 4
     ahead = nope_quad(0)
     for pair in range(HEADS // 2):
         turned = rotate(rope_raw[:, pair * 128:(pair + 1) * 128]).astype(bf16).astype(f32)
         qr_scr[pl.ds(2 * pair, rows, stride=HEAD_PAD), :] = turned
         qr_scr[pl.ds(2 * pair + 1, rows, stride=HEAD_PAD), :] = pltpu.roll(turned, rope_dim, 1)
+    ahead2 = nope_quad(1)
+    early[4].wait()
+    start_group(1)
+    pending_quads = [ahead, ahead2, nope_quad(2)]
+    early[5].wait()
+    start_group(2)
     for quad in range(quads):
-        now = ahead
-        if quad + 1 < quads:
-            ahead = nope_quad(quad + 1)
-        if quad == 0:
-            early[4].wait()
-        absorb_quad(quad, now)
+        absorb_quad(quad, pending_quads[quad])
+        if quad + 3 < quads:
+            pending_quads.append(nope_quad(quad + 3))
 
     for copy in outgoing:
         copy.start()
@@ -215,6 +225,7 @@
 
     first = members(0)
     wait_members(0)
+    start_group(3)
 
     def first_scores(span):
         for sub, (row, slot) in enumerate(first):
@@ -226,6 +237,11 @@
         now = members(group)
         later = members(group + 1)
         wait_members(group + 1)
+        pl.when(group + 4 < groups)(lambda: start_group(group + 4))
+        pl.when(group == 0)(uv_copy.start)
+        for extra in range(WO_STEP):
+            part = group * WO_STEP + extra
+            pl.when(part < WO_PARTS)(lambda part=part: wo_copy(part).start())
 
         def run(span):
             pending = None
@@ -240,18 +256,6 @@
 
         by_span(group_blocks(group), run)
 
-        @pl.when(group < groups - RING // GROUP)
-        def _():
-            for sub in range(GROUP):
-                start_place(group * GROUP + RING + sub, now[sub][1])
-
-        @pl.when(group == 0)
-        def _():
-            uv_copy.start()
-
-        for extra in range(WO_STEP):
-            part = group * WO_STEP + extra
-            pl.when(part < WO_PARTS)(lambda part=part: wo_copy(part).start())
         return 0
 
     lax.fori_loop(0, groups - 1, group_step, 0)
@@ -292,7 +296,7 @@
         pltpu.VMEM((kv_dim // 128, rows * HEAD_PAD, 128), f32),
         pltpu.VMEM(hidden.shape, bf16),
         pltpu.VMEM(uv_t.shape, bf16),
-        pltpu.VMEM((w_o.shape[0], width // 2), bf16),
+        pltpu.VMEM((w_o.shape[0], width * 3 // 4), bf16),
     )
     return pl.pallas_call(
         attn_kernel,
@@ -318,7 +322,7 @@
             pltpu.SMEM((rows,), jnp.int32),
             pltpu.SMEM((rows,), jnp.int32),
             pltpu.SMEM((9,), jnp.int32),
-            dma((5,)), dma((2,)), dma((5,)), dma((2,)), dma((RING,)), dma((RING,)),
+            dma((6,)), dma((2,)), dma((5,)), dma((2,)), dma((RING,)), dma((RING,)),
         ],
         compiler_params=pltpu.CompilerParams(vmem_limit_bytes=VMEM_LIMIT),
         name="attention",
@@ -331,7 +335,7 @@
 
 def mlp_kernel(o_ref, hid_ref, wuv, wo_low, gm_hbm, wo_hbm, wg_hbm, wu_hbm, wd_hbm, out_ref,
                gm_ref, wo_high, wg, wu, wd, heads_scr, h_scr, gath, m_scr, keep, s1_send, s1_recv, s2_send, s2_recv,
-               w_sems, wo_sems, near_send, near_recv, far_send, far_recv, fw_send, fw_recv, p1_send, p1_recv, p2_send, p2_recv):
+               w_sems, wo_sem, near_send, near_recv, far_send, far_recv, fw_send, fw_recv, p1_send, p1_recv, p2_send, p2_recv):
     rows, width = hid_ref.shape
     part_width = width // CHUNKS
     heads, kv_dim, v_dim = wuv.shape
@@ -372,11 +376,10 @@
     def chip_copy(rel):
         return remote(s2_send.at[rel], s2_recv.at[rel], p2_send.at[rel], p2_recv.at[rel], peer(rel))
 
-    half_width = wo_low.shape[1]
-    late = [pltpu.make_async_copy(wo_hbm.at[:, pl.ds(half_width + k * part_width, part_width)], wo_high.at[k], wo_sems.at[k]) for k in range(2)]
+    held_width = wo_low.shape[1]
+    late = pltpu.make_async_copy(wo_hbm.at[:, pl.ds(held_width, part_width)], wo_high, wo_sem)
     loads = [pltpu.make_async_copy(src, dst, w_sems.at[k]) for k, (src, dst) in enumerate(((wg_hbm, wg), (wu_hbm, wu), (wd_hbm, wd), (gm_hbm, gm_ref)))]
-    for load in late + loads:
-        load.start()
+    late.start()
     barrier = pltpu.get_barrier_semaphore()
     for target in (sibling, peer(1), peer(2), peer(3)):
         pl.semaphore_signal(barrier, inc=1, device_id={"g": target}, device_id_type=MESH)
@@ -390,16 +393,18 @@
         return pl.ds(part * part_width, part_width)
 
     for part in range(CHUNKS):
-        if part < 2:
+        if part < CHUNKS - 1:
             weights = wo_low[:, columns(part)]
         else:
-            late[part - 2].wait()
-            weights = wo_high[part - 2]
+            late.wait()
+            weights = wo_high[...]
         attn_out = jnp.dot(heads_scr[...], weights, preferred_element_type=f32)
         resid = (hid_ref[:, columns(part)].astype(f32) + attn_out).astype(bf16)
         h_scr[part] = resid
         gath[0, part, mine] = resid
         if part == 0:
+            for load in loads:
+                load.start()
             pl.semaphore_wait(barrier, 4)
         near_copy(1, part).start()
         near_copy(2, part).start()
@@ -498,7 +503,7 @@
         out_specs=vmem,
         scratch_shapes=[
             pltpu.VMEM(gain_mlp.shape, bf16),
-            pltpu.VMEM((2, w_o.shape[0], part_width), bf16),
+            pltpu.VMEM((w_o.shape[0], part_width), bf16),
             pltpu.VMEM((width, cols), bf16),
             pltpu.VMEM((width, cols), bf16),
             pltpu.VMEM((cols, width), bf16),
@@ -511,7 +516,7 @@
             pltpu.VMEM((4, rows, width), f32),
             pltpu.VMEM((4, rows, width), bf16),
             pltpu.VMEM((4, rows, width), bf16),
-            dma((4,)), dma((2,)), dma((4, CHUNKS)), dma((4, CHUNKS)), dma((4,)), dma((4,)), dma((4,)), dma((4,)), dma((4,)), dma((4,)), dma((4,)), dma((4,)),
+            dma((4,)), dma, dma((4, CHUNKS)), dma((4, CHUNKS)), dma((4,)), dma((4,)), dma((4,)), dma((4,)), dma((4,)), dma((4,)), dma((4,)), dma((4,)),
         ],
         compiler_params=pltpu.CompilerParams(collective_id=0, has_side_effects=True, vmem_limit_bytes=VMEM_LIMIT),
         name="mlp_exchange",

time: 57.3 us -> 52.1 us (0.909)
  Pallas kernels: 55.9 us -> 50.4 us
    pallas_call x1, Pallas kernels: 29.8 us -> 25.5 us  [mlp_call(): pl.pallas_call(mlp_kernel, out_shape=pltpu.VMEM((rows, width), bf16), in_...]
    pallas_call x1, Pallas kernels: 26.1 us -> 24.9 us  [attn_call(): pl.pallas_call(attn_kernel, out_shape=(jax.ShapeDtypeStruct((rows, kv_dim...]
where the time goes in v7:
time: 52.1 us; the launch traced here: 51.7 us
  Pallas kernels  50.4 us (97%)
  local copies, waits for them, and re-layouts  0.66 us (1%)
  between operations  0.65 us (1%)
    pallas_call x1, Pallas kernels, mlp_call(): pl.pallas_call(mlp_kernel, out_shape=pltpu.VMEM((rows, width), bf16), in_...  25.5 us
    pallas_call x1, Pallas kernels, attn_call(): pl.pallas_call(attn_kernel, out_shape=(jax.ShapeDtypeStruct((rows, kv_dim...  24.9 us

profile of v7, /device:TPU:0, one launch (start us, length us, event | category | flops | bytes accessed | tf_op | source)
XLA Modules:
  0.0 51.7 jit_solution(8972764982411472738)
XLA Ops:
  0.6 24.9 %attention.1 = (bf16[32,512]{1,0:T(8,128)(2,1)}, bf16[32,64]{1,0:T(8,128)(2,1)}, f32[4,768,128]{2,1,0:T(8,128)S(1)}, bf16[32,2048]{1,0:T(8,128)(2,1)S(1)}, bf16[...) custom-call(s32[32]{0:T(128)} %lens_hbm.1, bf16[32,2048]{1,0:T(8,128)(2,1)} %hid_hbm.1, ...), custom_call_target="tpu_custom_call" | custom-call | tf_op jit(solution)/shard_map/attention/pallas_call | solution.py:301
  25.6 25.5 %mlp_exchange.1 = bf16[32,2048]{1,0:T(8,128)(2,1)S(1)} custom-call(f32[4,768,128]{2,1,0:T(8,128)S(1)} %get-tuple-element.9.o_ref, bf16[32,2048]{1,0:T(8,128)(2,1)S(1)} %get-tuple-element.10.hid_ref, bf16[20,512,256]{2,1,0:T(8,128)(2,1)S(1)} %get-tuple-element.11.wuv, bf16[5120,1536]{1,0:T(8,128)(2,1)S(1)} %get-tuple-element.12.wo_low, ...), custom_call_target="tpu_custom_call" | custom-call | tf_op jit(solution)/shard_map/mlp_exchange/pallas_call | solution.py:499
  51.0 0.7 %copy.22 = bf16[32,2048]{1,0:T(8,128)(2,1)} copy(bf16[32,2048]{1,0:T(8,128)(2,1)S(1)} %mlp_exchange.1) | data formatting | bytes 262144

commit v8 on v7

--- a/solution.py
+++ b/solution.py
@@ -12,6 +12,7 @@
 HEAD_PAD = 24
 RING = 20
 GROUP = 4
+SPANS = (384, 512, 640, 768, 896, 1024)
 VMEM_LIMIT = 39 * 1024 * 1024
 WO_PARTS = 16
 WO_STEP = 3
@@ -71,7 +72,7 @@
 
     def lat_copy(place_id, slot):
         row = order[place_id]
-        span = jnp.maximum((lens_ref[order[(place_id // GROUP) * GROUP]] + 255) >> 8, 2) << 8
+        span = jnp.maximum((lens_ref[order[(place_id // GROUP) * GROUP]] + 127) >> 7, SPANS[0] // 128) << 7
         count = jnp.where(place_id < RING, span, ((lens_ref[row] + 15) >> 4) << 4)
         count = pl.multiple_of(count, 16)
         return pltpu.make_async_copy(lat_hbm.at[row, pl.ds(0, count)], lat_buf.at[slot, pl.ds(0, count)], lat_sems.at[slot])
@@ -217,11 +218,12 @@
             rope_copy(row, slot).wait()
 
     def group_blocks(group):
-        return (lens_ref[order[group * GROUP]] + 255) >> 8
-
-    def by_span(blocks, run):
-        for size, test in ((2, blocks <= 2), (3, blocks == 3), (4, blocks == 4)):
-            pl.when(test)(functools.partial(run, size * cache_len // 4))
+        return (lens_ref[order[group * GROUP]] + 127) >> 7
+
+    def by_span(blocks, run, spans):
+        for index, span in enumerate(spans):
+            low = spans[index - 1] // 128 if index else 0
+            pl.when((blocks > low) & (blocks <= span // 128))(functools.partial(run, span))
 
     first = members(0)
     wait_members(0)
@@ -231,7 +233,7 @@
         for sub, (row, slot) in enumerate(first):
             s_scr[sub, :, pl.ds(0, span)] = score_part(row, slot, span)
 
-    by_span(group_blocks(0), first_scores)
+    by_span(group_blocks(0), first_scores, (512, 768, 1024))
 
     def group_step(group, _):
         now = members(group)
@@ -254,7 +256,7 @@
                 pending = (*now[sub], *probs)
             mix_part(*pending, span)
 
-        by_span(group_blocks(group), run)
+        by_span(group_blocks(group), run, SPANS)
 
         return 0
 
@@ -270,7 +272,7 @@
             pending = (*last[sub], *probs)
         mix_part(*pending, span)
 
-    by_span(group_blocks(groups - 1), last_mix)
+    by_span(group_blocks(groups - 1), last_mix, SPANS)
     uv_copy.wait()
     pltpu.make_async_copy(wo_hbm.at[:, pl.ds(0, wo.shape[1])], wo, o_sems.at[1]).wait()
     for copy in outgoing:
@@ -296,7 +298,7 @@
         pltpu.VMEM((kv_dim // 128, rows * HEAD_PAD, 128), f32),
         pltpu.VMEM(hidden.shape, bf16),
         pltpu.VMEM(uv_t.shape, bf16),
-        pltpu.VMEM((w_o.shape[0], width * 3 // 4), bf16),
+        pltpu.VMEM((w_o.shape[0], width // 2), bf16),
     )
     return pl.pallas_call(
         attn_kernel,
@@ -335,7 +337,7 @@
 
 def mlp_kernel(o_ref, hid_ref, wuv, wo_low, gm_hbm, wo_hbm, wg_hbm, wu_hbm, wd_hbm, out_ref,
                gm_ref, wo_high, wg, wu, wd, heads_scr, h_scr, gath, m_scr, keep, s1_send, s1_recv, s2_send, s2_recv,
-               w_sems, wo_sem, near_send, near_recv, far_send, far_recv, fw_send, fw_recv, p1_send, p1_recv, p2_send, p2_recv):
+               w_sems, wo_sems, near_send, near_recv, far_send, far_recv, fw_send, fw_recv, p1_send, p1_recv, p2_send, p2_recv):
     rows, width = hid_ref.shape
     part_width = width // CHUNKS
     heads, kv_dim, v_dim = wuv.shape
@@ -370,16 +372,16 @@
     def forward_arrived(rel):
         remote(gath.at[rel, :, theirs], gath.at[rel, :, theirs], fw_send.at[rel], fw_recv.at[rel], sibling).wait_recv()
 
-    def pair_copy(rel):
-        return remote(s1_send.at[rel], s1_recv.at[rel], p1_send.at[rel], p1_recv.at[rel], sibling)
-
-    def chip_copy(rel):
-        return remote(s2_send.at[rel], s2_recv.at[rel], p2_send.at[rel], p2_recv.at[rel], peer(rel))
+    def pair_copy(rel, half):
+        return remote(s1_send.at[rel, half], s1_recv.at[rel, half], p1_send.at[rel, half], p1_recv.at[rel, half], sibling)
+
+    def chip_copy(rel, half):
+        return remote(s2_send.at[rel, half], s2_recv.at[rel, half], p2_send.at[rel, half], p2_recv.at[rel, half], peer(rel))
 
     held_width = wo_low.shape[1]
-    late = pltpu.make_async_copy(wo_hbm.at[:, pl.ds(held_width, part_width)], wo_high, wo_sem)
+    late = [pltpu.make_async_copy(wo_hbm.at[:, pl.ds(held_width + k * part_width, part_width)], wo_high.at[k], wo_sems.at[k]) for k in range(2)]
     loads = [pltpu.make_async_copy(src, dst, w_sems.at[k]) for k, (src, dst) in enumerate(((wg_hbm, wg), (wu_hbm, wu), (wd_hbm, wd), (gm_hbm, gm_ref)))]
-    late.start()
+    late[0].start()
     barrier = pltpu.get_barrier_semaphore()
     for target in (sibling, peer(1), peer(2), peer(3)):
         pl.semaphore_signal(barrier, inc=1, device_id={"g": target}, device_id_type=MESH)
@@ -393,19 +395,21 @@
         return pl.ds(part * part_width, part_width)
 
     for part in range(CHUNKS):
-        if part < CHUNKS - 1:
+        if part < 2:
             weights = wo_low[:, columns(part)]
         else:
-            late.wait()
-            weights = wo_high[...]
+            late[part - 2].wait()
+            weights = wo_high[part - 2]
         attn_out = jnp.dot(heads_scr[...], weights, preferred_element_type=f32)
         resid = (hid_ref[:, columns(part)].astype(f32) + attn_out).astype(bf16)
         h_scr[part] = resid
         gath[0, part, mine] = resid
         if part == 0:
+            late[1].start()
+            pl.semaphore_wait(barrier, 4)
+        if part == 1:
             for load in loads:
                 load.start()
-            pl.semaphore_wait(barrier, 4)
         near_copy(1, part).start()
         near_copy(2, part).start()
         if part > 0:
@@ -429,19 +433,22 @@
         up = jnp.dot(block, wu[...], preferred_element_type=f32)
         return (jax.nn.silu(gate) * up).astype(bf16)
 
+    half_width = width // 2
+
     def contract(act, rels):
-        part = jnp.dot(act, wd[...], preferred_element_type=f32)
-        for index, rel in enumerate(rels):
-            low = part[2 * index * rows:(2 * index + 1) * rows]
-            high = part[(2 * index + 1) * rows:(2 * index + 2) * rows]
-            s1_send[rel] = jnp.where(is_low, high, low)
-            keep[rel] = jnp.where(is_low, low, high)
-            pair_copy(rel).start()
-
-    def send_sum(rel):
-        pair_copy(rel).wait_recv()
-        s2_send[rel] = (keep[rel] + s1_recv[rel]).astype(bf16)
-        chip_copy(rel).start()
+        for half in range(2):
+            part = jnp.dot(act, wd[:, pl.ds(half * half_width, half_width)], preferred_element_type=f32)
+            for index, rel in enumerate(rels):
+                low = part[2 * index * rows:(2 * index + 1) * rows]
+                high = part[(2 * index + 1) * rows:(2 * index + 2) * rows]
+                s1_send[rel, half] = jnp.where(is_low, high, low)
+                keep[rel, half] = jnp.where(is_low, low, high)
+                pair_copy(rel, half).start()
+
+    def send_sum(rel, half):
+        pair_copy(rel, half).wait_recv()
+        s2_send[rel, half] = (keep[rel, half] + s1_recv[rel, half]).astype(bf16)
+        chip_copy(rel, half).start()
 
     for rel in (1, 2):
         for part in range(CHUNKS):
@@ -460,30 +467,37 @@
     sibling_rows_arrived()
     normed_rows(0, 2 * rows)
 
+    for half in range(2):
+        send_sum(1, half)
+        send_sum(2, half)
+
     forward_arrived(3)
     normed_rows(3, 0)
-    act = activation(4 * rows)
-    send_sum(1)
-    send_sum(2)
-    contract(act, (3, 0))
-    send_sum(3)
-    pair_copy(0).wait_recv()
-
-    cols = [h_scr[part].astype(f32) for part in range(CHUNKS)]
-    total = jnp.concatenate(cols, axis=1) + (keep[0] + s1_recv[0])
+    contract(activation(4 * rows), (3, 0))
+    send_sum(3, 0)
+    send_sum(3, 1)
+    totals = []
+    for half in range(2):
+        pair_copy(0, half).wait_recv()
+        residual = jnp.concatenate([h_scr[2 * half].astype(f32), h_scr[2 * half + 1].astype(f32)], axis=1)
+        totals.append(residual + (keep[0, half] + s1_recv[0, half]))
     for rel in (1, 2, 3):
-        chip_copy(rel).wait_recv()
-        total = total + s2_recv[rel].astype(f32)
-    out_ref[...] = total.astype(bf16)
+        for half in range(2):
+            chip_copy(rel, half).wait_recv()
+            totals[half] = totals[half] + s2_recv[rel, half].astype(f32)
+    for half in range(2):
+        out_ref[:, half * half_width:(half + 1) * half_width] = totals[half].astype(bf16)
     for rel in (1, 2, 3):
         for part in range(CHUNKS):
             near_copy(rel, part).wait_send()
     far_copy(0).wait_send()
-    for rel in range(4):
-        pair_copy(rel).wait_send()
+    for half in range(2):
+        for rel in range(4):
+            pair_copy(rel, half).wait_send()
+        for rel in (1, 2, 3):
+            chip_copy(rel, half).wait_send()
     for rel in (1, 2, 3):
         forward_copy(rel).wait_send()
-        chip_copy(rel).wait_send()
 
 
 def mlp_call(o_lat, hidden, w_uv, wo_low, gain_mlp, w_o, w_gate, w_up, w_down):
@@ -503,7 +517,7 @@
         out_specs=vmem,
         scratch_shapes=[
             pltpu.VMEM(gain_mlp.shape, bf16),
-            pltpu.VMEM((w_o.shape[0], part_width), bf16),
+            pltpu.VMEM((2, w_o.shape[0], part_width), bf16),
             pltpu.VMEM((width, cols), bf16),
             pltpu.VMEM((width, cols), bf16),
             pltpu.VMEM((cols, width), bf16),
@@ -511,12 +525,12 @@
             pltpu.VMEM((CHUNKS, rows, part_width), bf16),
             pltpu.VMEM((4, CHUNKS, 2 * rows, part_width), bf16),
             pltpu.VMEM((4 * rows, width), bf16),
-            pltpu.VMEM((4, rows, width), f32),
-            pltpu.VMEM((4, rows, width), f32),
-            pltpu.VMEM((4, rows, width), f32),
-            pltpu.VMEM((4, rows, width), bf16),
-            pltpu.VMEM((4, rows, width), bf16),
-            dma((4,)), dma, dma((4, CHUNKS)), dma((4, CHUNKS)), dma((4,)), dma((4,)), dma((4,)), dma((4,)), dma((4,)), dma((4,)), dma((4,)), dma((4,)),
+            pltpu.VMEM((4, 2, rows, width // 2), f32),
+            pltpu.VMEM((4, 2, rows, width // 2), f32),
+            pltpu.VMEM((4, 2, rows, width // 2), f32),
+            pltpu.VMEM((4, 2, rows, width // 2), bf16),
+            pltpu.VMEM((4, 2, rows, width // 2), bf16),
+            dma((4,)), dma((2,)), dma((4, CHUNKS)), dma((4, CHUNKS)), dma((4,)), dma((4,)), dma((4,)), dma((4,)), dma((4, 2)), dma((4, 2)), dma((4, 2)), dma((4, 2)),
         ],
         compiler_params=pltpu.CompilerParams(collective_id=0, has_side_effects=True, vmem_limit_bytes=VMEM_LIMIT),
         name="mlp_exchange",

time: 52.1 us -> 50.9 us (0.977)
  Pallas kernels: 50.4 us -> 49.7 us
    pallas_call x1, Pallas kernels: 24.9 us -> 22.4 us  [attn_call(): pl.pallas_call(attn_kernel, out_shape=(jax.ShapeDtypeStruct((rows, kv_dim...]
    pallas_call x1, Pallas kernels: 25.5 us -> 27.3 us  [mlp_call(): pl.pallas_call(mlp_kernel, out_shape=pltpu.VMEM((rows, width), bf16), in_...]
where the time goes in v8:
time: 50.9 us; the launch traced here: 51 us
  Pallas kernels  49.7 us (98%)
  local copies, waits for them, and re-layouts  0.66 us (1%)
  between operations  0.65 us (1%)
    pallas_call x1, Pallas kernels, mlp_call(): pl.pallas_call(mlp_kernel, out_shape=pltpu.VMEM((rows, width), bf16), in_...  27.3 us
    pallas_call x1, Pallas kernels, attn_call(): pl.pallas_call(attn_kernel, out_shape=(jax.ShapeDtypeStruct((rows, kv_dim...  22.4 us

profile of v8, /device:TPU:0, one launch (start us, length us, event | category | flops | bytes accessed | tf_op | source)
XLA Modules:
  0.0 51.0 jit_solution(11940034296299194812)
XLA Ops:
  0.6 22.4 %attention.1 = (bf16[32,512]{1,0:T(8,128)(2,1)}, bf16[32,64]{1,0:T(8,128)(2,1)}, f32[4,768,128]{2,1,0:T(8,128)S(1)}, bf16[32,2048]{1,0:T(8,128)(2,1)S(1)}, bf16[...) custom-call(s32[32]{0:T(128)} %lens_hbm.1, bf16[32,2048]{1,0:T(8,128)(2,1)} %hid_hbm.1, ...), custom_call_target="tpu_custom_call" | custom-call | tf_op jit(solution)/shard_map/attention/pallas_call | solution.py:303
  23.0 27.3 %mlp_exchange.1 = bf16[32,2048]{1,0:T(8,128)(2,1)S(1)} custom-call(f32[4,768,128]{2,1,0:T(8,128)S(1)} %get-tuple-element.9.o_ref, bf16[32,2048]{1,0:T(8,128)(2,1)S(1)} %get-tuple-element.10.hid_ref, bf16[20,512,256]{2,1,0:T(8,128)(2,1)S(1)} %get-tuple-element.11.wuv, bf16[5120,1024]{1,0:T(8,128)(2,1)S(1)} %get-tuple-element.12.wo_low, ...), custom_call_target="tpu_custom_call" | custom-call | tf_op jit(solution)/shard_map/mlp_exchange/pallas_call | solution.py:513
  50.3 0.7 %copy.22 = bf16[32,2048]{1,0:T(8,128)(2,1)} copy(bf16[32,2048]{1,0:T(8,128)(2,1)S(1)} %mlp_exchange.1) | data formatting | bytes 262144

commit v9 on v8

--- a/solution.py
+++ b/solution.py
@@ -70,29 +70,28 @@
 
     lax.fori_loop(0, rows, place, 0)
 
-    def lat_copy(place_id, slot):
-        row = order[place_id]
-        span = jnp.maximum((lens_ref[order[(place_id // GROUP) * GROUP]] + 127) >> 7, SPANS[0] // 128) << 7
-        count = jnp.where(place_id < RING, span, ((lens_ref[row] + 15) >> 4) << 4)
-        count = pl.multiple_of(count, 16)
-        return pltpu.make_async_copy(lat_hbm.at[row, pl.ds(0, count)], lat_buf.at[slot, pl.ds(0, count)], lat_sems.at[slot])
-
-    def rope_copy(row, slot):
-        return pltpu.make_async_copy(rope_hbm.at[row], rope_buf.at[slot], rope_sems.at[slot])
-
-    def start_place(place_id, slot):
-        lat_copy(place_id, slot).start()
-        rope_copy(order[place_id], slot).start()
+    def group_blocks(group):
+        return (lens_ref[order[group * GROUP]] + 127) >> 7
+
+    def group_copies(group):
+        count = pl.multiple_of(jnp.maximum(group_blocks(group), SPANS[0] // 128) << 7, 128)
+        base = lax.rem(group * GROUP, RING)
+        copies = []
+        for sub in range(GROUP):
+            row, slot = order[group * GROUP + sub], base + sub
+            copies.append(pltpu.make_async_copy(lat_hbm.at[row, pl.ds(0, count)], lat_buf.at[slot, pl.ds(0, count)], lat_sems.at[slot]))
+            copies.append(pltpu.make_async_copy(rope_hbm.at[row], rope_buf.at[slot], rope_sems.at[slot]))
+        return copies
+
+    def start_group(group):
+        for copy in group_copies(group):
+            copy.start()
 
     wo_rows = wo.shape[0] // WO_PARTS
 
     def wo_copy(part):
         span = pl.ds(pl.multiple_of(part * wo_rows, 32), wo_rows)
         return pltpu.make_async_copy(wo_hbm.at[span, pl.ds(0, wo.shape[1])], wo.at[span], o_sems.at[1])
-
-    def start_group(group):
-        for sub in range(GROUP):
-            start_place(group * GROUP + sub, lax.rem(group * GROUP, RING) + sub)
 
     uv_copy = pltpu.make_async_copy(wuv_hbm, wuv, o_sems.at[0])
 
@@ -125,16 +124,17 @@
 
     small[3].wait()
     small[4].wait()
-    early[0].wait()
     early[2].start()
     early[3].start()
+    early[0].wait()
+    early[4].start()
+    early[5].start()
     q_raw = jnp.dot(normed, wdq[...], preferred_element_type=f32)
     early[1].wait()
-    early[4].start()
+    start_group(0)
     kv_raw = lax.dot_general(normed, wdkv[...], nt, preferred_element_type=f32)
     q_in = norm(q_raw, gq_ref).astype(bf16)
     early[2].wait()
-    early[5].start()
     rope_raw = lax.dot_general(q_in, wo[pl.ds(HEADS * nope_dim, HEADS * rope_dim), pl.ds(0, q_dim)], nt, preferred_element_type=f32)
     new_lat = norm(kv_raw[:, :kv_dim], gkv_ref).astype(bf16)
     newlat_ref[...] = new_lat
@@ -157,7 +157,7 @@
                 q_scr[col, pl.ds(head, rows, stride=HEAD_PAD), :] = q_abs[:, col * 128:(col + 1) * 128]
 
     early[3].wait()
-    start_group(0)
+    start_group(1)
     quads = HEADS // 4
     ahead = nope_quad(0)
     for pair in range(HEADS // 2):
@@ -166,10 +166,9 @@
         qr_scr[pl.ds(2 * pair + 1, rows, stride=HEAD_PAD), :] = pltpu.roll(turned, rope_dim, 1)
     ahead2 = nope_quad(1)
     early[4].wait()
-    start_group(1)
+    start_group(2)
     pending_quads = [ahead, ahead2, nope_quad(2)]
     early[5].wait()
-    start_group(2)
     for quad in range(quads):
         absorb_quad(quad, pending_quads[quad])
         if quad + 3 < quads:
@@ -213,12 +212,8 @@
         return [(order[group * GROUP + sub], lax.rem(group * GROUP, RING) + sub) for sub in range(GROUP)]
 
     def wait_members(group):
-        for sub, (row, slot) in enumerate(members(group)):
-            lat_copy(group * GROUP + sub, slot).wait()
-            rope_copy(row, slot).wait()
-
-    def group_blocks(group):
-        return (lens_ref[order[group * GROUP]] + 127) >> 7
+        for copy in group_copies(group):
+            copy.wait()
 
     def by_span(blocks, run, spans):
         for index, span in enumerate(spans):
@@ -427,9 +422,11 @@
             piece = gath[rel, part].astype(f32) * factor * gm_ref[columns(part)].astype(f32)
             m_scr[pl.ds(at, 2 * rows), columns(part)] = piece.astype(bf16)
 
-    def activation(count):
+    def activation(count, between=()):
         block = m_scr[pl.ds(0, count)]
         gate = jnp.dot(block, wg[...], preferred_element_type=f32)
+        for rel, half in between:
+            send_sum(rel, half)
         up = jnp.dot(block, wu[...], preferred_element_type=f32)
         return (jax.nn.silu(gate) * up).astype(bf16)
 
@@ -467,13 +464,9 @@
     sibling_rows_arrived()
     normed_rows(0, 2 * rows)
 
-    for half in range(2):
-        send_sum(1, half)
-        send_sum(2, half)
-
     forward_arrived(3)
     normed_rows(3, 0)
-    contract(activation(4 * rows), (3, 0))
+    contract(activation(4 * rows, ((1, 0), (2, 0), (1, 1), (2, 1))), (3, 0))
     send_sum(3, 0)
     send_sum(3, 1)
     totals = []

time: 50.9 us -> 50.3 us (0.988); the launches traced: 51 us -> 51.1 us
  no operation moved by 1% of the time
where the time goes in v9:
time: 50.3 us; the launch traced here: 51.1 us
  Pallas kernels  49.8 us (99%)
  local copies, waits for them, and re-layouts  0.66 us (1%)
  between operations  0.65 us (1%)
    pallas_call x1, Pallas kernels, mlp_call(): pl.pallas_call(mlp_kernel, out_shape=pltpu.VMEM((rows, width), bf16), in_...  27.1 us
    pallas_call x1, Pallas kernels, attn_call(): pl.pallas_call(attn_kernel, out_shape=(jax.ShapeDtypeStruct((rows, kv_dim...  22.6 us

profile of v9, /device:TPU:0, one launch (start us, length us, event | category | flops | bytes accessed | tf_op | source)
XLA Modules:
  0.0 51.1 jit_solution(12540207157549620005)
XLA Ops:
  0.6 22.6 %attention.1 = (bf16[32,512]{1,0:T(8,128)(2,1)}, bf16[32,64]{1,0:T(8,128)(2,1)}, f32[4,768,128]{2,1,0:T(8,128)S(1)}, bf16[32,2048]{1,0:T(8,128)(2,1)S(1)}, bf16[...) custom-call(s32[32]{0:T(128)} %lens_hbm.1, bf16[32,2048]{1,0:T(8,128)(2,1)} %hid_hbm.1, ...), custom_call_target="tpu_custom_call" | custom-call | tf_op jit(solution)/shard_map/attention/pallas_call | solution.py:298
  23.2 27.1 %mlp_exchange.1 = bf16[32,2048]{1,0:T(8,128)(2,1)S(1)} custom-call(f32[4,768,128]{2,1,0:T(8,128)S(1)} %get-tuple-element.9.o_ref, bf16[32,2048]{1,0:T(8,128)(2,1)S(1)} %get-tuple-element.10.hid_ref, bf16[20,512,256]{2,1,0:T(8,128)(2,1)S(1)} %get-tuple-element.11.wuv, bf16[5120,1024]{1,0:T(8,128)(2,1)S(1)} %get-tuple-element.12.wo_low, ...), custom_call_target="tpu_custom_call" | custom-call | tf_op jit(solution)/shard_map/mlp_exchange/pallas_call | solution.py:506
  50.4 0.7 %copy.22 = bf16[32,2048]{1,0:T(8,128)(2,1)} copy(bf16[32,2048]{1,0:T(8,128)(2,1)S(1)} %mlp_exchange.1) | data formatting | bytes 262144

commit v10 on v9

--- a/solution.py
+++ b/solution.py
@@ -80,7 +80,7 @@
         for sub in range(GROUP):
             row, slot = order[group * GROUP + sub], base + sub
             copies.append(pltpu.make_async_copy(lat_hbm.at[row, pl.ds(0, count)], lat_buf.at[slot, pl.ds(0, count)], lat_sems.at[slot]))
-            copies.append(pltpu.make_async_copy(rope_hbm.at[row], rope_buf.at[slot], rope_sems.at[slot]))
+            copies.append(pltpu.make_async_copy(rope_hbm.at[row, :, pl.ds(0, count)], rope_buf.at[slot, :, pl.ds(0, count)], rope_sems.at[slot]))
         return copies
 
     def start_group(group):
@@ -293,7 +293,7 @@
         pltpu.VMEM((kv_dim // 128, rows * HEAD_PAD, 128), f32),
         pltpu.VMEM(hidden.shape, bf16),
         pltpu.VMEM(uv_t.shape, bf16),
-        pltpu.VMEM((w_o.shape[0], width // 2), bf16),
+        pltpu.VMEM((w_o.shape[0], width * 3 // 4), bf16),
     )
     return pl.pallas_call(
         attn_kernel,
@@ -374,7 +374,7 @@
         return remote(s2_send.at[rel, half], s2_recv.at[rel, half], p2_send.at[rel, half], p2_recv.at[rel, half], peer(rel))
 
     held_width = wo_low.shape[1]
-    late = [pltpu.make_async_copy(wo_hbm.at[:, pl.ds(held_width + k * part_width, part_width)], wo_high.at[k], wo_sems.at[k]) for k in range(2)]
+    late = [pltpu.make_async_copy(wo_hbm.at[:, pl.ds(held_width + k * part_width, part_width)], wo_high.at[k], wo_sems.at[k]) for k in range(1)]
     loads = [pltpu.make_async_copy(src, dst, w_sems.at[k]) for k, (src, dst) in enumerate(((wg_hbm, wg), (wu_hbm, wu), (wd_hbm, wd), (gm_hbm, gm_ref)))]
     late[0].start()
     barrier = pltpu.get_barrier_semaphore()
@@ -390,21 +390,19 @@
         return pl.ds(part * part_width, part_width)
 
     for part in range(CHUNKS):
-        if part < 2:
+        if part < CHUNKS - 1:
             weights = wo_low[:, columns(part)]
         else:
-            late[part - 2].wait()
-            weights = wo_high[part - 2]
+            late[0].wait()
+            weights = wo_high[0]
         attn_out = jnp.dot(heads_scr[...], weights, preferred_element_type=f32)
         resid = (hid_ref[:, columns(part)].astype(f32) + attn_out).astype(bf16)
         h_scr[part] = resid
         gath[0, part, mine] = resid
         if part == 0:
-            late[1].start()
-            pl.semaphore_wait(barrier, 4)
-        if part == 1:
             for load in loads:
                 load.start()
+            pl.semaphore_wait(barrier, 4)
         near_copy(1, part).start()
         near_copy(2, part).start()
         if part > 0:
@@ -510,7 +508,7 @@
         out_specs=vmem,
         scratch_shapes=[
             pltpu.VMEM(gain_mlp.shape, bf16),
-            pltpu.VMEM((2, w_o.shape[0], part_width), bf16),
+            pltpu.VMEM((1, w_o.shape[0], part_width), bf16),
             pltpu.VMEM((width, cols), bf16),
             pltpu.VMEM((width, cols), bf16),
             pltpu.VMEM((cols, width), bf16),
@@ -523,7 +521,7 @@
             pltpu.VMEM((4, 2, rows, width // 2), f32),
             pltpu.VMEM((4, 2, rows, width // 2), bf16),
             pltpu.VMEM((4, 2, rows, width // 2), bf16),
-            dma((4,)), dma((2,)), dma((4, CHUNKS)), dma((4, CHUNKS)), dma((4,)), dma((4,)), dma((4,)), dma((4,)), dma((4, 2)), dma((4, 2)), dma((4, 2)), dma((4, 2)),
+            dma((4,)), dma((1,)), dma((4, CHUNKS)), dma((4, CHUNKS)), dma((4,)), dma((4,)), dma((4,)), dma((4,)), dma((4, 2)), dma((4, 2)), dma((4, 2)), dma((4, 2)),
         ],
         compiler_params=pltpu.CompilerParams(collective_id=0, has_side_effects=True, vmem_limit_bytes=VMEM_LIMIT),
         name="mlp_exchange",

time: 50.3 us -> 50.8 us (level); the launches traced: 51.1 us -> 50.6 us
    pallas_call x1, Pallas kernels: 27.1 us -> 26 us  [mlp_call(): pl.pallas_call(mlp_kernel, out_shape=pltpu.VMEM((rows, width), bf16), in_...]
    pallas_call x1, Pallas kernels: 22.6 us -> 23.3 us  [attn_call(): pl.pallas_call(attn_kernel, out_shape=(jax.ShapeDtypeStruct((rows, kv_dim...]
where the time goes in v10:
time: 50.8 us; the launch traced here: 50.6 us
  Pallas kernels  49.3 us (97%)
  local copies, waits for them, and re-layouts  0.66 us (1%)
  between operations  0.65 us (1%)
    pallas_call x1, Pallas kernels, mlp_call(): pl.pallas_call(mlp_kernel, out_shape=pltpu.VMEM((rows, width), bf16), in_...  26 us
    pallas_call x1, Pallas kernels, attn_call(): pl.pallas_call(attn_kernel, out_shape=(jax.ShapeDtypeStruct((rows, kv_dim...  23.3 us

profile of v10, /device:TPU:0, one launch (start us, length us, event | category | flops | bytes accessed | tf_op | source)
XLA Modules:
  0.0 50.6 jit_solution(8646439953732506823)
XLA Ops:
  0.6 23.3 %attention.1 = (bf16[32,512]{1,0:T(8,128)(2,1)}, bf16[32,64]{1,0:T(8,128)(2,1)}, f32[4,768,128]{2,1,0:T(8,128)S(1)}, bf16[32,2048]{1,0:T(8,128)(2,1)S(1)}, bf16[...) custom-call(s32[32]{0:T(128)} %lens_hbm.1, bf16[32,2048]{1,0:T(8,128)(2,1)} %hid_hbm.1, ...), custom_call_target="tpu_custom_call" | custom-call | tf_op jit(solution)/shard_map/attention/pallas_call | solution.py:298
  23.9 26.0 %mlp_exchange.1 = bf16[32,2048]{1,0:T(8,128)(2,1)S(1)} custom-call(f32[4,768,128]{2,1,0:T(8,128)S(1)} %get-tuple-element.9.o_ref, bf16[32,2048]{1,0:T(8,128)(2,1)S(1)} %get-tuple-element.10.hid_ref, bf16[20,512,256]{2,1,0:T(8,128)(2,1)S(1)} %get-tuple-element.11.wuv, bf16[5120,1536]{1,0:T(8,128)(2,1)S(1)} %get-tuple-element.12.wo_low, ...), custom_call_target="tpu_custom_call" | custom-call | tf_op jit(solution)/shard_map/mlp_exchange/pallas_call | solution.py:504
  50.0 0.7 %copy.22 = bf16[32,2048]{1,0:T(8,128)(2,1)} copy(bf16[32,2048]{1,0:T(8,128)(2,1)S(1)} %mlp_exchange.1) | data formatting | bytes 262144

commit v11 on v10

--- a/solution.py
+++ b/solution.py
@@ -361,11 +361,16 @@
     def sibling_rows_arrived():
         remote(h_scr, gath.at[0, :, theirs], far_send.at[0], far_recv.at[0], sibling).wait_recv()
 
-    def forward_copy(rel):
-        return remote(gath.at[rel, :, mine], gath.at[rel, :, mine], fw_send.at[rel], fw_recv.at[rel], sibling)
+    def forward_copy(rel, part):
+        return remote(gath.at[rel, part, mine], gath.at[rel, part, mine], fw_send.at[rel, part], fw_recv.at[rel, part], sibling)
+
+    def pass_on(rel, part):
+        near_copy(rel, part).wait_recv()
+        forward_copy(rel, part).start()
 
     def forward_arrived(rel):
-        remote(gath.at[rel, :, theirs], gath.at[rel, :, theirs], fw_send.at[rel], fw_recv.at[rel], sibling).wait_recv()
+        for part in range(CHUNKS):
+            remote(gath.at[rel, part, theirs], gath.at[rel, part, theirs], fw_send.at[rel, part], fw_recv.at[rel, part], sibling).wait_recv()
 
     def pair_copy(rel, half):
         return remote(s1_send.at[rel, half], s1_recv.at[rel, half], p1_send.at[rel, half], p1_recv.at[rel, half], sibling)
@@ -376,6 +381,7 @@
     held_width = wo_low.shape[1]
     late = [pltpu.make_async_copy(wo_hbm.at[:, pl.ds(held_width + k * part_width, part_width)], wo_high.at[k], wo_sems.at[k]) for k in range(1)]
     loads = [pltpu.make_async_copy(src, dst, w_sems.at[k]) for k, (src, dst) in enumerate(((wg_hbm, wg), (wu_hbm, wu), (wd_hbm, wd), (gm_hbm, gm_ref)))]
+    loads[3].start()
     late[0].start()
     barrier = pltpu.get_barrier_semaphore()
     for target in (sibling, peer(1), peer(2), peer(3)):
@@ -400,7 +406,7 @@
         h_scr[part] = resid
         gath[0, part, mine] = resid
         if part == 0:
-            for load in loads:
+            for load in loads[:3]:
                 load.start()
             pl.semaphore_wait(barrier, 4)
         near_copy(1, part).start()
@@ -420,11 +426,10 @@
             piece = gath[rel, part].astype(f32) * factor * gm_ref[columns(part)].astype(f32)
             m_scr[pl.ds(at, 2 * rows), columns(part)] = piece.astype(bf16)
 
-    def activation(count, between=()):
-        block = m_scr[pl.ds(0, count)]
+    def activation(at, between):
+        block = m_scr[pl.ds(at, 4 * rows)]
         gate = jnp.dot(block, wg[...], preferred_element_type=f32)
-        for rel, half in between:
-            send_sum(rel, half)
+        between()
         up = jnp.dot(block, wu[...], preferred_element_type=f32)
         return (jax.nn.silu(gate) * up).astype(bf16)
 
@@ -445,26 +450,34 @@
         s2_send[rel, half] = (keep[rel, half] + s1_recv[rel, half]).astype(bf16)
         chip_copy(rel, half).start()
 
-    for rel in (1, 2):
+    def pass_diagonal():
         for part in range(CHUNKS):
-            near_copy(rel, part).wait_recv()
-        forward_copy(rel).start()
-    for load in loads:
+            pass_on(3, part)
+
+    def send_neighbour_sums():
+        for half in range(2):
+            send_sum(1, half)
+            send_sum(2, half)
+
+    for part in range(CHUNKS - 1):
+        pass_on(1, part)
+        pass_on(2, part)
+    loads[3].wait()
+    sibling_rows_arrived()
+    normed_rows(0, 6 * rows)
+    pass_on(1, CHUNKS - 1)
+    pass_on(2, CHUNKS - 1)
+    for load in loads[:3]:
         load.wait()
     forward_arrived(1)
     normed_rows(1, 0)
     forward_arrived(2)
     normed_rows(2, 2 * rows)
-    contract(activation(4 * rows), (1, 2))
-    for part in range(CHUNKS):
-        near_copy(3, part).wait_recv()
-    forward_copy(3).start()
-    sibling_rows_arrived()
-    normed_rows(0, 2 * rows)
+    contract(activation(0, pass_diagonal), (1, 2))
 
     forward_arrived(3)
-    normed_rows(3, 0)
-    contract(activation(4 * rows, ((1, 0), (2, 0), (1, 1), (2, 1))), (3, 0))
+    normed_rows(3, 4 * rows)
+    contract(activation(4 * rows, send_neighbour_sums), (3, 0))
     send_sum(3, 0)
     send_sum(3, 1)
     totals = []
@@ -488,7 +501,8 @@
         for rel in (1, 2, 3):
             chip_copy(rel, half).wait_send()
     for rel in (1, 2, 3):
-        forward_copy(rel).wait_send()
+        for part in range(CHUNKS):
+            forward_copy(rel, part).wait_send()
 
 
 def mlp_call(o_lat, hidden, w_uv, wo_low, gain_mlp, w_o, w_gate, w_up, w_down):
@@ -515,13 +529,13 @@
             pltpu.VMEM((rows, w_o.shape[0]), bf16),
             pltpu.VMEM((CHUNKS, rows, part_width), bf16),
             pltpu.VMEM((4, CHUNKS, 2 * rows, part_width), bf16),
-            pltpu.VMEM((4 * rows, width), bf16),
+            pltpu.VMEM((8 * rows, width), bf16),
             pltpu.VMEM((4, 2, rows, width // 2), f32),
             pltpu.VMEM((4, 2, rows, width // 2), f32),
             pltpu.VMEM((4, 2, rows, width // 2), f32),
             pltpu.VMEM((4, 2, rows, width // 2), bf16),
             pltpu.VMEM((4, 2, rows, width // 2), bf16),
-            dma((4,)), dma((1,)), dma((4, CHUNKS)), dma((4, CHUNKS)), dma((4,)), dma((4,)), dma((4,)), dma((4,)), dma((4, 2)), dma((4, 2)), dma((4, 2)), dma((4, 2)),
+            dma((4,)), dma((1,)), dma((4, CHUNKS)), dma((4, CHUNKS)), dma((4,)), dma((4,)), dma((4, CHUNKS)), dma((4, CHUNKS)), dma((4, 2)), dma((4, 2)), dma((4, 2)), dma((4, 2)),
         ],
         compiler_params=pltpu.CompilerParams(collective_id=0, has_side_effects=True, vmem_limit_bytes=VMEM_LIMIT),
         name="mlp_exchange",

time: 50.8 us -> 50.4 us (level)
  Pallas kernels: 49.3 us -> 48.7 us
    pallas_call x1, Pallas kernels: 23.3 us -> 22.4 us  [attn_call(): pl.pallas_call(attn_kernel, out_shape=(jax.ShapeDtypeStruct((rows, kv_dim...]
where the time goes in v11:
time: 50.4 us; the launch traced here: 50 us
  Pallas kernels  48.7 us (97%)
  local copies, waits for them, and re-layouts  0.66 us (1%)
  between operations  0.65 us (1%)
    pallas_call x1, Pallas kernels, mlp_call(): pl.pallas_call(mlp_kernel, out_shape=pltpu.VMEM((rows, width), bf16), in_...  26.2 us
    pallas_call x1, Pallas kernels, attn_call(): pl.pallas_call(attn_kernel, out_shape=(jax.ShapeDtypeStruct((rows, kv_dim...  22.4 us

profile of v11, /device:TPU:0, one launch (start us, length us, event | category | flops | bytes accessed | tf_op | source)
XLA Modules:
  0.0 50.0 jit_solution(3897410615468048247)
XLA Ops:
  0.6 22.4 %attention.1 = (bf16[32,512]{1,0:T(8,128)(2,1)}, bf16[32,64]{1,0:T(8,128)(2,1)}, f32[4,768,128]{2,1,0:T(8,128)S(1)}, bf16[32,2048]{1,0:T(8,128)(2,1)S(1)}, bf16[...) custom-call(s32[32]{0:T(128)} %lens_hbm.1, bf16[32,2048]{1,0:T(8,128)(2,1)} %hid_hbm.1, ...), custom_call_target="tpu_custom_call" | custom-call | tf_op jit(solution)/shard_map/attention/pallas_call | solution.py:298
  23.1 26.2 %mlp_exchange.1 = bf16[32,2048]{1,0:T(8,128)(2,1)S(1)} custom-call(f32[4,768,128]{2,1,0:T(8,128)S(1)} %get-tuple-element.9.o_ref, bf16[32,2048]{1,0:T(8,128)(2,1)S(1)} %get-tuple-element.10.hid_ref, bf16[20,512,256]{2,1,0:T(8,128)(2,1)S(1)} %get-tuple-element.11.wuv, bf16[5120,1536]{1,0:T(8,128)(2,1)S(1)} %get-tuple-element.12.wo_low, ...), custom_call_target="tpu_custom_call" | custom-call | tf_op jit(solution)/shard_map/mlp_exchange/pallas_call | solution.py:518
  49.3 0.7 %copy.22 = bf16[32,2048]{1,0:T(8,128)(2,1)} copy(bf16[32,2048]{1,0:T(8,128)(2,1)S(1)} %mlp_exchange.1) | data formatting | bytes 262144

commit v12 on v11

--- a/solution.py
+++ b/solution.py
@@ -411,10 +411,9 @@
             pl.semaphore_wait(barrier, 4)
         near_copy(1, part).start()
         near_copy(2, part).start()
-        if part > 0:
-            near_copy(3, part - 1).start()
-    near_copy(3, CHUNKS - 1).start()
     far_copy(0).start()
+    for part in range(CHUNKS):
+        near_copy(3, part).start()
 
     def normed_rows(rel, at):
         square = jnp.zeros((2 * rows, 1), f32)

time: 50.4 us -> 50.9 us (level); the launches traced: 50 us -> 51.8 us
  Pallas kernels: 48.7 us -> 50.5 us
    pallas_call x1, Pallas kernels: 26.2 us -> 28 us  [mlp_call(): pl.pallas_call(mlp_kernel, out_shape=pltpu.VMEM((rows, width), bf16), in_...]
where the time goes in v12:
time: 50.9 us; the launch traced here: 51.8 us
  Pallas kernels  50.5 us (99%)
  local copies, waits for them, and re-layouts  0.66 us (1%)
  between operations  0.65 us (1%)
    pallas_call x1, Pallas kernels, mlp_call(): pl.pallas_call(mlp_kernel, out_shape=pltpu.VMEM((rows, width), bf16), in_...  28 us
    pallas_call x1, Pallas kernels, attn_call(): pl.pallas_call(attn_kernel, out_shape=(jax.ShapeDtypeStruct((rows, kv_dim...  22.5 us

profile of v12, /device:TPU:0, one launch (start us, length us, event | category | flops | bytes accessed | tf_op | source)
XLA Modules:
  0.0 51.8 jit_solution(4807717826471956923)
XLA Ops:
  0.6 22.5 %attention.1 = (bf16[32,512]{1,0:T(8,128)(2,1)}, bf16[32,64]{1,0:T(8,128)(2,1)}, f32[4,768,128]{2,1,0:T(8,128)S(1)}, bf16[32,2048]{1,0:T(8,128)(2,1)S(1)}, bf16[...) custom-call(s32[32]{0:T(128)} %lens_hbm.1, bf16[32,2048]{1,0:T(8,128)(2,1)} %hid_hbm.1, ...), custom_call_target="tpu_custom_call" | custom-call | tf_op jit(solution)/shard_map/attention/pallas_call | solution.py:298
  23.1 28.0 %mlp_exchange.1 = bf16[32,2048]{1,0:T(8,128)(2,1)S(1)} custom-call(f32[4,768,128]{2,1,0:T(8,128)S(1)} %get-tuple-element.9.o_ref, bf16[32,2048]{1,0:T(8,128)(2,1)S(1)} %get-tuple-element.10.hid_ref, bf16[20,512,256]{2,1,0:T(8,128)(2,1)S(1)} %get-tuple-element.11.wuv, bf16[5120,1536]{1,0:T(8,128)(2,1)S(1)} %get-tuple-element.12.wo_low, ...), custom_call_target="tpu_custom_call" | custom-call | tf_op jit(solution)/shard_map/mlp_exchange/pallas_call | solution.py:517
  51.1 0.7 %copy.22 = bf16[32,2048]{1,0:T(8,128)(2,1)} copy(bf16[32,2048]{1,0:T(8,128)(2,1)S(1)} %mlp_exchange.1) | data formatting | bytes 262144
